TPU v7x, 32 devices: a whole 2x2x4 slice. The times are simulated.
32 devices in a mesh: dp: 16 (over z, y, core), tensor: 2 (over x).
Axes of the slice: x: 2, y: 2, z: 4, core: 2. Of those that a mesh axis runs over, the one named last changes fastest.
Arguments:
- tokens: bfloat16 [12288, 2048], P('dp'), may hold values from -6 to 6
- cotangent: bfloat16 [12288, 2048], P('dp'), may hold values from -8 to 8
- w_query: float32 [2048, 2048], P('dp', 'tensor'), may hold values from -0.125 to 0.125
- w_keyval: float32 [2048, 256], P('dp'), may hold values from -0.125 to 0.125
- w_out: float32 [2048, 2048], P('dp', 'tensor'), may hold values from -1 to 1
- w_up: float32 [2048, 8192], P('dp', 'tensor'), may hold values from -0.125 to 0.125
- w_down: float32 [2048, 8192], P('dp', 'tensor'), may hold values from -0.0625 to 0.0625
- norm1_gain: float32 [2048], P('dp'), may hold values from 0.25 to 1.75
- norm1_bias: float32 [2048], P('dp'), may hold values from -3 to 3
- norm2_gain: float32 [2048], P('dp'), may hold values from 0.25 to 1.75
- norm2_bias: float32 [2048], P('dp'), may hold values from -3 to 3
- route: int32 [12288], replicated, may hold values from 0 to 12287, as said below
- lengths: int32 [16, 4], P('dp'), may hold values from 1 to 512, 768 in all within a row
Outputs:
- output: bfloat16 [12288, 2048], P('dp')
- grad_tokens: bfloat16 [12288, 2048], P('dp')
- grad_w_query: float32 [2048, 2048], P('dp', 'tensor')
- grad_w_keyval: float32 [2048, 256], P('dp')
- grad_w_out: float32 [2048, 2048], P('dp', 'tensor')
- grad_w_up: float32 [2048, 8192], P('dp', 'tensor')
- grad_w_down: float32 [2048, 8192], P('dp', 'tensor')
- grad_norm1_gain: float32 [2048], P('dp')
- grad_norm1_bias: float32 [2048], P('dp')
- grad_norm2_gain: float32 [2048], P('dp')
- grad_norm2_bias: float32 [2048], P('dp')
Inputs may be any that keep to these rules, and one draw needn't show every extreme that they name: route is a permutation of the 12288 places; places g * 768 to (g + 1) * 768 - 1 belong to index g of dp, and the 768 tokens of each index of dp name exactly 48 places of every index of dp. Row g lists the lengths of the 4 sequences at index g of dp in order; they sum to 768, and the longest of each row is exactly 512.
All inputs are finite; a program needn't handle non-finite values.
Results may differ from a plain program's by a relative error of at most 0.012.
The roundings to bfloat16 on the way count: a program that leaves them out, or rounds other values in their place, can miss the bound.
Values may be sent and summed in bfloat16 or wider, within the bound.
A program may use at most 320 MiB of HBM per device.

v0:
```python
import jax
import jax.numpy as jnp
from jax import lax
from jax.sharding import PartitionSpec as P

norm_eps = 1e-05


def layer_norm(values, gain_vector, shift_vector):
    row_mean = jnp.mean(values, axis=-1, keepdims=True)
    centered = values - row_mean
    spread = jnp.mean(centered * centered, axis=-1, keepdims=True)
    return centered * lax.rsqrt(spread + norm_eps) * gain_vector + shift_vector


def gelu_tanh(values):
    return jax.nn.gelu(values, approximate=True)


def visible_pairs(lengths_row, row_count):
    boundaries = jnp.cumsum(lengths_row)
    places = jnp.arange(row_count, dtype=jnp.int32)
    segment = jnp.sum((places[:, None] >= boundaries[None, :]).astype(jnp.int32), axis=1)
    return jnp.logical_and(segment[:, None] == segment[None, :], places[None, :] <= places[:, None])


def right_product(first_op, second_op):
    return lax.dot_general(
        first_op, second_op, (((1,), (1,)), ((), ())), preferred_element_type=jnp.float32
    )


def left_product(first_op, second_op):
    return lax.dot_general(
        first_op, second_op, (((0,), (0,)), ((), ())), preferred_element_type=jnp.float32
    )


def column_term(first_op, second_op):
    return left_product(first_op, second_op)


def masked_scores(query_heads, key_rows, visible, score_scale):
    scores = (
        jnp.einsum("qhd,kd->hqk", query_heads, key_rows, preferred_element_type=jnp.float32)
        * score_scale
    )
    return jnp.where(visible, scores, -1e30)


def per_device(
    tokens,
    cotangent,
    w_query,
    w_keyval,
    w_out,
    w_up,
    w_down,
    norm1_gain,
    norm1_bias,
    norm2_gain,
    norm2_bias,
    route,
    lengths,
):
    row_count = tokens.shape[0]
    head_dim = w_keyval.shape[1] // 2
    heads_here = w_query.shape[1] // head_dim
    score_scale = head_dim ** (-0.5)
    group_index = lax.axis_index("dp")
    own_route = lax.dynamic_slice_in_dim(route, group_index * row_count, row_count)
    send_order = jnp.argsort(own_route, stable=True)
    inverse = jnp.argsort(route, stable=True)
    sources = lax.dynamic_slice_in_dim(inverse, group_index * row_count, row_count) // row_count
    recv_order = jnp.argsort(sources, stable=True)
    placing = jnp.argsort(recv_order, stable=True)
    arrived = (
        lax.all_to_all(tokens[send_order], "dp", split_axis=0, concat_axis=0, tiled=True),
        lax.all_to_all(cotangent[send_order], "dp", split_axis=0, concat_axis=0, tiled=True),
    )
    tokens_here = arrived[0][placing]
    grad_here = arrived[1][placing]
    fetched = (
        lax.all_gather(w_query.astype(jnp.bfloat16), "dp", axis=0, tiled=True),
        lax.all_gather(w_keyval.astype(jnp.bfloat16), "dp", axis=0, tiled=True),
        lax.all_gather(w_out.astype(jnp.bfloat16), "dp", axis=0, tiled=True),
        lax.all_gather(w_up.astype(jnp.bfloat16), "dp", axis=0, tiled=True),
        lax.all_gather(w_down.astype(jnp.bfloat16), "dp", axis=0, tiled=True),
        lax.all_gather(norm1_gain.astype(jnp.bfloat16), "dp", axis=0, tiled=True),
        lax.all_gather(norm1_bias.astype(jnp.bfloat16), "dp", axis=0, tiled=True),
        lax.all_gather(norm2_gain.astype(jnp.bfloat16), "dp", axis=0, tiled=True),
        lax.all_gather(norm2_bias.astype(jnp.bfloat16), "dp", axis=0, tiled=True),
    )
    full_query, full_keyval, full_out, full_up, full_down = (
        fetched[0],
        fetched[1],
        fetched[2],
        fetched[3],
        fetched[4],
    )
    first_gain = fetched[5].astype(jnp.float32)
    first_shift = fetched[6].astype(jnp.float32)
    second_gain = fetched[7].astype(jnp.float32)
    second_shift = fetched[8].astype(jnp.float32)
    resid_in = tokens_here.astype(jnp.float32)
    normed_one = layer_norm(resid_in, first_gain, first_shift).astype(jnp.bfloat16)
    queries = jnp.dot(normed_one, full_query, preferred_element_type=jnp.float32).astype(
        jnp.bfloat16
    )
    keyval = jnp.dot(normed_one, full_keyval, preferred_element_type=jnp.float32).astype(
        jnp.bfloat16
    )
    query_heads = queries.reshape(row_count, heads_here, head_dim)
    key_rows = keyval[:, :head_dim]
    value_rows = keyval[:, head_dim:]
    visible = visible_pairs(lengths[0], row_count)[None]
    masked = masked_scores(query_heads, key_rows, visible, score_scale)
    row_max = jnp.max(masked, axis=2, keepdims=True)
    weights_exp = jnp.exp(masked - row_max)
    row_total = jnp.sum(weights_exp, axis=2, keepdims=True)
    probs_first = (weights_exp / row_total).astype(jnp.bfloat16)
    log_total = row_max + jnp.log(row_total)
    context = jnp.einsum("hqk,kd->qhd", probs_first, value_rows, preferred_element_type=jnp.float32)
    context = context.reshape(row_count, heads_here * head_dim).astype(jnp.bfloat16)
    attn_output = lax.psum(right_product(context, full_out), "tensor")
    resid_mid = resid_in + attn_output
    normed_two = layer_norm(resid_mid, second_gain, second_shift).astype(jnp.bfloat16)
    hidden_pre = jnp.dot(normed_two, full_up, preferred_element_type=jnp.float32)
    active = gelu_tanh(hidden_pre).astype(jnp.bfloat16)
    mlp_output = lax.psum(right_product(active, full_down).astype(jnp.bfloat16), "tensor").astype(
        jnp.float32
    )
    result = (resid_mid + mlp_output).astype(jnp.bfloat16)
    refetched = (
        lax.all_gather(w_query.astype(jnp.bfloat16), "dp", axis=0, tiled=True),
        lax.all_gather(w_keyval.astype(jnp.bfloat16), "dp", axis=0, tiled=True),
        lax.all_gather(w_out.astype(jnp.bfloat16), "dp", axis=0, tiled=True),
        lax.all_gather(w_up.astype(jnp.bfloat16), "dp", axis=0, tiled=True),
        lax.all_gather(w_down.astype(jnp.bfloat16), "dp", axis=0, tiled=True),
    )
    back_query, back_keyval, back_out, back_up, back_down = (
        refetched[0],
        refetched[1],
        refetched[2],
        refetched[3],
        refetched[4],
    )
    grad_out = grad_here.astype(jnp.float32)
    grad_active = jnp.dot(grad_here, back_down, preferred_element_type=jnp.float32)
    gelu_back = jax.vjp(gelu_tanh, hidden_pre)[1]
    grad_up = gelu_back(grad_active)[0].astype(jnp.bfloat16)
    grad_norm_two = lax.psum(right_product(grad_up, back_up), "tensor")
    norm_two_back = jax.vjp(layer_norm, resid_mid, second_gain, second_shift)[1]
    grad_mid_norm, grad_gain_two, grad_shift_two = norm_two_back(grad_norm_two)
    grad_mid = grad_out + grad_mid_norm
    grad_mid_low = grad_mid.astype(jnp.bfloat16)
    grad_context = jnp.dot(grad_mid_low, back_out, preferred_element_type=jnp.float32).astype(
        jnp.bfloat16
    )
    grad_ctx_heads = grad_context.reshape(row_count, heads_here, head_dim)
    masked_again = masked_scores(query_heads, key_rows, visible, score_scale)
    probs_again = jnp.exp(masked_again - log_total)
    probs_low = probs_again.astype(jnp.bfloat16)
    grad_probs = jnp.einsum(
        "qhd,kd->hqk", grad_ctx_heads, value_rows, preferred_element_type=jnp.float32
    )
    row_delta = jnp.sum(grad_probs * probs_again, axis=2, keepdims=True)
    grad_scores = (probs_again * (grad_probs - row_delta)).astype(jnp.bfloat16)
    grad_query = (
        jnp.einsum("hqk,kd->qhd", grad_scores, key_rows, preferred_element_type=jnp.float32)
        * score_scale
    )
    grad_query = grad_query.reshape(row_count, heads_here * head_dim).astype(jnp.bfloat16)
    grad_keys = (
        jnp.einsum("hqk,qhd->kd", grad_scores, query_heads, preferred_element_type=jnp.float32)
        * score_scale
    )
    grad_values = jnp.einsum(
        "hqk,qhd->kd", probs_low, grad_ctx_heads, preferred_element_type=jnp.float32
    )
    grad_keyval_part = jnp.concatenate([grad_keys, grad_values], axis=1)
    grad_norm_query, grad_keyval = lax.psum(
        (right_product(grad_query, back_query), grad_keyval_part), "tensor"
    )
    grad_keyval_low = grad_keyval.astype(jnp.bfloat16)
    grad_norm_one = grad_norm_query + right_product(grad_keyval_low, back_keyval)
    norm_one_back = jax.vjp(layer_norm, resid_in, first_gain, first_shift)[1]
    grad_in_norm, grad_gain_one, grad_shift_one = norm_one_back(grad_norm_one)
    grad_resid = (grad_mid + grad_in_norm).astype(jnp.bfloat16)
    edge_one = w_query.shape[1]
    edge_two = edge_one + w_keyval.shape[1]
    up_cols = w_up.shape[1]
    summed = lax.psum_scatter(
        jnp.concatenate(
            [
                column_term(normed_one, grad_query),
                column_term(normed_one, grad_keyval_low),
                column_term(grad_mid_low, context),
                column_term(normed_two, grad_up),
                column_term(grad_here, active),
            ],
            axis=1,
        ),
        "dp",
        scatter_dimension=0,
        tiled=True,
    )
    edge_three = edge_two + w_out.shape[1]
    edge_four = edge_three + up_cols
    grad_wq = summed[:, :edge_one]
    grad_wkv = summed[:, edge_one:edge_two]
    grad_wo = summed[:, edge_two:edge_three]
    grad_wup = summed[:, edge_three:edge_four]
    grad_wdown = summed[:, edge_four:]
    norm_parts = (
        lax.psum_scatter(grad_gain_one, "dp", scatter_dimension=0, tiled=True),
        lax.psum_scatter(grad_shift_one, "dp", scatter_dimension=0, tiled=True),
        lax.psum_scatter(grad_gain_two, "dp", scatter_dimension=0, tiled=True),
        lax.psum_scatter(grad_shift_two, "dp", scatter_dimension=0, tiled=True),
    )
    returned = (
        lax.all_to_all(result[recv_order], "dp", split_axis=0, concat_axis=0, tiled=True),
        lax.all_to_all(grad_resid[recv_order], "dp", split_axis=0, concat_axis=0, tiled=True),
    )
    restore = jnp.argsort(send_order, stable=True)
    output = returned[0][restore]
    grad_tokens = returned[1][restore]
    return (
        output,
        grad_tokens,
        grad_wq,
        grad_wkv,
        grad_wo,
        grad_wup,
        grad_wdown,
        norm_parts[0],
        norm_parts[1],
        norm_parts[2],
        norm_parts[3],
    )


def solution(mesh):
    placed = (
        P("dp", None),
        P("dp", None),
        P("dp", "tensor"),
        P("dp", None),
        P("dp", "tensor"),
        P("dp", "tensor"),
        P("dp", "tensor"),
        P("dp"),
        P("dp"),
        P("dp"),
        P("dp"),
        P(),
        P("dp", None),
    )
    return jax.shard_map(
        per_device,
        mesh=mesh,
        in_specs=placed,
        out_specs=(
            P("dp", None),
            P("dp", None),
            P("dp", "tensor"),
            P("dp", None),
            P("dp", "tensor"),
            P("dp", "tensor"),
            P("dp", "tensor"),
            P("dp"),
            P("dp"),
            P("dp"),
            P("dp"),
        ),
        check_vma=False,
    )
```

profile of v0, /device:TPU:0, one launch (start us, length us, event | category | flops | bytes accessed | tf_op | source)
XLA Modules:
  0.0 1982.8 jit_solution(17851792786017311539)
XLA Ops:
  20.3 7.6 all-to-all-start
  29.9 69.7 %all-gather.1 = bf16[16,1,128]{2,1,0:T(2,128)(2,1)S(1)} all-gather(bf16[1,1,128]{2,1,0:T(2,128)(2,1)S(1)} %convert_bitcast_fusion.2), channel_id=1, replica_groups=mesh['dp'=16,'tensor'=2] {'dp'}, dimensions={0}, use_global_device_ids=true | all-gather | bytes 4352 | tf_op jit(solution)/shard_map/all_gather | solution.py:90
  99.6 48.6 %all-gather = bf16[16,1,128]{2,1,0:T(2,128)(2,1)S(1)} all-gather(bf16[1,1,128]{2,1,0:T(2,128)(2,1)S(1)} %convert_bitcast_fusion.3), channel_id=1, replica_groups=mesh['dp'=16,'tensor'=2] {'dp'}, dimensions={0}, use_global_device_ids=true | all-gather | bytes 4352 | tf_op jit(solution)/shard_map/all_gather | solution.py:89
  148.3 8.2 sort.77
  192.4 9.4 fusion.47
  201.8 8.9 fusion.3
  210.7 8.8 fusion.29
  219.6 8.2 fusion.48
  242.1 67.0 %all-gather.3 = bf16[16,1,128]{2,1,0:T(2,128)(2,1)S(1)} all-gather(bf16[1,1,128]{2,1,0:T(2,128)(2,1)S(1)} %convert_bitcast_fusion), channel_id=1, replica_groups=mesh['dp'=16,'tensor'=2] {'dp'}, dimensions={0}, use_global_device_ids=true | all-gather | bytes 4352 | tf_op jit(solution)/shard_map/all_gather | solution.py:92
  309.2 32.8 %all-gather.2 = bf16[16,1,128]{2,1,0:T(2,128)(2,1)S(1)} all-gather(bf16[1,1,128]{2,1,0:T(2,128)(2,1)S(1)} %convert_bitcast_fusion.1), channel_id=1, replica_groups=mesh['dp'=16,'tensor'=2] {'dp'}, dimensions={0}, use_global_device_ids=true | all-gather | bytes 4352 | tf_op jit(solution)/shard_map/all_gather | solution.py:91
  346.7 31.9 %all-reduce.11.cloned.1.call-done = f32[768,2048]{1,0:T(8,128)} async-done(((f32[768,2048]{1,0:T(8,128)}), f32[768,2048]{1,0:T(8,128)}) %all-reduce.11.cloned.1.call-update) | async-done | bytes 6291472 | tf_op jit(solution)/shard_map/psum | solution.py:125
  386.9 120.7 %all-gather.18.cloned.1.call-done = bf16[2048,4096]{1,0:T(8,128)(2,1)} async-done(((bf16[128,4096]{1,0:T(8,128)(2,1)}), bf16[2048,4096]{1,0:T(8,128)(2,1)}) %all-gather.18.cloned.1.call-update) | async-done | bytes 16777232 | tf_op jit(solution)/shard_map/all_gather | solution.py:88
  507.6 19.3 fusion.49
  526.9 107.9 %all-gather.16.cloned.1.call-done = bf16[2048,4096]{1,0:T(8,128)(2,1)} async-done(((bf16[128,4096]{1,0:T(8,128)(2,1)}), bf16[2048,4096]{1,0:T(8,128)(2,1)}) %all-gather.16.cloned.1.call-update) | async-done | bytes 16777232 | tf_op jit(solution)/shard_map/all_gather | solution.py:87
  634.8 30.8 %fusion.11 = (bf16[768,4096]{1,0:T(8,128)(2,1)}, f32[768,4096]{1,0:T(8,128)}) fusion(f32[768,4096]{1,0:T(8,128)} %fusion.49, bf16[2048,4096]{1,0:T(8,128)(2,1)} %all-gather.16.cloned.1.call-done, f32[768,2048]{1,0:T(8,128)} %copy-done.5, f32[2048]{0:T(1024)S(1)} %bitcast.116, f32[2048]{0:T(1024)S(1)} %bitcast.111, f32[768]{0:T(1024)S(1)} %fusion.39, ...), kind=kOutput, calls=%fused_computation.29 | convolution fusion | flops 12955680768 | bytes 54548480 | tf_op jit(solution)/shard_map/dot_general | solution.py:128
  665.7 20.5 %fusion.50 = f32[768,2048]{1,0:T(8,128)} fusion(bf16[768,4096]{1,0:T(8,128)(2,1)} %get-tuple-element.43, bf16[2048,4096]{1,0:T(8,128)(2,1)} %all-gather.16.cloned.1.call-done), kind=kOutput, calls=%fused_computation.118 | convolution fusion | flops 12884901888 | bytes 29360128 | tf_op jit(solution)/shard_map/dot_general | solution.py:28
  686.3 31.9 %convolution_convert_fusion = bf16[768,2048]{1,0:T(8,128)(2,1)} fusion(bf16[2048,4096]{1,0:T(8,128)(2,1)} %all-gather.18.cloned.1.call-done, f32[768,4096]{1,0:T(8,128)} %get-tuple-element.44), kind=kOutput, calls=%fused_computation.61 | convolution fusion | flops 12914786304 | bytes 32505856 | tf_op jit(solution)/shard_map/dot_general | solution.py:28
  718.3 119.5 %all-reduce.15.cloned.1.call-done = f32[768,2048]{1,0:T(8,128)} async-done(((f32[768,2048]{1,0:T(8,128)}), f32[768,2048]{1,0:T(8,128)}) %all-reduce.15.cloned.1.call-update) | async-done | bytes 6291472 | tf_op jit(solution)/shard_map/psum | solution.py:152
  844.6 81.4 %all-reduce.13.cloned.1.call-done = bf16[768,2048]{1,0:T(8,128)(2,1)} async-done(((bf16[768,2048]{1,0:T(8,128)(2,1)}), bf16[768,2048]{1,0:T(8,128)(2,1)}) %all-reduce.13.cloned.1.call-update) | async-done | bytes 3145744 | tf_op jit(solution)/shard_map/psum | solution.py:130
  925.9 6.9 fusion.43
  945.2 8.5 fusion.31
  953.8 12.1 fusion
  965.9 12.9 fusion.2
  985.5 22.9 %all-reduce.18 = bf16[768,256]{0,1:T(8,128)(2,1)S(1)} all-reduce(f32[768,256]{0,1:T(8,128)} %pad_maximum_fusion), channel_id=1, replica_groups=mesh['dp'=16,'tensor'=2] {'tensor'}, use_global_device_ids=true, to_apply=%region_20.21 | all-reduce | flops 196608 | bytes 1179648 | tf_op jit(solution)/shard_map/psum | solution.py:182
  1008.5 9.3 convolution_dynamic-update-slice_fusion.3
  1033.7 23.6 %convolution_dynamic-update-slice_fusion.1 = f32[2048,10496]{1,0:T(8,128)} fusion(f32[2048,10496]{1,0:T(8,128)} %convolution_dynamic-update-slice_fusion.2, bf16[768,4096]{1,0:T(8,128)(2,1)} %get-tuple-element.43, f32[768,2048]{1,0:T(8,128)} %copy-done.5, f32[2048]{0:T(1024)S(1)} %bitcast.117, f32[2048]{0:T(1024)S(1)} %bitcast.114, f32[768]{0:T(1024)S(1)} %fusion.39, ...), kind=kOutput, calls=%fused_computation.9 | convolution fusion | flops 12892766208 | bytes 46159872 | tf_op jit(solution)/shard_map/dot_general | solution.py:34
  1057.3 25.4 %convolution_dynamic-update-slice_fusion = f32[2048,10496]{1,0:T(8,128)} fusion(f32[2048,10496]{1,0:T(8,128)} %convolution_dynamic-update-slice_fusion.1, bf16[768,2048]{1,0:T(8,128)(2,1)} %gather_fusion.5, f32[768,4096]{1,0:T(8,128)} %get-tuple-element.44), kind=kOutput, calls=%fused_computation.8 | convolution fusion | flops 12913213440 | bytes 49283072 | tf_op jit(solution)/shard_map/dot_general | solution.py:34
  1094.2 83.2 %all-reduce.17.cloned.1.call-done = f32[768,2048]{1,0:T(8,128)} async-done(((f32[768,2048]{1,0:T(8,128)}), f32[768,2048]{1,0:T(8,128)}) %all-reduce.17.cloned.1.call-update) | async-done | bytes 6291472 | tf_op jit(solution)/shard_map/psum | solution.py:182
  1192.8 10.1 gather_fusion.6
  1219.1 100.9 %all-reduce.4 = (f32[2048]{0:T(1024)S(1)}, f32[2048]{0:T(1024)S(1)}, f32[2048]{0:T(1024)S(1)}, f32[2048]{0:T(1024)S(1)}) all-reduce(f32[2048]{0:T(1024)S(1)} %get-tuple-element.23, f32[2048]{0:T(1024)S(1)} %copy-done.36, f32[2048]{0:T(1024)S(1)} %copy-done.37, f32[2048]{0:T(1024)S(1)} %copy-done.38), channel_id=3, replica_groups=mesh['dp'=16,'tensor'=2] {'dp'}, use_global_device_ids=true, to_apply=%region_25.26.clone | all-reduce | flops 8192 | bytes 65536
  1322.3 9.6 gather_fusion.7
  1331.9 635.1 %reduce-scatter.2.cloned.1.call-done = f32[128,10496]{1,0:T(8,128)} async-done(((f32[2048,10496]{1,0:T(8,128)}), f32[128,10496]{1,0:T(8,128)}) %reduce-scatter.2.cloned.1.call-update) | async-done | bytes 5373968 | tf_op jit(solution)/shard_map/reduce_scatter | solution.py:193
  (219 shorter events, 173.4 us)
Async XLA Ops:
  7.2 173.3 %all-gather.10.cloned.1.call-start = ((), (), s32[]{:S(2)}) async-start(), calls=%async_computation.5 | async-start | bytes 1114112 | tf_op jit(solution)/shard_map/all_gather | solution.py:85
  9.0 174.9 %all-gather.12.cloned.1.call-start = ((), (), s32[]{:S(2)}) async-start(), calls=%async_computation.6 | async-start | bytes 4456448 | tf_op jit(solution)/shard_map/all_gather | solution.py:84
  20.2 9.5 copy-start.47
  20.2 9.5 copy-start.48
  20.2 9.5 copy-start.49
  20.2 128.1 %copy-start.29 = (s32[12288]{0:T(1024)S(1)}, s32[12288]{0:T(1024)}, u32[]{:S(2)}) copy-start(s32[12288]{0:T(1024)} %param.24) | copy-start | bytes 147460
  20.3 146.4 %all-to-all-start = ((bf16[16,48,2048]{2,1,0:T(8,128)(2,1)}), bf16[16,48,2048]{2,1,0:T(8,128)(2,1)S(1)}, u32[]{:S(2)}, u32[]{:S(2)}) async-start(bf16[16,48,2048]{2,1,0:T(8,128)(2,1)} %bitcast.99), calls=%async_computation | async-start | bytes 6291456 | tf_op jit(solution)/shard_map/all_to_all | solution.py:78
  27.8 191.8 %all-gather.14.cloned.1.call-start = ((), (), s32[]{:S(2)}) async-start(), calls=%async_computation.7 | async-start | bytes 4456448 | tf_op jit(solution)/shard_map/all_gather | solution.py:86
  29.7 348.9 %all-reduce.11.cloned.1.call-start = ((), (), s32[]{:S(2)}) async-start(), calls=%async_computation.8 | async-start | bytes 12582912 | tf_op jit(solution)/shard_map/psum | solution.py:125
  148.3 28.8 %copy-start.21 = (f32[16,1,128]{2,1,0:T(1,128)}, f32[16,1,128]{2,1,0:T(1,128)S(1)}, u32[]{:S(2)}) copy-start(f32[16,1,128]{2,1,0:T(1,128)S(1)} %convert_element_type.157) | copy-start | bytes 24580
  161.0 10.1 copy-start.41
  183.9 26.8 %copy-start.17 = (bf16[768,256]{1,0:T(8,128)(2,1)}, bf16[768,256]{1,0:T(8,128)(2,1)S(1)}, u32[]{:S(2)}) copy-start(bf16[768,256]{1,0:T(8,128)(2,1)S(1)} %convolution_convert_fusion.3) | copy-start | bytes 1179652
  227.9 279.7 %all-gather.18.cloned.1.call-start = ((), (), s32[]{:S(2)}) async-start(), calls=%async_computation.10 | async-start | bytes 17825792 | tf_op jit(solution)/shard_map/all_gather | solution.py:88
  230.8 404.0 %all-gather.16.cloned.1.call-start = ((), (), s32[]{:S(2)}) async-start(), calls=%async_computation.9 | async-start | bytes 17825792 | tf_op jit(solution)/shard_map/all_gather | solution.py:87
  238.2 71.0 %copy-start.51 = (f32[128]{0:T(128)S(1)}, f32[128]{0:T(128)}, u32[]{:S(2)}) copy-start(f32[128]{0:T(128)} %param.22) | copy-start | bytes 1540
  238.2 103.8 %all-to-all-start.2 = ((bf16[16,48,2048]{2,1,0:T(8,128)(2,1)}), bf16[16,48,2048]{2,1,0:T(8,128)(2,1)S(1)}, u32[]{:S(2)}, u32[]{:S(2)}) async-start(bf16[16,48,2048]{2,1,0:T(8,128)(2,1)} %bitcast.102), calls=%async_computation.2 | async-start | bytes 6291456 | tf_op jit(solution)/shard_map/all_to_all | solution.py:79
  242.1 595.7 %all-reduce.15.cloned.1.call-start = ((), (), s32[]{:S(2)}) async-start(), calls=%async_computation.12 | async-start | bytes 12582912 | tf_op jit(solution)/shard_map/psum | solution.py:152
  309.1 325.7 %copy-start.43 = (f32[16,1,128]{2,1,0:T(1,128)}, f32[16,1,128]{2,1,0:T(1,128)S(1)}, u32[]{:S(2)}) copy-start(f32[16,1,128]{2,1,0:T(1,128)S(1)} %convert_element_type.160) | copy-start | bytes 24580
  382.9 124.7 %copy-start.7 = (bf16[768,2048]{1,0:T(8,128)(2,1)S(1)}, bf16[768,2048]{1,0:T(8,128)(2,1)}, u32[]{:S(2)}) copy-start(bf16[768,2048]{1,0:T(8,128)(2,1)} %gather_fusion.5) | copy-start | bytes 9437188
  686.2 239.7 %all-reduce.13.cloned.1.call-start = ((), (), s32[]{:S(2)}) async-start(), calls=%async_computation.11 | async-start | bytes 6291456 | tf_op jit(solution)/shard_map/psum | solution.py:130
  686.3 32.0 %copy-start.20 = (f32[8,768]{1,0:T(8,128)S(1)}, f32[8,768]{1,0:T(8,128)}, u32[]{:S(2)}) copy-start(f32[8,768]{1,0:T(8,128)} %copy-done.19) | copy-start | bytes 73732
  686.3 32.0 %copy-start.26 = (f32[8,768]{1,0:T(8,128)S(1)}, f32[8,768]{1,0:T(8,128)}, u32[]{:S(2)}) copy-start(f32[8,768]{1,0:T(8,128)} %copy-done.25) | copy-start | bytes 73732
  718.2 459.1 %all-reduce.17.cloned.1.call-start = ((), (), s32[]{:S(2)}) async-start(), calls=%async_computation.13 | async-start | bytes 12582912 | tf_op jit(solution)/shard_map/psum | solution.py:182
  965.9 12.9 copy-start.13
  1023.1 943.8 %reduce-scatter.2.cloned.1.call-start = ((), (), s32[]{:S(2)}) async-start(), calls=%async_computation.14 | async-start | bytes 91357184 | tf_op jit(solution)/shard_map/reduce_scatter | solution.py:193
  1088.3 89.1 %copy-start.22 = (f32[16,1,128]{2,1,0:T(1,128)S(1)}, f32[16,1,128]{2,1,0:T(1,128)}, u32[]{:S(2)}) copy-start(f32[16,1,128]{2,1,0:T(1,128)} %copy-done.21) | copy-start | bytes 24580
  1088.3 89.1 %copy-start.24 = (f32[768]{0:T(1024)S(1)}, f32[768]{0:T(1024)}, u32[]{:S(2)}) copy-start(f32[768]{0:T(1024)} %copy-done.23) | copy-start | bytes 9220
  1088.3 114.7 %all-to-all-start.1 = ((bf16[16,48,2048]{2,1,0:T(8,128)(2,1)}), bf16[16,48,2048]{2,1,0:T(8,128)(2,1)S(1)}, u32[]{:S(2)}, u32[]{:S(2)}) async-start(bf16[16,48,2048]{2,1,0:T(8,128)(2,1)} %bitcast.101), calls=%async_computation.1 | async-start | bytes 6291456 | tf_op jit(solution)/shard_map/all_to_all | solution.py:222
  1094.1 89.3 %copy-start.28 = (f32[768]{0:T(1024)S(1)}, f32[768]{0:T(1024)}, u32[]{:S(2)}) copy-start(f32[768]{0:T(1024)} %copy-done.27) | copy-start | bytes 9220
  1203.0 10.6 copy-start.54
  1203.0 119.4 %all-to-all-start.3 = ((bf16[16,48,2048]{2,1,0:T(8,128)(2,1)}), bf16[16,48,2048]{2,1,0:T(8,128)(2,1)}, u32[]{:S(2)}, u32[]{:S(2)}) async-start(bf16[16,48,2048]{2,1,0:T(8,128)(2,1)} %bitcast.100), calls=%async_computation.3 | async-start | bytes 6291456 | tf_op jit(solution)/shard_map/all_to_all | solution.py:223
  1322.3 653.2 %copy-start.1 = (bf16[768,2048]{1,0:T(8,128)(2,1)S(1)}, bf16[768,2048]{1,0:T(8,128)(2,1)}, u32[]{:S(2)}) copy-start(bf16[768,2048]{1,0:T(8,128)(2,1)} %param.13) | copy-start | bytes 9437188
  (37 other events, 192.3 us)
Sparse Core Ops, SparseCore 0:
  10.7 62.2 all-gather.9
  75.7 56.6 all-gather.11
  134.6 50.0 all-gather.13
  228.0 150.5 all-reduce.10
  381.1 126.4 all-gather.17
  510.2 124.5 all-gather.15
  686.3 151.4 all-reduce.14
  840.1 85.8 all-reduce.12
  1023.3 154.0 all-reduce.16
  1181.4 785.5 reduce-scatter.1
where the time goes:
time: 1990 us; the launch traced here: 1980 us
  waiting for transfers between devices  1180 us (59%)
  blocking collectives  342 us (17%)
  matrix products  250 us (13%)
  other arithmetic  98.3 us (5%)
  local copies, waits for them, and re-layouts  72.6 us (4%)
  starting transfers between devices  23.9 us (1%)
    reduce_scatter x1, waiting for transfers between devices, per_device(): lax.psum_scatter(jnp.concatenate([column_term(normed_one, grad_query), co...  635 us
    all_gather x1, waiting for transfers between devices, per_device(): lax.all_gather(w_down.astype(jnp.bfloat16), 'dp', axis=0, tiled=True)  121 us
    psum x1, waiting for transfers between devices, per_device(): grad_norm_two = lax.psum(right_product(grad_up, back_up), 'tensor')  120 us
    all_gather x1, waiting for transfers between devices, per_device(): lax.all_gather(w_up.astype(jnp.bfloat16), 'dp', axis=0, tiled=True)  108 us
    unnamed x1, blocking collectives  101 us
    psum x1, waiting for transfers between devices, per_device(): lax.psum((right_product(grad_query, back_query), grad_keyval_part), 'tens...  83.2 us
    psum x1, waiting for transfers between devices, per_device(): lax.psum(right_product(active, full_down).astype(jnp.bfloat16), 'tensor')  81.4 us
    dot_general x5, matrix products, right_product(): lax.dot_general(first_op, second_op, (((1,), (1,)), ((), ())), preferred_...  72.1 us
  transfers between devices with their start and end apart: 14, of which 7 were waited for; matrix products, arithmetic and copies ran while one was open for 14% of the time, Pallas kernels for 0%

commit v1 on v0

v1 whole, which is shorter than its diff:
```python
import jax
import jax.numpy as jnp
from jax import lax
from jax.sharding import PartitionSpec as P

norm_eps = 1e-05


def layer_norm(values, gain_vector, shift_vector):
    row_mean = jnp.mean(values, axis=-1, keepdims=True)
    centered = values - row_mean
    spread = jnp.mean(centered * centered, axis=-1, keepdims=True)
    return centered * lax.rsqrt(spread + norm_eps) * gain_vector + shift_vector


def gelu_tanh(values):
    return jax.nn.gelu(values, approximate=True)


def visible_pairs(lengths_row, row_count):
    boundaries = jnp.cumsum(lengths_row)
    places = jnp.arange(row_count, dtype=jnp.int32)
    segment = jnp.sum((places[:, None] >= boundaries[None, :]).astype(jnp.int32), axis=1)
    return jnp.logical_and(segment[:, None] == segment[None, :], places[None, :] <= places[:, None])


def right_product(first_op, second_op):
    return lax.dot_general(
        first_op, second_op, (((1,), (1,)), ((), ())), preferred_element_type=jnp.float32
    )


def left_product(first_op, second_op):
    return lax.dot_general(
        first_op, second_op, (((0,), (0,)), ((), ())), preferred_element_type=jnp.float32
    )


def as_columns(vectors):
    columns = jnp.stack([vector.astype(jnp.bfloat16) for vector in vectors], axis=1)
    return jnp.pad(columns, ((0, 0), (0, 128 - len(vectors))))


def tensor_sum(values, ride_along=None):
    own = lax.optimization_barrier(values.astype(jnp.bfloat16))
    total = own.astype(jnp.float32)
    if lax.axis_size("tensor") == 2:
        other = lax.ppermute(own, "tensor", [(0, 1), (1, 0)])
        if ride_along is not None:
            other, ride_along = lax.optimization_barrier((other, ride_along))
        summed = total + other.astype(jnp.float32)
    else:
        summed = lax.psum(own, "tensor").astype(jnp.float32)
    return summed if ride_along is None else (summed, ride_along)


def summed_rows(low):
    total = lax.psum_scatter(low, "dp", scatter_dimension=0, tiled=True)
    return total.astype(jnp.float32)


def weight_term(first_op, second_op):
    return left_product(first_op, second_op).astype(jnp.bfloat16)


def masked_scores(query_heads, key_rows, visible, score_scale):
    scores = (
        jnp.einsum("qhd,kd->hqk", query_heads, key_rows, preferred_element_type=jnp.float32)
        * score_scale
    )
    return jnp.where(visible, scores, -1e30)


def per_device(
    tokens,
    cotangent,
    w_query,
    w_keyval,
    w_out,
    w_up,
    w_down,
    norm1_gain,
    norm1_bias,
    norm2_gain,
    norm2_bias,
    route,
    lengths,
):
    row_count = tokens.shape[0]
    head_dim = w_keyval.shape[1] // 2
    heads_here = w_query.shape[1] // head_dim
    score_scale = head_dim ** (-0.5)
    group_index = lax.axis_index("dp")
    first_block = jnp.concatenate(
        [
            w_query.astype(jnp.bfloat16),
            w_keyval.astype(jnp.bfloat16),
            as_columns((norm1_gain, norm1_bias, norm2_gain, norm2_bias)),
        ],
        axis=1,
    )
    full_first = lax.all_gather(first_block, "dp", axis=0, tiled=True)
    full_out = lax.all_gather(w_out.astype(jnp.bfloat16), "dp", axis=0, tiled=True)
    full_up = lax.all_gather(w_up.astype(jnp.bfloat16), "dp", axis=0, tiled=True)
    full_down = lax.all_gather(w_down.astype(jnp.bfloat16), "dp", axis=0, tiled=True)
    own_route = lax.dynamic_slice_in_dim(route, group_index * row_count, row_count)
    send_order = jnp.argsort(own_route, stable=True)
    inverse = jnp.argsort(route, stable=True)
    sources = lax.dynamic_slice_in_dim(inverse, group_index * row_count, row_count) // row_count
    recv_order = jnp.argsort(sources, stable=True)
    placing = jnp.argsort(recv_order, stable=True)
    arrived = (
        lax.all_to_all(tokens[send_order], "dp", split_axis=0, concat_axis=0, tiled=True),
        lax.all_to_all(cotangent[send_order], "dp", split_axis=0, concat_axis=0, tiled=True),
    )
    tokens_here = arrived[0][placing]
    grad_here = arrived[1][placing]
    qkv_cols = w_query.shape[1] + w_keyval.shape[1]
    full_qkv = full_first[:, :qkv_cols]
    norm_rows = full_first[:, qkv_cols : qkv_cols + 4].astype(jnp.float32).T
    first_gain, first_shift, second_gain, second_shift = (
        norm_rows[0],
        norm_rows[1],
        norm_rows[2],
        norm_rows[3],
    )
    resid_in = tokens_here.astype(jnp.float32)
    normed_one = layer_norm(resid_in, first_gain, first_shift).astype(jnp.bfloat16)
    qkv = jnp.dot(normed_one, full_qkv, preferred_element_type=jnp.float32).astype(jnp.bfloat16)
    query_heads = qkv[:, : w_query.shape[1]].reshape(row_count, heads_here, head_dim)
    key_rows = qkv[:, w_query.shape[1] : w_query.shape[1] + head_dim]
    value_rows = qkv[:, w_query.shape[1] + head_dim :]
    visible = visible_pairs(lengths[0], row_count)[None]
    masked = masked_scores(query_heads, key_rows, visible, score_scale)
    row_max = jnp.max(masked, axis=2, keepdims=True)
    weights_exp = jnp.exp(masked - row_max)
    row_total = jnp.sum(weights_exp, axis=2, keepdims=True)
    probs_first = (weights_exp / row_total).astype(jnp.bfloat16)
    log_total = row_max + jnp.log(row_total)
    context = jnp.einsum("hqk,kd->qhd", probs_first, value_rows, preferred_element_type=jnp.float32)
    context = context.reshape(row_count, heads_here * head_dim).astype(jnp.bfloat16)
    attn_output = tensor_sum(right_product(context, full_out))
    resid_mid = resid_in + attn_output
    normed_two = layer_norm(resid_mid, second_gain, second_shift).astype(jnp.bfloat16)
    hidden_pre = jnp.dot(normed_two, full_up, preferred_element_type=jnp.float32)
    active = gelu_tanh(hidden_pre).astype(jnp.bfloat16)
    grad_out = grad_here.astype(jnp.float32)
    grad_here, wdown_term = lax.optimization_barrier((grad_here, weight_term(grad_here, active)))
    grad_wdown = summed_rows(wdown_term)
    grad_active = jnp.dot(grad_here, full_down, preferred_element_type=jnp.float32)
    gelu_back = jax.vjp(gelu_tanh, hidden_pre)[1]
    grad_up = gelu_back(grad_active)[0].astype(jnp.bfloat16)
    norm_two_part = right_product(grad_up, full_up)
    grad_norm_two, wup_term = tensor_sum(norm_two_part, weight_term(normed_two, grad_up))
    grad_wup = summed_rows(wup_term)
    norm_two_back = jax.vjp(layer_norm, resid_mid, second_gain, second_shift)[1]
    grad_mid_norm, grad_gain_two, grad_shift_two = norm_two_back(grad_norm_two)
    grad_mid = grad_out + grad_mid_norm
    grad_mid_low = grad_mid.astype(jnp.bfloat16)
    grad_context = jnp.dot(grad_mid_low, full_out, preferred_element_type=jnp.float32)
    grad_context = grad_context.astype(jnp.bfloat16)
    grad_ctx_heads = grad_context.reshape(row_count, heads_here, head_dim)
    masked_again = masked_scores(query_heads, key_rows, visible, score_scale)
    probs_again = jnp.exp(masked_again - log_total)
    probs_low = probs_again.astype(jnp.bfloat16)
    grad_probs = jnp.einsum(
        "qhd,kd->hqk", grad_ctx_heads, value_rows, preferred_element_type=jnp.float32
    )
    row_delta = jnp.sum(grad_probs * probs_again, axis=2, keepdims=True)
    grad_scores = (probs_again * (grad_probs - row_delta)).astype(jnp.bfloat16)
    grad_query = (
        jnp.einsum("hqk,kd->qhd", grad_scores, key_rows, preferred_element_type=jnp.float32)
        * score_scale
    )
    grad_query = grad_query.reshape(row_count, heads_here * head_dim).astype(jnp.bfloat16)
    grad_keys = (
        jnp.einsum("hqk,qhd->kd", grad_scores, query_heads, preferred_element_type=jnp.float32)
        * score_scale
    )
    grad_values = jnp.einsum(
        "hqk,qhd->kd", probs_low, grad_ctx_heads, preferred_element_type=jnp.float32
    )
    grad_keyval_part = jnp.concatenate([grad_keys, grad_values], axis=1)
    grad_keyval_low = tensor_sum(grad_keyval_part).astype(jnp.bfloat16)
    grad_qkv_part = jnp.concatenate([grad_query, grad_keyval_part.astype(jnp.bfloat16)], axis=1)
    grad_norm_one, wo_term = tensor_sum(
        right_product(grad_qkv_part, full_qkv), weight_term(grad_mid_low, context)
    )
    grad_wo = summed_rows(wo_term)
    norm_one_back = jax.vjp(layer_norm, resid_in, first_gain, first_shift)[1]
    grad_in_norm, grad_gain_one, grad_shift_one = norm_one_back(grad_norm_one)
    grad_resid = (grad_mid + grad_in_norm).astype(jnp.bfloat16)
    mlp_output = tensor_sum(right_product(active, full_down))
    result = (resid_mid + mlp_output).astype(jnp.bfloat16)
    grad_qkv = jnp.concatenate([grad_query, grad_keyval_low], axis=1)
    last_rows = summed_rows(
        jnp.concatenate(
            [
                weight_term(normed_one, grad_qkv),
                as_columns((grad_gain_one, grad_shift_one, grad_gain_two, grad_shift_two)),
            ],
            axis=1,
        ),
    )
    norm_grads = last_rows[:, qkv_cols : qkv_cols + 4].T
    returned = (
        lax.all_to_all(result[recv_order], "dp", split_axis=0, concat_axis=0, tiled=True),
        lax.all_to_all(grad_resid[recv_order], "dp", split_axis=0, concat_axis=0, tiled=True),
    )
    restore = jnp.argsort(send_order, stable=True)
    output = returned[0][restore]
    grad_tokens = returned[1][restore]
    return (
        output,
        grad_tokens,
        last_rows[:, : w_query.shape[1]],
        last_rows[:, w_query.shape[1] : qkv_cols],
        grad_wo,
        grad_wup,
        grad_wdown,
        norm_grads[0],
        norm_grads[1],
        norm_grads[2],
        norm_grads[3],
    )


def solution(mesh):
    placed = (
        P("dp", None),
        P("dp", None),
        P("dp", "tensor"),
        P("dp", None),
        P("dp", "tensor"),
        P("dp", "tensor"),
        P("dp", "tensor"),
        P("dp"),
        P("dp"),
        P("dp"),
        P("dp"),
        P(),
        P("dp", None),
    )

    return jax.shard_map(
        per_device,
        mesh=mesh,
        in_specs=placed,
        out_specs=(
            P("dp", None),
            P("dp", None),
            P("dp", "tensor"),
            P("dp", None),
            P("dp", "tensor"),
            P("dp", "tensor"),
            P("dp", "tensor"),
            P("dp"),
            P("dp"),
            P("dp"),
            P("dp"),
        ),
        check_vma=False,
    )
```

time: 1990 us -> 1390 us (0.70)
  blocking collectives: 342 us -> 0 us
  waiting for transfers between devices: 1180 us -> 877 us
  starting transfers between devices: 23.9 us -> 50.3 us
    psum x4 -> x0, waiting for transfers between devices: 316 us -> none  [the longest x1 120 us: per_device(): grad_norm_two = lax.psum(right_product(grad_up, back_up), 'tensor')]
    reduce_scatter x1 -> x3, waiting for transfers between devices: 635 us -> 343 us  [summed_rows(): total = lax.psum_scatter(low, 'dp', scatter_dimension=0, tiled=True)]
    all_gather x4 -> x0, blocking collectives: 218 us -> none  [the longest x1 69.7 us: per_device(): lax.all_gather(norm1_bias.astype(jnp.bfloat16), 'dp', axis=0, tiled=True)]
    ppermute x0 -> x5, waiting for transfers between devices: none -> 206 us  [tensor_sum(): other = lax.ppermute(own, 'tensor', [(0, 1), (1, 0)])]
    unnamed x1 -> x0, blocking collectives: 101 us -> none
    all_to_all x1, waiting for transfers between devices: 0.01 us -> 77.2 us  [per_device(): lax.all_to_all(grad_resid[recv_order], 'dp', split_axis=0, concat_axis=0,...]
    all_gather x1, waiting for transfers between devices: 108 us -> 42.8 us  [per_device(): lax.all_gather(w_up.astype(jnp.bfloat16), 'dp', axis=0, tiled=True)]
    all_to_all x1, waiting for transfers between devices: 0.01 us -> 55.4 us  [per_device(): lax.all_to_all(tokens[send_order], 'dp', split_axis=0, concat_axis=0, til...]
  transfers between devices with their start and end apart: 14 -> 17, of which waited for: 7 -> 13; matrix products, arithmetic and copies ran while one was open for 14% -> 23% of each run, Pallas kernels for 0% -> 0%
where the time goes in v1:
time: 1390 us; the launch traced here: 1380 us
  waiting for transfers between devices  877 us (63%)
  matrix products  231 us (17%)
  other arithmetic  118 us (8%)
  local copies, waits for them, and re-layouts  90.8 us (7%)
  starting transfers between devices  50.3 us (4%)
  between operations  15 us (1%)
    reduce_scatter x3, waiting for transfers between devices, summed_rows(): total = lax.psum_scatter(low, 'dp', scatter_dimension=0, tiled=True)  343 us
    ppermute x5, waiting for transfers between devices, tensor_sum(): other = lax.ppermute(own, 'tensor', [(0, 1), (1, 0)])  206 us
    all_gather x1, waiting for transfers between devices, per_device(): lax.all_gather(w_down.astype(jnp.bfloat16), 'dp', axis=0, tiled=True)  83.1 us
    all_to_all x1, waiting for transfers between devices, per_device(): lax.all_to_all(grad_resid[recv_order], 'dp', split_axis=0, concat_axis=0,...  77.2 us
    dot_general x4, matrix products, right_product(): lax.dot_general(first_op, second_op, (((1,), (1,)), ((), ())), preferred_...  63.4 us
    dot_general x4, matrix products, left_product(): lax.dot_general(first_op, second_op, (((0,), (0,)), ((), ())), preferred_...  55.6 us
    all_to_all x1, waiting for transfers between devices, per_device(): lax.all_to_all(tokens[send_order], 'dp', split_axis=0, concat_axis=0, til...  55.4 us
    all_to_all x1, waiting for transfers between devices, per_device(): lax.all_to_all(result[recv_order], 'dp', split_axis=0, concat_axis=0, til...  48.7 us
  transfers between devices with their start and end apart: 17, of which 13 were waited for; matrix products, arithmetic and copies ran while one was open for 23% of the time, Pallas kernels for 0%

profile of v1, /device:TPU:0, one launch (start us, length us, event | category | flops | bytes accessed | tf_op | source)
XLA Modules:
  0.0 1382.0 jit_solution(12695282535610113549)
XLA Ops:
  43.9 9.5 gather_fusion.4
  63.5 55.4 %all-to-all-done = bf16[16,48,2048]{2,1,0:T(8,128)(2,1)S(1)} async-done(((bf16[16,48,2048]{2,1,0:T(8,128)(2,1)}), bf16[16,48,2048]{2,1,0:T(8,128)(2,1)S(1)}, u32[]{:S(2)}, u32[]{:S(2)}) %all-to-all-start) | async-done | bytes 3145760 | tf_op jit(solution)/shard_map/all_to_all | solution.py:113
  118.9 15.8 %all-to-all-start.2 = ((bf16[16,48,2048]{2,1,0:T(8,128)(2,1)}), bf16[16,48,2048]{2,1,0:T(8,128)(2,1)}, u32[]{:S(2)}, u32[]{:S(2)}) async-start(bf16[16,48,2048]{2,1,0:T(8,128)(2,1)} %bitcast.98), calls=%async_computation.2 | async-start | bytes 6291456 | tf_op jit(solution)/shard_map/all_to_all | solution.py:114
  160.6 11.1 fusion.79
  171.7 8.9 fusion.3
  180.6 11.4 fusion.49
  192.0 19.1 %all-gather.7.cloned.1.call-done = bf16[2048,1024]{1,0:T(8,128)(2,1)} async-done(((bf16[128,1024]{1,0:T(8,128)(2,1)}), bf16[2048,1024]{1,0:T(8,128)(2,1)}) %all-gather.7.cloned.1.call-update) | async-done | bytes 4194320 | tf_op jit(solution)/shard_map/all_gather | solution.py:103
  220.6 9.9 gather_fusion.5
  231.1 58.6 %collective-permute-done = bf16[768,2048]{1,0:T(8,128)(2,1)} collective-permute-done((bf16[768,2048]{1,0:T(8,128)(2,1)}, bf16[768,2048]{1,0:T(8,128)(2,1)}, u32[]{:S(2)}, u32[]{:S(2)}) %collective-permute-start) | collective-permute-done | bytes 3145760 | tf_op jit(solution)/shard_map/ppermute | solution.py:48
  297.5 42.8 %all-gather.9.cloned.1.call-done = bf16[2048,4096]{1,0:T(8,128)(2,1)} async-done(((bf16[128,4096]{1,0:T(8,128)(2,1)}), bf16[2048,4096]{1,0:T(8,128)(2,1)}) %all-gather.9.cloned.1.call-update) | async-done | bytes 16777232 | tf_op jit(solution)/shard_map/all_gather | solution.py:104
  340.3 21.6 %fusion.76 = f32[768,4096]{1,0:T(8,128)} fusion(bf16[2048,4096]{1,0:T(8,128)(2,1)} %all-gather.9.cloned.1.call-done, f32[768,2048]{1,0:T(8,128)} %copy-done.4, f32[2048]{0:T(1024)S(1)} %get-tuple-element.84, f32[2048]{0:T(1024)S(1)} %get-tuple-element.83, f32[768]{0:T(1024)S(1)} %fusion.70, f32[768]{0:T(1024)S(1)} %broadcast_multiply_fusion), kind=kOutput, calls=%fused_computation.151 | convolution fusion | flops 12892766208 | bytes 35674112 | tf_op jit(solution)/shard_map/dot_general | solution.py:145
  361.9 21.9 %convolution_convert_fusion.1 = bf16[2048,4096]{1,0:T(8,128)(2,1)} fusion(bf16[768,2048]{1,0:T(8,128)(2,1)S(1)} %copy-done.6, f32[768,4096]{1,0:T(8,128)} %fusion.76), kind=kOutput, calls=%fused_computation.21 | convolution fusion | flops 12921602048 | bytes 32505856 | tf_op jit(solution)/shard_map/dot_general | solution.py:34
  383.8 83.1 %all-gather.11.cloned.1.call-done = bf16[2048,4096]{1,0:T(8,128)(2,1)} async-done(((bf16[128,4096]{1,0:T(8,128)(2,1)}), bf16[2048,4096]{1,0:T(8,128)(2,1)}) %all-gather.11.cloned.1.call-update) | async-done | bytes 16777232 | tf_op jit(solution)/shard_map/all_gather | solution.py:105
  467.0 27.1 %fusion.11 = bf16[768,4096]{1,0:T(8,128)(2,1)} fusion(f32[768,4096]{1,0:T(8,128)} %fusion.76, bf16[768,2048]{1,0:T(8,128)(2,1)S(1)} %copy-done.6, bf16[2048,4096]{1,0:T(8,128)(2,1)} %all-gather.11.cloned.1.call-done), kind=kOutput, calls=%fused_computation.29 | convolution fusion | flops 12947816448 | bytes 38797312 | tf_op jit(solution)/shard_map/dot_general | solution.py:150
  494.0 18.7 %convolution_convert_fusion.4 = bf16[768,2048]{1,0:T(8,128)(2,1)S(1)} fusion(bf16[768,4096]{1,0:T(8,128)(2,1)} %fusion.11, bf16[2048,4096]{1,0:T(8,128)(2,1)} %all-gather.9.cloned.1.call-done), kind=kOutput, calls=%fused_computation.69 | convolution fusion | flops 12886474752 | bytes 26214400 | tf_op jit(solution)/shard_map/dot_general | solution.py:28
  514.3 30.8 %convolution_convert_fusion.5 = bf16[768,2048]{1,0:T(8,128)(2,1)} fusion(bf16[2048,4096]{1,0:T(8,128)(2,1)} %all-gather.11.cloned.1.call-done, f32[768,4096]{1,0:T(8,128)} %fusion.76), kind=kOutput, calls=%fused_computation.70 | convolution fusion | flops 12914786304 | bytes 32505856 | tf_op jit(solution)/shard_map/dot_general | solution.py:28
  546.1 21.3 %convolution_convert_fusion = bf16[2048,4096]{1,0:T(8,128)(2,1)} fusion(bf16[768,4096]{1,0:T(8,128)(2,1)} %fusion.11, f32[768,2048]{1,0:T(8,128)} %copy-done.4, f32[2048]{0:T(1024)S(1)} %get-tuple-element.84, f32[2048]{0:T(1024)S(1)} %get-tuple-element.83, f32[768]{0:T(1024)S(1)} %fusion.70, f32[768]{0:T(1024)S(1)} %broadcast_multiply_fusion), kind=kOutput, calls=%fused_computation.20 | convolution fusion | flops 12901154816 | bytes 29382656 | tf_op jit(solution)/shard_map/dot_general | solution.py:34
  567.4 16.5 %collective-permute-done.2 = bf16[768,2048]{1,0:T(8,128)(2,1)} collective-permute-done((bf16[768,2048]{1,0:T(8,128)(2,1)S(1)}, bf16[768,2048]{1,0:T(8,128)(2,1)}, u32[]{:S(2)}, u32[]{:S(2)}) %collective-permute-start.2) | collective-permute-done | bytes 3145760 | tf_op jit(solution)/shard_map/ppermute | solution.py:48
  589.8 60.8 %collective-permute-done.1 = bf16[768,2048]{1,0:T(8,128)(2,1)} collective-permute-done((bf16[768,2048]{1,0:T(8,128)(2,1)}, bf16[768,2048]{1,0:T(8,128)(2,1)}, u32[]{:S(2)}, u32[]{:S(2)}) %collective-permute-start.1) | collective-permute-done | bytes 3145760 | tf_op jit(solution)/shard_map/ppermute | solution.py:48
  670.8 10.2 fusion.54
  681.0 12.9 fusion
  693.8 12.9 fusion.2
  725.1 63.0 %collective-permute-done.3 = bf16[768,2048]{1,0:T(8,128)(2,1)} collective-permute-done((bf16[768,2048]{1,0:T(8,128)(2,1)}, bf16[768,2048]{1,0:T(8,128)(2,1)}, u32[]{:S(2)}, u32[]{:S(2)}) %collective-permute-start.3) | collective-permute-done | bytes 3145760 | tf_op jit(solution)/shard_map/ppermute | solution.py:48
  818.8 8.4 copy.84
  837.1 9.5 add_convert_fusion
  846.6 9.4 gather_fusion.6
  856.0 48.7 %all-to-all-done.1 = bf16[16,48,2048]{2,1,0:T(8,128)(2,1)S(1)} async-done(((bf16[16,48,2048]{2,1,0:T(8,128)(2,1)}), bf16[16,48,2048]{2,1,0:T(8,128)(2,1)S(1)}, u32[]{:S(2)}, u32[]{:S(2)}) %all-to-all-start.1) | async-done | bytes 3145760 | tf_op jit(solution)/shard_map/all_to_all | solution.py:207
  904.7 15.4 %all-to-all-start.3 = ((bf16[16,48,2048]{2,1,0:T(8,128)(2,1)}), bf16[16,48,2048]{2,1,0:T(8,128)(2,1)}, u32[]{:S(2)}, u32[]{:S(2)}) async-start(bf16[16,48,2048]{2,1,0:T(8,128)(2,1)} %bitcast.100), calls=%async_computation.3 | async-start | bytes 6291456 | tf_op jit(solution)/shard_map/all_to_all | solution.py:208
  928.7 77.2 %all-to-all-done.3 = bf16[16,48,2048]{2,1,0:T(8,128)(2,1)} async-done(((bf16[16,48,2048]{2,1,0:T(8,128)(2,1)}), bf16[16,48,2048]{2,1,0:T(8,128)(2,1)}, u32[]{:S(2)}, u32[]{:S(2)}) %all-to-all-start.3) | async-done | bytes 3145760 | tf_op jit(solution)/shard_map/all_to_all | solution.py:208
  1005.9 9.5 gather_fusion.7
  1025.9 165.7 %reduce-scatter.11.cloned.1.call-done = bf16[128,4096]{1,0:T(8,128)(2,1)} async-done(((bf16[2048,4096]{1,0:T(8,128)(2,1)}), bf16[128,4096]{1,0:T(8,128)(2,1)}) %reduce-scatter.11.cloned.1.call-update) | async-done | bytes 1048592 | tf_op jit(solution)/shard_map/reduce_scatter | solution.py:58
  1194.4 177.8 %reduce-scatter.9.cloned.1.call-done = bf16[128,4096]{1,0:T(8,128)(2,1)} async-done(((bf16[2048,4096]{1,0:T(8,128)(2,1)}), bf16[128,4096]{1,0:T(8,128)(2,1)}) %reduce-scatter.9.cloned.1.call-update) | async-done | bytes 1048592 | tf_op jit(solution)/shard_map/reduce_scatter | solution.py:58
  (196 shorter events, 202.0 us)
Async XLA Ops:
  7.2 16.5 %copy-start = (bf16[768,2048]{1,0:T(8,128)(2,1)S(1)}, bf16[768,2048]{1,0:T(8,128)(2,1)}, u32[]{:S(2)}) copy-start(bf16[768,2048]{1,0:T(8,128)(2,1)} %param.13) | copy-start | bytes 9437188
  7.2 137.7 %all-gather.5.cloned.1.call-start = ((), (), s32[]{:S(2)}) async-start(), calls=%async_computation.8 | async-start | bytes 6127616 | tf_op jit(solution)/shard_map/all_gather | solution.py:102
  11.8 199.4 %all-gather.7.cloned.1.call-start = ((), (), s32[]{:S(2)}) async-start(), calls=%async_computation.9 | async-start | bytes 4456448 | tf_op jit(solution)/shard_map/all_gather | solution.py:103
  13.6 326.7 %all-gather.9.cloned.1.call-start = ((), (), s32[]{:S(2)}) async-start(), calls=%async_computation.10 | async-start | bytes 17825792 | tf_op jit(solution)/shard_map/all_gather | solution.py:104
  16.4 450.5 %all-gather.11.cloned.1.call-start = ((), (), s32[]{:S(2)}) async-start(), calls=%async_computation.11 | async-start | bytes 17825792 | tf_op jit(solution)/shard_map/all_gather | solution.py:105
  27.9 91.0 %all-to-all-start = ((bf16[16,48,2048]{2,1,0:T(8,128)(2,1)}), bf16[16,48,2048]{2,1,0:T(8,128)(2,1)S(1)}, u32[]{:S(2)}, u32[]{:S(2)}) async-start(bf16[16,48,2048]{2,1,0:T(8,128)(2,1)} %bitcast.99), calls=%async_computation | async-start | bytes 6291456 | tf_op jit(solution)/shard_map/all_to_all | solution.py:113
  57.8 81.1 %copy-start.32 = (s32[768]{0:T(1024)}, s32[768]{0:T(1024)S(1)}, u32[]{:S(2)}) copy-start(s32[768]{0:T(1024)S(1)} %get-tuple-element.24) | copy-start | bytes 9220
  118.9 101.8 %all-to-all-start.2 = ((bf16[16,48,2048]{2,1,0:T(8,128)(2,1)}), bf16[16,48,2048]{2,1,0:T(8,128)(2,1)}, u32[]{:S(2)}, u32[]{:S(2)}) async-start(bf16[16,48,2048]{2,1,0:T(8,128)(2,1)} %bitcast.98), calls=%async_computation.2 | async-start | bytes 6291456 | tf_op jit(solution)/shard_map/all_to_all | solution.py:114
  134.7 880.8 %reduce-scatter.7.cloned.1.call-start = ((), (), s32[]{:S(2)}) async-start(), calls=%async_computation.12 | async-start | bytes 4456448 | tf_op jit(solution)/shard_map/reduce_scatter | solution.py:58
  219.2 70.6 %collective-permute-start = (bf16[768,2048]{1,0:T(8,128)(2,1)}, bf16[768,2048]{1,0:T(8,128)(2,1)}, u32[]{:S(2)}, u32[]{:S(2)}) collective-permute-start(bf16[768,2048]{1,0:T(8,128)(2,1)} %convolution_convert_fusion.6), channel_id=1, source_target_pairs={{0,1},{1,0},{2,3},{3,2},{4,5},{5,4},{6,7},{7,6},{8,9},{9,8},{10,11... | collective-permute-start | bytes 9437192 | tf_op jit(solution)/shard_map/ppermute | solution.py:48
  297.5 64.4 %copy-start.28 = (f32[768]{0:T(1024)}, f32[768]{0:T(1024)S(1)}, u32[]{:S(2)}) copy-start(f32[768]{0:T(1024)S(1)} %multiply_reduce_fusion.2) | copy-start | bytes 9220
  340.3 21.6 %copy-start.6 = (bf16[768,2048]{1,0:T(8,128)(2,1)S(1)}, bf16[768,2048]{1,0:T(8,128)(2,1)}, u32[]{:S(2)}) copy-start(bf16[768,2048]{1,0:T(8,128)(2,1)} %gather_fusion.5) | copy-start | bytes 9437188
  512.8 71.2 %copy-start.9 = (bf16[768,2048]{1,0:T(8,128)(2,1)}, bf16[768,2048]{1,0:T(8,128)(2,1)S(1)}, u32[]{:S(2)}) copy-start(bf16[768,2048]{1,0:T(8,128)(2,1)S(1)} %convolution_convert_fusion.4) | copy-start | bytes 9437188
  512.8 71.1 %collective-permute-start.2 = (bf16[768,2048]{1,0:T(8,128)(2,1)S(1)}, bf16[768,2048]{1,0:T(8,128)(2,1)}, u32[]{:S(2)}, u32[]{:S(2)}) collective-permute-start(bf16[768,2048]{1,0:T(8,128)(2,1)S(1)} %convolution_convert_fusion.4), channel_id=1, source_target_pairs={{0,1},{1,0},{2,3},{3,2},{4,5},{5,4},{6,7},{7,6},{8,9},{9,8},{10,11... | collective-permute-start | bytes 9437192 | tf_op jit(solution)/shard_map/ppermute | solution.py:48
  545.1 105.5 %collective-permute-start.1 = (bf16[768,2048]{1,0:T(8,128)(2,1)}, bf16[768,2048]{1,0:T(8,128)(2,1)}, u32[]{:S(2)}, u32[]{:S(2)}) collective-permute-start(bf16[768,2048]{1,0:T(8,128)(2,1)} %convolution_convert_fusion.5), channel_id=1, source_target_pairs={{0,1},{1,0},{2,3},{3,2},{4,5},{5,4},{6,7},{7,6},{8,9},{9,8},{10,11... | collective-permute-start | bytes 9437192 | tf_op jit(solution)/shard_map/ppermute | solution.py:48
  567.4 22.4 %copy-start.29 = (f32[768]{0:T(1024)S(1)}, f32[768]{0:T(1024)}, u32[]{:S(2)}) copy-start(f32[768]{0:T(1024)} %copy-done.28) | copy-start | bytes 9220
  567.4 83.2 %copy-start.11 = (bf16[768,2048]{1,0:T(8,128)(2,1)S(1)}, bf16[768,2048]{1,0:T(8,128)(2,1)}, u32[]{:S(2)}) copy-start(bf16[768,2048]{1,0:T(8,128)(2,1)} %convolution_convert_fusion.5) | copy-start | bytes 9437188
  589.8 68.1 %copy-start.7 = (bf16[768,2048]{1,0:T(8,128)(2,1)S(1)}, bf16[768,2048]{1,0:T(8,128)(2,1)}, u32[]{:S(2)}) copy-start(bf16[768,2048]{1,0:T(8,128)(2,1)} %gather_fusion.5) | copy-start | bytes 9437188
  680.9 31.5 %slice-start = ((s8[5767168]{0:T(1024)(128)(4,1)}), s8[4194304]{0:T(1024)(128)(4,1)S(1)}, s32[]{:S(2)}) async-start(s8[5767168]{0:T(1024)(128)(4,1)} %bitcast.106), calls=%async_computation.16 | async-start | bytes 8388608
  693.8 18.6 %slice-start.1 = ((s8[5767168]{0:T(1024)(128)(4,1)}), s8[1572864]{0:T(1024)(128)(4,1)S(1)}, s32[]{:S(2)}) async-start(s8[5767168]{0:T(1024)(128)(4,1)} %bitcast.106), calls=%async_computation.17 | async-start | bytes 3145728
  718.3 79.6 %copy-start.18 = (f32[2048]{0:T(1024)S(1)}, f32[2048]{0:T(1024)}, u32[]{:S(2)}) copy-start(f32[2048]{0:T(1024)} %copy-done.17) | copy-start | bytes 24580
  718.3 79.6 %copy-start.20 = (f32[768]{0:T(1024)S(1)}, f32[768]{0:T(1024)}, u32[]{:S(2)}) copy-start(f32[768]{0:T(1024)} %copy-done.19) | copy-start | bytes 9220
  718.3 79.6 %copy-start.23 = (f32[768]{0:T(1024)S(1)}, f32[768]{0:T(1024)}, u32[]{:S(2)}) copy-start(f32[768]{0:T(1024)} %copy-done.22) | copy-start | bytes 9220
  718.4 69.8 %collective-permute-start.3 = (bf16[768,2048]{1,0:T(8,128)(2,1)}, bf16[768,2048]{1,0:T(8,128)(2,1)}, u32[]{:S(2)}, u32[]{:S(2)}) collective-permute-start(bf16[768,2048]{1,0:T(8,128)(2,1)} %fusion.37), channel_id=1, source_target_pairs={{0,1},{1,0},{2,3},{3,2},{4,5},{5,4},{6,7},{7,6},{8,9},{9,8},{10,11... | collective-permute-start | bytes 9437192 | tf_op jit(solution)/shard_map/ppermute | solution.py:48
  788.2 229.1 %reduce-scatter.13.cloned.1.call-start = ((), (), s32[]{:S(2)}) async-start(), calls=%async_computation.15 | async-start | bytes 6127616
  788.2 9.6 collective-permute-start.4
  827.2 364.4 %reduce-scatter.11.cloned.1.call-start = ((), (), s32[]{:S(2)}) async-start(), calls=%async_computation.14 | async-start | bytes 17825792 | tf_op jit(solution)/shard_map/reduce_scatter | solution.py:58
  828.0 544.2 %reduce-scatter.9.cloned.1.call-start = ((), (), s32[]{:S(2)}) async-start(), calls=%async_computation.13 | async-start | bytes 17825792 | tf_op jit(solution)/shard_map/reduce_scatter | solution.py:58
  833.0 71.7 %all-to-all-start.1 = ((bf16[16,48,2048]{2,1,0:T(8,128)(2,1)}), bf16[16,48,2048]{2,1,0:T(8,128)(2,1)S(1)}, u32[]{:S(2)}, u32[]{:S(2)}) async-start(bf16[16,48,2048]{2,1,0:T(8,128)(2,1)} %bitcast.101), calls=%async_computation.1 | async-start | bytes 6291456 | tf_op jit(solution)/shard_map/all_to_all | solution.py:207
  856.0 64.1 %copy-start.31 = (s32[768]{0:T(1024)S(1)}, s32[768]{0:T(1024)}, u32[]{:S(2)}) copy-start(s32[768]{0:T(1024)} %copy-done.30) | copy-start | bytes 9220
  904.7 101.3 %all-to-all-start.3 = ((bf16[16,48,2048]{2,1,0:T(8,128)(2,1)}), bf16[16,48,2048]{2,1,0:T(8,128)(2,1)}, u32[]{:S(2)}, u32[]{:S(2)}) async-start(bf16[16,48,2048]{2,1,0:T(8,128)(2,1)} %bitcast.100), calls=%async_computation.3 | async-start | bytes 6291456 | tf_op jit(solution)/shard_map/all_to_all | solution.py:208
  1005.9 369.0 %copy-start.1 = (bf16[768,2048]{1,0:T(8,128)(2,1)S(1)}, bf16[768,2048]{1,0:T(8,128)(2,1)}, u32[]{:S(2)}) copy-start(bf16[768,2048]{1,0:T(8,128)(2,1)} %param.13) | copy-start | bytes 9437188
  (25 other events, 157.5 us)
Sparse Core Ops, SparseCore 0:
  11.9 107.1 all-gather.4
  121.9 89.2 all-gather.6
  213.3 126.9 all-gather.8
  342.3 124.5 all-gather.10
  788.3 91.1 reduce-scatter.6
  883.2 127.5 reduce-scatter.12
  1014.9 176.6 reduce-scatter.10
  1195.7 176.3 reduce-scatter.8

commit v2 on v1

--- a/solution.py
+++ b/solution.py
@@ -17,9 +17,8 @@
     return jax.nn.gelu(values, approximate=True)
 
 
-def visible_pairs(lengths_row, row_count):
+def visible_pairs(lengths_row, places):
     boundaries = jnp.cumsum(lengths_row)
-    places = jnp.arange(row_count, dtype=jnp.int32)
     segment = jnp.sum((places[:, None] >= boundaries[None, :]).astype(jnp.int32), axis=1)
     return jnp.logical_and(segment[:, None] == segment[None, :], places[None, :] <= places[:, None])
 
@@ -44,19 +43,59 @@
 def tensor_sum(values, ride_along=None):
     own = lax.optimization_barrier(values.astype(jnp.bfloat16))
     total = own.astype(jnp.float32)
-    if lax.axis_size("tensor") == 2:
-        other = lax.ppermute(own, "tensor", [(0, 1), (1, 0)])
-        if ride_along is not None:
-            other, ride_along = lax.optimization_barrier((other, ride_along))
-        summed = total + other.astype(jnp.float32)
-    else:
-        summed = lax.psum(own, "tensor").astype(jnp.float32)
+    other = swap_tensor(own)
+    if ride_along is not None:
+        other, ride_along = lax.optimization_barrier((other, ride_along))
+    summed = total + other.astype(jnp.float32)
     return summed if ride_along is None else (summed, ride_along)
 
 
+def swap_cores(values):
+    members = lax.axis_size("dp")
+    return lax.ppermute(values, "dp", [(i, i ^ 1) for i in range(members)])
+
+
+def column_half(values, half):
+    width = values.shape[1] // 2
+    return lax.dynamic_slice_in_dim(values, half * width, width, axis=1)
+
+
+def own_rows(values, part, parts):
+    count = values.shape[0] // parts
+    return lax.dynamic_slice_in_dim(values, part * count, count, axis=0)
+
+
+def both_cores(values):
+    return jnp.concatenate([values, swap_cores(values)], axis=0)
+
+
+def half_of_both(values, core):
+    other = swap_cores(column_half(values, 1 - core))
+    return jnp.concatenate([column_half(values, core), other], axis=0)
+
+
 def summed_rows(low):
-    total = lax.psum_scatter(low, "dp", scatter_dimension=0, tiled=True)
-    return total.astype(jnp.float32)
+    members = lax.axis_size("dp")
+    groups = [list(range(core, members, 2)) for core in range(2)]
+    return lax.psum_scatter(low, "dp", scatter_dimension=0, axis_index_groups=groups, tiled=True)
+
+
+def own_columns(chip_rows, core):
+    kept = own_rows(chip_rows, core, 2)
+    other = swap_cores(own_rows(chip_rows, 1 - core, 2))
+    first = jnp.where(core == 0, kept, other)
+    second = jnp.where(core == 0, other, kept)
+    return jnp.concatenate([first, second], axis=1).astype(jnp.float32)
+
+
+def swap_tensor(values):
+    return lax.ppermute(values, "tensor", [(0, 1), (1, 0)])
+
+
+def tensor_rows(values, place):
+    low = values.astype(jnp.bfloat16)
+    arriving = swap_tensor(own_rows(low, 1 - place, 2))
+    return own_rows(low, place, 2).astype(jnp.float32) + arriving.astype(jnp.float32)
 
 
 def weight_term(first_op, second_op):
@@ -91,33 +130,58 @@
     heads_here = w_query.shape[1] // head_dim
     score_scale = head_dim ** (-0.5)
     group_index = lax.axis_index("dp")
-    first_block = jnp.concatenate(
-        [
-            w_query.astype(jnp.bfloat16),
-            w_keyval.astype(jnp.bfloat16),
-            as_columns((norm1_gain, norm1_bias, norm2_gain, norm2_bias)),
-        ],
-        axis=1,
-    )
-    full_first = lax.all_gather(first_block, "dp", axis=0, tiled=True)
-    full_out = lax.all_gather(w_out.astype(jnp.bfloat16), "dp", axis=0, tiled=True)
-    full_up = lax.all_gather(w_up.astype(jnp.bfloat16), "dp", axis=0, tiled=True)
-    full_down = lax.all_gather(w_down.astype(jnp.bfloat16), "dp", axis=0, tiled=True)
+    groups = lax.axis_size("dp")
+    core = lax.rem(group_index, 2)
+    place = lax.axis_index("tensor")
+    query_cols = w_query.shape[1]
+    qkv_cols = query_cols + w_keyval.shape[1]
+    up_cols = w_up.shape[1]
+    full_attn = lax.all_gather(
+        jnp.concatenate(
+            [
+                w_query.astype(jnp.bfloat16),
+                w_keyval.astype(jnp.bfloat16),
+                w_out.astype(jnp.bfloat16),
+                as_columns((norm1_gain, norm1_bias, norm2_gain, norm2_bias)),
+            ],
+            axis=1,
+        ),
+        "dp",
+        axis=0,
+        tiled=True,
+    )
+    full_ffn = lax.all_gather(
+        jnp.concatenate([w_up.astype(jnp.bfloat16), w_down.astype(jnp.bfloat16)], axis=1),
+        "dp",
+        axis=0,
+        tiled=True,
+    )
+    full_up = full_ffn[:, :up_cols]
+    full_down = full_ffn[:, up_cols:]
+
+    def by_member(order):
+        return order.reshape(groups, 2, -1).transpose(1, 0, 2)
+
     own_route = lax.dynamic_slice_in_dim(route, group_index * row_count, row_count)
-    send_order = jnp.argsort(own_route, stable=True)
+    send_order = by_member(jnp.argsort(own_route, stable=True))
+    own_sends = lax.dynamic_index_in_dim(send_order, place, keepdims=False).reshape(-1)
+
+    def fetched(rows):
+        mine = lax.all_to_all(rows[own_sends], "dp", split_axis=0, concat_axis=0, tiled=True)
+        other = swap_tensor(mine)
+        first = jnp.where(place == 0, mine, other)
+        second = jnp.where(place == 0, other, mine)
+        return jnp.concatenate([first, second], axis=0)
+
+    tokens_here = fetched(tokens)
+    grad_here = fetched(cotangent)
     inverse = jnp.argsort(route, stable=True)
     sources = lax.dynamic_slice_in_dim(inverse, group_index * row_count, row_count) // row_count
-    recv_order = jnp.argsort(sources, stable=True)
-    placing = jnp.argsort(recv_order, stable=True)
-    arrived = (
-        lax.all_to_all(tokens[send_order], "dp", split_axis=0, concat_axis=0, tiled=True),
-        lax.all_to_all(cotangent[send_order], "dp", split_axis=0, concat_axis=0, tiled=True),
-    )
-    tokens_here = arrived[0][placing]
-    grad_here = arrived[1][placing]
-    qkv_cols = w_query.shape[1] + w_keyval.shape[1]
-    full_qkv = full_first[:, :qkv_cols]
-    norm_rows = full_first[:, qkv_cols : qkv_cols + 4].astype(jnp.float32).T
+    places = by_member(jnp.argsort(sources, stable=True)).reshape(-1).astype(jnp.int32)
+    full_qkv = full_attn[:, :qkv_cols]
+    norm_at = qkv_cols + query_cols
+    full_out = full_attn[:, qkv_cols:norm_at]
+    norm_rows = full_attn[:, norm_at : norm_at + 4].astype(jnp.float32).T
     first_gain, first_shift, second_gain, second_shift = (
         norm_rows[0],
         norm_rows[1],
@@ -127,10 +191,10 @@
     resid_in = tokens_here.astype(jnp.float32)
     normed_one = layer_norm(resid_in, first_gain, first_shift).astype(jnp.bfloat16)
     qkv = jnp.dot(normed_one, full_qkv, preferred_element_type=jnp.float32).astype(jnp.bfloat16)
-    query_heads = qkv[:, : w_query.shape[1]].reshape(row_count, heads_here, head_dim)
-    key_rows = qkv[:, w_query.shape[1] : w_query.shape[1] + head_dim]
-    value_rows = qkv[:, w_query.shape[1] + head_dim :]
-    visible = visible_pairs(lengths[0], row_count)[None]
+    query_heads = qkv[:, :query_cols].reshape(row_count, heads_here, head_dim)
+    key_rows = qkv[:, query_cols : query_cols + head_dim]
+    value_rows = qkv[:, query_cols + head_dim :]
+    visible = visible_pairs(lengths[0], places)[None]
     masked = masked_scores(query_heads, key_rows, visible, score_scale)
     row_max = jnp.max(masked, axis=2, keepdims=True)
     weights_exp = jnp.exp(masked - row_max)
@@ -142,17 +206,21 @@
     attn_output = tensor_sum(right_product(context, full_out))
     resid_mid = resid_in + attn_output
     normed_two = layer_norm(resid_mid, second_gain, second_shift).astype(jnp.bfloat16)
+    both_grads = both_cores(grad_here)
+    both_normed_two = both_cores(normed_two)
     hidden_pre = jnp.dot(normed_two, full_up, preferred_element_type=jnp.float32)
     active = gelu_tanh(hidden_pre).astype(jnp.bfloat16)
     grad_out = grad_here.astype(jnp.float32)
-    grad_here, wdown_term = lax.optimization_barrier((grad_here, weight_term(grad_here, active)))
-    grad_wdown = summed_rows(wdown_term)
+    wdown_term = weight_term(both_grads, half_of_both(active, core))
+    grad_here, wdown_term = lax.optimization_barrier((grad_here, wdown_term))
+    wdown_rows = summed_rows(wdown_term)
     grad_active = jnp.dot(grad_here, full_down, preferred_element_type=jnp.float32)
     gelu_back = jax.vjp(gelu_tanh, hidden_pre)[1]
     grad_up = gelu_back(grad_active)[0].astype(jnp.bfloat16)
     norm_two_part = right_product(grad_up, full_up)
-    grad_norm_two, wup_term = tensor_sum(norm_two_part, weight_term(normed_two, grad_up))
-    grad_wup = summed_rows(wup_term)
+    wup_term = weight_term(both_normed_two, half_of_both(grad_up, core))
+    grad_norm_two, wup_term = tensor_sum(norm_two_part, wup_term)
+    wup_rows = summed_rows(wup_term)
     norm_two_back = jax.vjp(layer_norm, resid_mid, second_gain, second_shift)[1]
     grad_mid_norm, grad_gain_two, grad_shift_two = norm_two_back(grad_norm_two)
     grad_mid = grad_out + grad_mid_norm
@@ -183,38 +251,50 @@
     grad_keyval_part = jnp.concatenate([grad_keys, grad_values], axis=1)
     grad_keyval_low = tensor_sum(grad_keyval_part).astype(jnp.bfloat16)
     grad_qkv_part = jnp.concatenate([grad_query, grad_keyval_part.astype(jnp.bfloat16)], axis=1)
-    grad_norm_one, wo_term = tensor_sum(
-        right_product(grad_qkv_part, full_qkv), weight_term(grad_mid_low, context)
-    )
-    grad_wo = summed_rows(wo_term)
-    norm_one_back = jax.vjp(layer_norm, resid_in, first_gain, first_shift)[1]
+    grad_norm_one = tensor_rows(right_product(grad_qkv_part, full_qkv), place)
+    norm_one_back = jax.vjp(
+        layer_norm, own_rows(resid_in, place, 2), first_gain, first_shift
+    )[1]
     grad_in_norm, grad_gain_one, grad_shift_one = norm_one_back(grad_norm_one)
-    grad_resid = (grad_mid + grad_in_norm).astype(jnp.bfloat16)
-    mlp_output = tensor_sum(right_product(active, full_down))
-    result = (resid_mid + mlp_output).astype(jnp.bfloat16)
+    grad_resid = (own_rows(grad_mid, place, 2) + grad_in_norm).astype(jnp.bfloat16)
+    mlp_output = tensor_rows(right_product(active, full_down), place)
+    result = (own_rows(resid_mid, place, 2) + mlp_output).astype(jnp.bfloat16)
+    norm_one_sums = jnp.stack([grad_gain_one, grad_shift_one])
+    norm_one_sums = norm_one_sums + swap_tensor(norm_one_sums)
+    norm_sums = jnp.concatenate([norm_one_sums, jnp.stack([grad_gain_two, grad_shift_two])])
+    norm_sums = norm_sums + swap_cores(norm_sums)
     grad_qkv = jnp.concatenate([grad_query, grad_keyval_low], axis=1)
     last_rows = summed_rows(
         jnp.concatenate(
             [
-                weight_term(normed_one, grad_qkv),
-                as_columns((grad_gain_one, grad_shift_one, grad_gain_two, grad_shift_two)),
+                weight_term(both_cores(normed_one), half_of_both(grad_qkv, core)),
+                weight_term(both_cores(grad_mid_low), half_of_both(context, core)),
+                as_columns((norm_sums[0], norm_sums[1], norm_sums[2], norm_sums[3])),
             ],
             axis=1,
         ),
     )
-    norm_grads = last_rows[:, qkv_cols : qkv_cols + 4].T
-    returned = (
-        lax.all_to_all(result[recv_order], "dp", split_axis=0, concat_axis=0, tiled=True),
-        lax.all_to_all(grad_resid[recv_order], "dp", split_axis=0, concat_axis=0, tiled=True),
-    )
-    restore = jnp.argsort(send_order, stable=True)
-    output = returned[0][restore]
-    grad_tokens = returned[1][restore]
+    qkv_half = qkv_cols // 2
+    out_end = qkv_half + query_cols // 2
+    grad_wdown = own_columns(wdown_rows, core)
+    grad_wup = own_columns(wup_rows, core)
+    grad_wqkv = own_columns(last_rows[:, :qkv_half], core)
+    grad_wo = own_columns(last_rows[:, qkv_half:out_end], core)
+    norm_grads = own_rows(last_rows[:, out_end : out_end + 4], core, 2).astype(jnp.float32).T
+    restore = jnp.argsort(send_order.reshape(-1), stable=True)
+    restore = lax.rem(restore + place * (row_count // 2), row_count)
+
+    def returned(rows):
+        mine = lax.all_to_all(rows, "dp", split_axis=0, concat_axis=0, tiled=True)
+        return jnp.concatenate([mine, swap_tensor(mine)], axis=0)[restore]
+
+    output = returned(result)
+    grad_tokens = returned(grad_resid)
     return (
         output,
         grad_tokens,
-        last_rows[:, : w_query.shape[1]],
-        last_rows[:, w_query.shape[1] : qkv_cols],
+        grad_wqkv[:, :query_cols],
+        grad_wqkv[:, query_cols:],
         grad_wo,
         grad_wup,
         grad_wdown,

time: 1390 us -> 1110 us (0.80)
  waiting for transfers between devices: 877 us -> 580 us
  blocking collectives: 0 us -> 75.3 us
  local copies, waits for them, and re-layouts: 90.8 us -> 50.6 us
  matrix products: 231 us -> 208 us
    all_gather x4 -> x2, waiting for transfers between devices: 145 us -> 5.7 us  [the longest x1 5.7 us: per_device(): lax.all_gather(jnp.concatenate([w_query.astype(jnp.bfloat16), w_keyval.as...]
    reduce_scatter x3, waiting for transfers between devices: 343 us -> 223 us  [summed_rows(): lax.psum_scatter(low, 'dp', scatter_dimension=0, axis_index_groups=groups...]
    all_to_all x4 -> x3, waiting for transfers between devices: 181 us -> 88.3 us  [the longest x2 88.3 us: returned(): mine = lax.all_to_all(rows, 'dp', split_axis=0, concat_axis=0, tiled=True)]
    all_to_all x0 -> x1, blocking collectives: none -> 75.3 us  [fetched(): lax.all_to_all(rows[own_sends], 'dp', split_axis=0, concat_axis=0, tiled=...]
    ppermute x5 -> x23, waiting for transfers between devices: 206 us -> 262 us  [the longest x10 257 us: swap_tensor(): return lax.ppermute(values, 'tensor', [(0, 1), (1, 0)])]
    gather x8 -> x4, local copies, waits for them, and re-layouts: 55.2 us -> 14.7 us  [the longest x2 8.47 us: returned(): return jnp.concatenate([mine, swap_tensor(mine)], axis=0)[restore]]
    concatenate x1 -> x7, other arithmetic: 2.96 us -> 20 us  [the longest x1 9.44 us: per_device(): jnp.concatenate([weight_term(both_cores(normed_one), half_of_both(grad_qk...]
    all_to_all x4 -> x3, starting transfers between devices: 42.8 us -> 29 us  [the longest x2 21.8 us: returned(): mine = lax.all_to_all(rows, 'dp', split_axis=0, concat_axis=0, tiled=True)]
  transfers between devices with their start and end apart: 17 -> 31, of which waited for: 13 -> 13; matrix products, arithmetic and copies ran while one was open for 23% -> 32% of each run, Pallas kernels for 0% -> 0%
where the time goes in v2:
time: 1110 us
  waiting for transfers between devices  580 us (52%)
  matrix products  208 us (19%)
  other arithmetic  126 us (11%)
  blocking collectives  75.3 us (7%)
  local copies, waits for them, and re-layouts  50.6 us (5%)
  starting transfers between devices  50 us (5%)
  between operations  15.2 us (1%)
    ppermute x10, waiting for transfers between devices, swap_tensor(): return lax.ppermute(values, 'tensor', [(0, 1), (1, 0)])  257 us
    reduce_scatter x3, waiting for transfers between devices, summed_rows(): lax.psum_scatter(low, 'dp', scatter_dimension=0, axis_index_groups=groups...  223 us
    all_to_all x2, waiting for transfers between devices, returned(): mine = lax.all_to_all(rows, 'dp', split_axis=0, concat_axis=0, tiled=True)  88.3 us
    all_to_all x1, blocking collectives, fetched(): lax.all_to_all(rows[own_sends], 'dp', split_axis=0, concat_axis=0, tiled=...  75.3 us
    dot_general x4, matrix products, right_product(): lax.dot_general(first_op, second_op, (((1,), (1,)), ((), ())), preferred_...  50.8 us
    dot_general x4, matrix products, left_product(): lax.dot_general(first_op, second_op, (((0,), (0,)), ((), ())), preferred_...  47.2 us
    dot_general x1, matrix products, per_device(): jnp.dot(grad_here, full_down, preferred_element_type=jnp.float32)  27.6 us
    dot_general x1, matrix products, per_device(): jnp.dot(normed_two, full_up, preferred_element_type=jnp.float32)  23.3 us
  transfers between devices with their start and end apart: 31, of which 13 were waited for; matrix products, arithmetic and copies ran while one was open for 32% of the time, Pallas kernels for 0%

profile of v2, /device:TPU:0, one launch (start us, length us, event | category | flops | bytes accessed | tf_op | source)
XLA Modules:
  0.0 1105.8 jit_solution(6854507046537699456)
XLA Ops:
  24.7 75.3 %all_to_all.48 = bf16[16,24,2048]{2,1,0:T(8,128)(2,1)} all-to-all(bf16[16,24,2048]{2,1,0:T(8,128)(2,1)} %bitcast.112), channel_id=1, replica_groups=mesh['dp'=16,'tensor'=2] {'dp'}, dimensions={0} | all-to-all | bytes 3145728 | tf_op jit(solution)/shard_map/all_to_all | solution.py:170
  104.6 7.2 all-to-all-start.2
  112.4 8.2 sort.63
  126.9 9.8 collective-permute-done
  161.7 11.4 %fusion.129 = (f32[8,768]{1,0:T(8,128)S(1)}, f32[8,768,768]{1,2,0:T(8,128)}) fusion(bf16[768,8,128]{0,2,1:T(8,128)(2,1)} %bitcast.106, bf16[768,1280]{1,0:T(8,128)(2,1)} %copy-done.20, pred[768,768]{0,1:T(8,128)(4,1)} %compare_and_fusion), kind=kOutput, calls=%fused_computation.232 | convolution fusion | flops 1222109184 | bytes 21258240 | tf_op jit(solution)/shard_map/qhd,kd->hqk/dot_general | solution.py:107
  173.1 9.3 fusion.3
  182.4 10.6 fusion.90
  193.0 7.7 fusion.57
  203.0 102.6 %collective-permute-done.4 = bf16[384,2048]{1,0:T(8,128)(2,1)} collective-permute-done((bf16[384,2048]{1,0:T(8,128)(2,1)}, bf16[384,2048]{1,0:T(8,128)(2,1)}, u32[]{:S(2)}, u32[]{:S(2)}) %collective-permute-start.4) | collective-permute-done | bytes 1572896 | tf_op jit(solution)/shard_map/ppermute | solution.py:92
  319.6 23.3 %multiply_convert_fusion = (bf16[768,4096]{1,0:T(8,128)(2,1)}, f32[768,4096]{1,0:T(8,128)}) fusion(bf16[768,2048]{1,0:T(8,128)(2,1)} %add_convert_fusion, bf16[2048,8192]{1,0:T(8,128)(2,1)} %all-gather.5.cloned.1.call-done), kind=kOutput, calls=%fused_computation.32 | convolution fusion | flops 12913213440 | bytes 38797312 | tf_op jit(solution)/shard_map/dot_general | solution.py:211
  352.4 17.8 %convolution_convert_fusion.1 = bf16[2048,2048]{1,0:T(8,128)(2,1)} fusion(bf16[768,2048]{1,0:T(8,128)(2,1)} %collective-permute-done.5, bf16[384,2048]{1,0:T(8,128)(2,1)S(1)} %copy-done.12, bf16[384,2048]{1,0:T(8,128)(2,1)S(1)} %copy-done.10, bf16[768,2048]{1,0:T(8,128)(2,1)S(1)} %collective-permute-done.6, bf16[768,2048]{1,0:T(8,128)(2,1)S(1)} %get-tuple-element.91), kind=kOutput, calls=%fused_computation.38 | convolution fusion | flops 12920553472 | bytes 20971520 | tf_op jit(solution)/shard_map/dot_general | solution.py:33
  370.2 27.6 %fusion.19 = bf16[768,4096]{1,0:T(8,128)(2,1)} fusion(f32[768,4096]{1,0:T(8,128)} %get-tuple-element.120, bf16[768,2048]{1,0:T(8,128)(2,1)} %pad_maximum_fusion.3, bf16[2048,8192]{1,0:T(8,128)(2,1)} %all-gather.5.cloned.1.call-done), kind=kOutput, calls=%fused_computation.31 | convolution fusion | flops 12947816448 | bytes 38797312 | tf_op jit(solution)/shard_map/dot_general | solution.py:217
  397.8 6.6 constant_dynamic-slice_fusion.9
  404.9 19.9 %fusion.66 = bf16[768,2048]{1,0:T(8,128)(2,1)} fusion(bf16[768,4096]{1,0:T(8,128)(2,1)} %fusion.19, bf16[2048,8192]{1,0:T(8,128)(2,1)} %all-gather.5.cloned.1.call-done), kind=kOutput, calls=%fused_computation.85 | convolution fusion | flops 12886474752 | bytes 26214400 | tf_op jit(solution)/shard_map/dot_general | solution.py:27
  426.6 19.8 %convolution_convert_fusion = bf16[2048,2048]{1,0:T(8,128)(2,1)} fusion(bf16[768,2048]{1,0:T(8,128)(2,1)} %collective-permute-done.8, bf16[768,2048]{1,0:T(8,128)(2,1)} %add_convert_fusion, bf16[768,2048]{1,0:T(8,128)(2,1)} %collective-permute-done.9, bf16[768,2048]{1,0:T(8,128)(2,1)} %get-tuple-element.89), kind=kOutput, calls=%fused_computation.37 | convolution fusion | flops 12914262016 | bytes 20971520 | tf_op jit(solution)/shard_map/dot_general | solution.py:33
  446.4 48.8 %collective-permute-done.7 = bf16[768,2048]{1,0:T(8,128)(2,1)} collective-permute-done((bf16[768,2048]{1,0:T(8,128)(2,1)}, bf16[768,2048]{1,0:T(8,128)(2,1)}, u32[]{:S(2)}, u32[]{:S(2)}) %collective-permute-start.7) | collective-permute-done | bytes 3145760 | tf_op jit(solution)/shard_map/ppermute | solution.py:92
  495.2 6.1 multiply_reduce_fusion
  501.3 5.9 fusion.127
  520.8 9.6 fusion.99
  530.4 12.1 %fusion = (f32[8,768]{1,0:T(8,128)S(1)}, f32[768,768,8]{1,0,2:T(8,128)}) fusion(f32[8,768,768]{1,2,0:T(8,128)} %get-tuple-element.118, f32[8,768]{1,0:T(8,128)S(1)} %log_add_fusion, bf16[768,8,128]{0,2,1:T(8,128)(2,1)S(1)} %bitcast.105, bf16[768,1280]{1,0:T(8,128)(2,1)} %copy-done.20), kind=kOutput, calls=%fused_computation.6 | convolution fusion | flops 1222109184 | bytes 39567360 | tf_op jit(solution)/shard_map/qhd,kd->hqk/dot_general | solution.py:234
  542.5 13.0 %fusion.2 = bf16[8,768,768]{1,2,0:T(8,128)(2,1)S(1)} fusion(f32[768,768,8]{1,0,2:T(8,128)} %get-tuple-element.122, f32[8,768,768]{1,2,0:T(8,128)} %get-tuple-element.118, f32[8,768]{1,0:T(8,128)S(1)} %get-tuple-element.121, f32[8,768]{1,0:T(8,128)S(1)} %log_add_fusion), kind=kLoop, calls=%fused_computation.8 | loop fusion | flops 18874368 | bytes 47235072 | tf_op jit(solution)/shard_map/convert_element_type | solution.py:238
  574.0 36.2 %collective-permute-done.13 = bf16[768,256]{0,1:T(8,128)(2,1)S(1)} collective-permute-done((bf16[768,256]{0,1:T(8,128)(2,1)S(1)}, bf16[768,256]{0,1:T(8,128)(2,1)S(1)}, u32[]{:S(2)}, u32[]{:S(2)}) %collective-permute-start.13) | collective-permute-done | bytes 393248 | tf_op jit(solution)/shard_map/ppermute | solution.py:92
  617.9 6.1 fusion.72
  627.7 9.4 pad_maximum_fusion
  638.4 18.6 %fusion.69 = bf16[768,2048]{1,0:T(8,128)(2,1)S(1)} fusion(bf16[768,4096]{1,0:T(8,128)(2,1)} %get-tuple-element.119, bf16[2048,8192]{1,0:T(8,128)(2,1)} %all-gather.5.cloned.1.call-done), kind=kOutput, calls=%fused_computation.86 | convolution fusion | flops 12886474752 | bytes 26214400 | tf_op jit(solution)/shard_map/dot_general | solution.py:27
  658.9 35.0 %collective-permute-done.2 = bf16[384,2048]{1,0:T(8,128)(2,1)S(1)} collective-permute-done((bf16[384,2048]{1,0:T(8,128)(2,1)S(1)}, bf16[384,2048]{1,0:T(8,128)(2,1)S(1)}, u32[]{:S(2)}, u32[]{:S(2)}) %collective-permute-start.2) | collective-permute-done | bytes 1572896 | tf_op jit(solution)/shard_map/ppermute | solution.py:92
  709.6 37.4 %all-to-all-done.1 = bf16[16,24,2048]{2,1,0:T(8,128)(2,1)} async-done(((bf16[16,24,2048]{2,1,0:T(8,128)(2,1)}), bf16[16,24,2048]{2,1,0:T(8,128)(2,1)}, u32[]{:S(2)}, u32[]{:S(2)}) %all-to-all-start.1) | async-done | bytes 1572896 | tf_op jit(solution)/shard_map/all_to_all | solution.py:288
  747.0 17.4 %all-to-all-start.3 = ((bf16[16,24,2048]{2,1,0:T(8,128)(2,1)}), bf16[16,24,2048]{2,1,0:T(8,128)(2,1)}, u32[]{:S(2)}, u32[]{:S(2)}) async-start(bf16[16,24,2048]{2,1,0:T(8,128)(2,1)} %bitcast.108), calls=%async_computation.3 | async-start | bytes 3145728 | tf_op jit(solution)/shard_map/all_to_all | solution.py:288
  766.2 50.9 %all-to-all-done.3 = bf16[16,24,2048]{2,1,0:T(8,128)(2,1)} async-done(((bf16[16,24,2048]{2,1,0:T(8,128)(2,1)}), bf16[16,24,2048]{2,1,0:T(8,128)(2,1)}, u32[]{:S(2)}, u32[]{:S(2)}) %all-to-all-start.3) | async-done | bytes 1572896 | tf_op jit(solution)/shard_map/all_to_all | solution.py:288
  830.2 22.6 %collective-permute-done.11 = bf16[384,2048]{1,0:T(8,128)(2,1)} collective-permute-done((bf16[384,2048]{1,0:T(8,128)(2,1)}, bf16[384,2048]{1,0:T(8,128)(2,1)}, u32[]{:S(2)}, u32[]{:S(2)}) %collective-permute-start.11) | collective-permute-done | bytes 1572896 | tf_op jit(solution)/shard_map/ppermute | solution.py:92
  863.5 79.4 %reduce-scatter.8.cloned.1.call-done = bf16[256,2048]{1,0:T(8,128)(2,1)} async-done(((bf16[2048,2048]{1,0:T(8,128)(2,1)}), bf16[256,2048]{1,0:T(8,128)(2,1)}) %reduce-scatter.8.cloned.1.call-update) | async-done | bytes 1048592 | tf_op jit(solution)/shard_map/reduce_scatter | solution.py:80
  949.0 143.9 %reduce-scatter.6.cloned.1.call-done = bf16[256,2048]{1,0:T(8,128)(2,1)} async-done(((bf16[2048,2048]{1,0:T(8,128)(2,1)}), bf16[256,2048]{1,0:T(8,128)(2,1)}) %reduce-scatter.6.cloned.1.call-update) | async-done | bytes 1048592 | tf_op jit(solution)/shard_map/reduce_scatter | solution.py:80
  (243 shorter events, 180.7 us)
Async XLA Ops:
  7.2 138.8 %all-gather.3.cloned.1.call-start = ((), (), s32[]{:S(2)}) async-start(), calls=%async_computation.7 | async-start | bytes 10584064 | tf_op jit(solution)/shard_map/all_gather | solution.py:139
  13.0 306.6 %all-gather.5.cloned.1.call-start = ((), (), s32[]{:S(2)}) async-start(), calls=%async_computation.8 | async-start | bytes 35651584 | tf_op jit(solution)/shard_map/all_gather | solution.py:153
  100.0 36.7 %collective-permute-start = (bf16[384,2048]{1,0:T(8,128)(2,1)}, bf16[384,2048]{1,0:T(8,128)(2,1)}, u32[]{:S(2)}, u32[]{:S(2)}) collective-permute-start(bf16[384,2048]{1,0:T(8,128)(2,1)} %bitcast.1), channel_id=1, source_target_pairs={{0,1},{1,0},{2,3},{3,2},{4,5},{5,4},{6,7},{7,6},{8,9},{9,8},{10,11... | collective-permute-start | bytes 4718600 | tf_op jit(solution)/shard_map/ppermute | solution.py:92
  104.6 98.3 %all-to-all-start.2 = ((bf16[16,24,2048]{2,1,0:T(8,128)(2,1)}), bf16[16,24,2048]{2,1,0:T(8,128)(2,1)}, u32[]{:S(2)}, u32[]{:S(2)}) async-start(bf16[16,24,2048]{2,1,0:T(8,128)(2,1)} %bitcast.109), calls=%async_computation.2 | async-start | bytes 3145728 | tf_op jit(solution)/shard_map/all_to_all | solution.py:170
  111.8 747.5 %reduce-scatter.4.cloned.1.call-start = ((), (), s32[]{:S(2)}) async-start(), calls=%async_computation.9 | async-start | bytes 5898240 | tf_op jit(solution)/shard_map/reduce_scatter | solution.py:80
  138.8 171.6 %copy-start.4 = (bf16[384,2048]{1,0:T(8,128)(2,1)}, bf16[384,2048]{1,0:T(8,128)(2,1)S(1)}, u32[]{:S(2)}) copy-start(bf16[384,2048]{1,0:T(8,128)(2,1)S(1)} %get-tuple-element.95) | copy-start | bytes 4718596
  200.7 109.7 %collective-permute-start.1 = (bf16[768,2048]{1,0:T(8,128)(2,1)}, bf16[768,2048]{1,0:T(8,128)(2,1)}, u32[]{:S(2)}, u32[]{:S(2)}) collective-permute-start(bf16[768,2048]{1,0:T(8,128)(2,1)} %fusion.57), channel_id=1, source_target_pairs={{0,1},{1,0},{2,3},{3,2},{4,5},{5,4},{6,7},{7,6},{8,9},{9,8},{10,11... | collective-permute-start | bytes 9437192 | tf_op jit(solution)/shard_map/ppermute | solution.py:92
  202.9 102.7 %collective-permute-start.4 = (bf16[384,2048]{1,0:T(8,128)(2,1)}, bf16[384,2048]{1,0:T(8,128)(2,1)}, u32[]{:S(2)}, u32[]{:S(2)}) collective-permute-start(bf16[384,2048]{1,0:T(8,128)(2,1)} %bitcast.19), channel_id=1, source_target_pairs={{0,1},{1,0},{2,3},{3,2},{4,5},{5,4},{6,7},{7,6},{8,9},{9,8},{10,11... | collective-permute-start | bytes 4718600 | tf_op jit(solution)/shard_map/ppermute | solution.py:92
  310.4 36.8 %collective-permute-start.5 = (bf16[768,2048]{1,0:T(8,128)(2,1)}, bf16[768,2048]{1,0:T(8,128)(2,1)}, u32[]{:S(2)}, u32[]{:S(2)}) collective-permute-start(bf16[768,2048]{1,0:T(8,128)(2,1)} %pad_maximum_fusion.3), channel_id=1, source_target_pairs={{0,2},{2,0},{4,6},{6,4},{8,10},{10,8},{12,14},{14,12},{16,18},{18,... | collective-permute-start | bytes 9437192 | tf_op jit(solution)/shard_map/ppermute | solution.py:55
  346.6 5.9 collective-permute-start.6
  347.1 79.4 %collective-permute-start.8 = (bf16[768,2048]{1,0:T(8,128)(2,1)}, bf16[768,2048]{1,0:T(8,128)(2,1)}, u32[]{:S(2)}, u32[]{:S(2)}) collective-permute-start(bf16[768,2048]{1,0:T(8,128)(2,1)} %add_convert_fusion), channel_id=1, source_target_pairs={{0,2},{2,0},{4,6},{6,4},{8,10},{10,8},{12,14},{14,12},{16,18},{18,... | collective-permute-start | bytes 9437192 | tf_op jit(solution)/shard_map/ppermute | solution.py:55
  404.5 22.1 %collective-permute-start.9 = (bf16[768,2048]{1,0:T(8,128)(2,1)}, bf16[768,2048]{1,0:T(8,128)(2,1)}, u32[]{:S(2)}, u32[]{:S(2)}) collective-permute-start(bf16[768,2048]{1,0:T(8,128)(2,1)} %get-tuple-element.90), channel_id=1, source_target_pairs={{0,2},{2,0},{4,6},{6,4},{8,10},{10,8},{12,14},{14,12},{16,18},{18,... | collective-permute-start | bytes 9437192 | tf_op jit(solution)/shard_map/ppermute | solution.py:55
  424.8 70.4 %collective-permute-start.7 = (bf16[768,2048]{1,0:T(8,128)(2,1)}, bf16[768,2048]{1,0:T(8,128)(2,1)}, u32[]{:S(2)}, u32[]{:S(2)}) collective-permute-start(bf16[768,2048]{1,0:T(8,128)(2,1)} %fusion.66), channel_id=1, source_target_pairs={{0,1},{1,0},{2,3},{3,2},{4,5},{5,4},{6,7},{7,6},{8,9},{9,8},{10,11... | collective-permute-start | bytes 9437192 | tf_op jit(solution)/shard_map/ppermute | solution.py:92
  426.5 191.4 %collective-permute-start.12 = (bf16[768,2048]{1,0:T(8,128)(2,1)}, bf16[768,2048]{1,0:T(8,128)(2,1)}, u32[]{:S(2)}, u32[]{:S(2)}) collective-permute-start(bf16[768,2048]{1,0:T(8,128)(2,1)} %copy-done.18), channel_id=1, source_target_pairs={{0,2},{2,0},{4,6},{6,4},{8,10},{10,8},{12,14},{14,12},{16,18},{18,... | collective-permute-start | bytes 9437192 | tf_op jit(solution)/shard_map/ppermute | solution.py:55
  566.1 46.4 %collective-permute-start.10 = (bf16[384,2048]{1,0:T(8,128)(2,1)S(1)}, bf16[384,2048]{1,0:T(8,128)(2,1)S(1)}, u32[]{:S(2)}, u32[]{:S(2)}) collective-permute-start(bf16[384,2048]{1,0:T(8,128)(2,1)S(1)} %constant_dynamic-slice_fusion.7), channel_id=1, source_target_pairs={{0,1},{1,0},{2,3},{3,2},{4,5},{5,4},{6,7},{7,6},{8,9},{9,8},{10,11... | collective-permute-start | bytes 4718600 | tf_op jit(solution)/shard_map/ppermute | solution.py:92
  570.1 40.1 %collective-permute-start.13 = (bf16[768,256]{0,1:T(8,128)(2,1)S(1)}, bf16[768,256]{0,1:T(8,128)(2,1)S(1)}, u32[]{:S(2)}, u32[]{:S(2)}) collective-permute-start(bf16[768,256]{0,1:T(8,128)(2,1)S(1)} %pad_maximum_fusion.6), channel_id=1, source_target_pairs={{0,1},{1,0},{2,3},{3,2},{4,5},{5,4},{6,7},{7,6},{8,9},{9,8},{10,11... | collective-permute-start | bytes 1179656 | tf_op jit(solution)/shard_map/ppermute | solution.py:92
  574.0 50.3 %collective-permute-start.15 = (bf16[768,2048]{1,0:T(8,128)(2,1)S(1)}, bf16[768,2048]{1,0:T(8,128)(2,1)S(1)}, u32[]{:S(2)}, u32[]{:S(2)}) collective-permute-start(bf16[768,2048]{1,0:T(8,128)(2,1)S(1)} %copy-done.17), channel_id=1, source_target_pairs={{0,2},{2,0},{4,6},{6,4},{8,10},{10,8},{12,14},{14,12},{16,18},{18,... | collective-permute-start | bytes 9437192 | tf_op jit(solution)/shard_map/ppermute | solution.py:55
  612.4 5.5 collective-permute-start.14
  613.9 3.8 collective-permute-start.17
  615.9 8.4 collective-permute-start.16
  617.8 6.3 collective-permute-start.18
  637.2 305.7 %reduce-scatter.8.cloned.1.call-start = ((), (), s32[]{:S(2)}) async-start(), calls=%async_computation.11 | async-start | bytes 9437184 | tf_op jit(solution)/shard_map/reduce_scatter | solution.py:80
  637.8 455.2 %reduce-scatter.6.cloned.1.call-start = ((), (), s32[]{:S(2)}) async-start(), calls=%async_computation.10 | async-start | bytes 9437184 | tf_op jit(solution)/shard_map/reduce_scatter | solution.py:80
  657.1 36.9 %collective-permute-start.2 = (bf16[384,2048]{1,0:T(8,128)(2,1)S(1)}, bf16[384,2048]{1,0:T(8,128)(2,1)S(1)}, u32[]{:S(2)}, u32[]{:S(2)}) collective-permute-start(bf16[384,2048]{1,0:T(8,128)(2,1)S(1)} %constant_dynamic-slice_fusion.12), channel_id=1, source_target_pairs={{0,1},{1,0},{2,3},{3,2},{4,5},{5,4},{6,7},{7,6},{8,9},{9,8},{10,11... | collective-permute-start | bytes 4718600 | tf_op jit(solution)/shard_map/ppermute | solution.py:92
  697.7 49.3 %all-to-all-start.1 = ((bf16[16,24,2048]{2,1,0:T(8,128)(2,1)}), bf16[16,24,2048]{2,1,0:T(8,128)(2,1)}, u32[]{:S(2)}, u32[]{:S(2)}) async-start(bf16[16,24,2048]{2,1,0:T(8,128)(2,1)} %bitcast.15), calls=%async_computation.1 | async-start | bytes 3145728 | tf_op jit(solution)/shard_map/all_to_all | solution.py:288
  747.0 70.1 %all-to-all-start.3 = ((bf16[16,24,2048]{2,1,0:T(8,128)(2,1)}), bf16[16,24,2048]{2,1,0:T(8,128)(2,1)}, u32[]{:S(2)}, u32[]{:S(2)}) async-start(bf16[16,24,2048]{2,1,0:T(8,128)(2,1)} %bitcast.108), calls=%async_computation.3 | async-start | bytes 3145728 | tf_op jit(solution)/shard_map/all_to_all | solution.py:288
  764.4 59.2 %collective-permute-start.3 = (bf16[384,2048]{1,0:T(8,128)(2,1)}, bf16[384,2048]{1,0:T(8,128)(2,1)}, u32[]{:S(2)}, u32[]{:S(2)}) collective-permute-start(bf16[384,2048]{1,0:T(8,128)(2,1)} %bitcast.16), channel_id=1, source_target_pairs={{0,1},{1,0},{2,3},{3,2},{4,5},{5,4},{6,7},{7,6},{8,9},{9,8},{10,11... | collective-permute-start | bytes 4718600 | tf_op jit(solution)/shard_map/ppermute | solution.py:92
  817.1 35.6 %collective-permute-start.11 = (bf16[384,2048]{1,0:T(8,128)(2,1)}, bf16[384,2048]{1,0:T(8,128)(2,1)}, u32[]{:S(2)}, u32[]{:S(2)}) collective-permute-start(bf16[384,2048]{1,0:T(8,128)(2,1)} %bitcast.28), channel_id=1, source_target_pairs={{0,1},{1,0},{2,3},{3,2},{4,5},{5,4},{6,7},{7,6},{8,9},{9,8},{10,11... | collective-permute-start | bytes 4718600 | tf_op jit(solution)/shard_map/ppermute | solution.py:92
  860.4 86.7 %collective-permute-start.19 = (bf16[128,640]{0,1:T(8,128)(2,1)S(1)}, bf16[128,640]{0,1:T(8,128)(2,1)S(1)}, u32[]{:S(2)}, u32[]{:S(2)}) collective-permute-start(bf16[128,640]{0,1:T(8,128)(2,1)S(1)} %constant_dynamic-slice_fusion.4), channel_id=1, source_target_pairs={{0,2},{2,0},{4,6},{6,4},{8,10},{10,8},{12,14},{14,12},{16,18},{18,... | collective-permute-start | bytes 491528 | tf_op jit(solution)/shard_map/ppermute | solution.py:55
  863.4 82.5 %collective-permute-start.20 = (bf16[128,512]{0,1:T(8,128)(2,1)S(1)}, bf16[128,512]{0,1:T(8,128)(2,1)S(1)}, u32[]{:S(2)}, u32[]{:S(2)}) collective-permute-start(bf16[128,512]{0,1:T(8,128)(2,1)S(1)} %constant_dynamic-slice_fusion.3), channel_id=1, source_target_pairs={{0,2},{2,0},{4,6},{6,4},{8,10},{10,8},{12,14},{14,12},{16,18},{18,... | collective-permute-start | bytes 393224 | tf_op jit(solution)/shard_map/ppermute | solution.py:55
  944.8 149.5 %collective-permute-start.22 = (bf16[128,2048]{1,0:T(8,128)(2,1)}, bf16[128,2048]{1,0:T(8,128)(2,1)}, u32[]{:S(2)}, u32[]{:S(2)}) collective-permute-start(bf16[128,2048]{1,0:T(8,128)(2,1)} %constant_dynamic-slice_fusion.1), channel_id=1, source_target_pairs={{0,2},{2,0},{4,6},{6,4},{8,10},{10,8},{12,14},{14,12},{16,18},{18,... | collective-permute-start | bytes 1572872 | tf_op jit(solution)/shard_map/ppermute | solution.py:55
  1094.1 2.9 collective-permute-start.21
  (35 other events, 778.1 us)
Sparse Core Ops, SparseCore 0:
  13.1 132.8 all-gather.2
  148.2 168.1 all-gather.4
  637.3 122.3 reduce-scatter.3
  763.2 179.6 reduce-scatter.7
  946.4 146.5 reduce-scatter.5

commit v3 on v2

--- a/solution.py
+++ b/solution.py
@@ -76,8 +76,21 @@
 
 def summed_rows(low):
     members = lax.axis_size("dp")
-    groups = [list(range(core, members, 2)) for core in range(2)]
-    return lax.psum_scatter(low, "dp", scatter_dimension=0, axis_index_groups=groups, tiled=True)
+    side = lax.rem(lax.axis_index("dp") // 2, 2)
+    rows, cols = low.shape
+    blocks = low.reshape(members // 4, 2, rows * 2 // members, cols)
+    kept = lax.dynamic_index_in_dim(blocks, side, axis=1, keepdims=False)
+    leaving = lax.dynamic_index_in_dim(blocks, 1 - side, axis=1, keepdims=False)
+    other = lax.ppermute(leaving, "dp", [(i, i ^ 2) for i in range(members)])
+    near = (kept.astype(jnp.float32) + other.astype(jnp.float32)).astype(jnp.bfloat16)
+    groups = [list(range(first, members, 4)) for first in range(4)]
+    return lax.psum_scatter(
+        near.reshape(rows // 2, cols),
+        "dp",
+        scatter_dimension=0,
+        axis_index_groups=groups,
+        tiled=True,
+    )
 
 
 def own_columns(chip_rows, core):
@@ -219,6 +232,7 @@
     grad_up = gelu_back(grad_active)[0].astype(jnp.bfloat16)
     norm_two_part = right_product(grad_up, full_up)
     wup_term = weight_term(both_normed_two, half_of_both(grad_up, core))
+    mlp_part = right_product(active, full_down)
     grad_norm_two, wup_term = tensor_sum(norm_two_part, wup_term)
     wup_rows = summed_rows(wup_term)
     norm_two_back = jax.vjp(layer_norm, resid_mid, second_gain, second_shift)[1]
@@ -251,14 +265,18 @@
     grad_keyval_part = jnp.concatenate([grad_keys, grad_values], axis=1)
     grad_keyval_low = tensor_sum(grad_keyval_part).astype(jnp.bfloat16)
     grad_qkv_part = jnp.concatenate([grad_query, grad_keyval_part.astype(jnp.bfloat16)], axis=1)
-    grad_norm_one = tensor_rows(right_product(grad_qkv_part, full_qkv), place)
+    mlp_output = tensor_rows(mlp_part, place)
+    result = (own_rows(resid_mid, place, 2) + mlp_output).astype(jnp.bfloat16)
+    result, grad_qkv_part = lax.optimization_barrier((result, grad_qkv_part))
+    output_rows = lax.all_to_all(result, "dp", split_axis=0, concat_axis=0, tiled=True)
+    norm_one_part = right_product(grad_qkv_part, full_qkv)
+    grad_norm_one = tensor_rows(norm_one_part, place)
+    output_rows, grad_norm_one = lax.optimization_barrier((output_rows, grad_norm_one))
     norm_one_back = jax.vjp(
         layer_norm, own_rows(resid_in, place, 2), first_gain, first_shift
     )[1]
     grad_in_norm, grad_gain_one, grad_shift_one = norm_one_back(grad_norm_one)
     grad_resid = (own_rows(grad_mid, place, 2) + grad_in_norm).astype(jnp.bfloat16)
-    mlp_output = tensor_rows(right_product(active, full_down), place)
-    result = (own_rows(resid_mid, place, 2) + mlp_output).astype(jnp.bfloat16)
     norm_one_sums = jnp.stack([grad_gain_one, grad_shift_one])
     norm_one_sums = norm_one_sums + swap_tensor(norm_one_sums)
     norm_sums = jnp.concatenate([norm_one_sums, jnp.stack([grad_gain_two, grad_shift_two])])
@@ -284,12 +302,13 @@
     restore = jnp.argsort(send_order.reshape(-1), stable=True)
     restore = lax.rem(restore + place * (row_count // 2), row_count)
 
-    def returned(rows):
-        mine = lax.all_to_all(rows, "dp", split_axis=0, concat_axis=0, tiled=True)
+    def returned(mine):
         return jnp.concatenate([mine, swap_tensor(mine)], axis=0)[restore]
 
-    output = returned(result)
-    grad_tokens = returned(grad_resid)
+    output = returned(output_rows)
+    grad_tokens = returned(
+        lax.all_to_all(grad_resid, "dp", split_axis=0, concat_axis=0, tiled=True)
+    )
     return (
         output,
         grad_tokens,

time: 1110 us -> 1040 us (0.937)
  the two profiles are of different devices: /device:TPU:0 before, /device:TPU:15 now
where the time goes in v3:
time: 1040 us; the launch traced here: 1030 us
  waiting for transfers between devices  430 us (41%)
  matrix products  220 us (21%)
  other arithmetic  152 us (15%)
  local copies, waits for them, and re-layouts  100 us (10%)
  blocking collectives  77.2 us (7%)
  starting transfers between devices  38.9 us (4%)
  between operations  15 us (1%)
    ppermute x10, waiting for transfers between devices, swap_tensor(): return lax.ppermute(values, 'tensor', [(0, 1), (1, 0)])  213 us
    ppermute x3, waiting for transfers between devices, summed_rows(): other = lax.ppermute(leaving, 'dp', [(i, i ^ 2) for i in range(members)])  138 us
    all_to_all x1, waiting for transfers between devices, per_device(): lax.all_to_all(grad_resid, 'dp', split_axis=0, concat_axis=0, tiled=True)  78.8 us
    all_to_all x1, blocking collectives, fetched(): lax.all_to_all(rows[own_sends], 'dp', split_axis=0, concat_axis=0, tiled=...  77.2 us
    dot_general x4, matrix products, right_product(): lax.dot_general(first_op, second_op, (((1,), (1,)), ((), ())), preferred_...  55.2 us
    dot_general x4, matrix products, left_product(): lax.dot_general(first_op, second_op, (((0,), (0,)), ((), ())), preferred_...  52 us
    dot_general x1, matrix products, per_device(): jnp.dot(grad_here, full_down, preferred_element_type=jnp.float32)  27.9 us
    unnamed x87, local copies, waits for them, and re-layouts  24.9 us
  transfers between devices with their start and end apart: 34, of which 8 were waited for; matrix products, arithmetic and copies ran while one was open for 45% of the time, Pallas kernels for 0%

profile of v3, /device:TPU:15, one launch (start us, length us, event | category | flops | bytes accessed | tf_op | source)
XLA Modules:
  0.0 1033.5 jit_solution(6075855465681716039)
XLA Ops:
  24.7 77.2 %all_to_all.48 = bf16[16,24,2048]{2,1,0:T(8,128)(2,1)} all-to-all(bf16[16,24,2048]{2,1,0:T(8,128)(2,1)} %bitcast.134), channel_id=1, replica_groups=mesh['dp'=16,'tensor'=2] {'dp'}, dimensions={0} | all-to-all | bytes 3145728 | tf_op jit(solution)/shard_map/all_to_all | solution.py:183
  110.6 8.2 sort.63
  125.1 12.8 %collective-permute-done = bf16[384,2048]{1,0:T(8,128)(2,1)} collective-permute-done((bf16[384,2048]{1,0:T(8,128)(2,1)}, bf16[384,2048]{1,0:T(8,128)(2,1)}, u32[]{:S(2)}, u32[]{:S(2)}) %collective-permute-start) | collective-permute-done | bytes 1572896 | tf_op jit(solution)/shard_map/ppermute | solution.py:105
  160.1 11.7 %fusion.126 = (f32[8,768]{1,0:T(8,128)S(1)}, f32[8,768,768]{1,2,0:T(8,128)}) fusion(bf16[768,8,128]{0,2,1:T(8,128)(2,1)} %bitcast.126, bf16[768,1280]{1,0:T(8,128)(2,1)} %copy-done.16, pred[768,768]{0,1:T(8,128)(4,1)} %compare_and_fusion), kind=kOutput, calls=%fused_computation.236 | convolution fusion | flops 1222109184 | bytes 21258240 | tf_op jit(solution)/shard_map/qhd,kd->hqk/dot_general | solution.py:120
  171.8 9.2 fusion.3
  181.0 10.6 %fusion.87 = bf16[128,8,768]{2,0,1:T(8,128)(2,1)S(1)} fusion(f32[8,768,768]{1,2,0:T(8,128)} %get-tuple-element.84, f32[8,768]{1,0:T(8,128)S(1)} %fusion.3, f32[8,768]{1,0:T(8,128)S(1)} %get-tuple-element.83, bf16[768,1280]{1,0:T(8,128)(2,1)} %copy-done.16), kind=kOutput, calls=%fused_computation.121 | convolution fusion | flops 1222901760 | bytes 20692992 | tf_op jit(solution)/shard_map/hqk,kd->qhd/dot_general | solution.py:217
  191.6 7.8 fusion.60
  200.9 101.0 %collective-permute-done.3 = bf16[384,2048]{1,0:T(8,128)(2,1)} collective-permute-done((bf16[384,2048]{1,0:T(8,128)(2,1)}, bf16[384,2048]{1,0:T(8,128)(2,1)}, u32[]{:S(2)}, u32[]{:S(2)}) %collective-permute-start.3) | collective-permute-done | bytes 1572896 | tf_op jit(solution)/shard_map/ppermute | solution.py:105
  316.9 23.2 %multiply_convert_fusion = (bf16[768,4096]{1,0:T(8,128)(2,1)}, f32[768,4096]{1,0:T(8,128)}) fusion(bf16[768,2048]{1,0:T(8,128)(2,1)} %add_convert_fusion, bf16[2048,8192]{1,0:T(8,128)(2,1)} %all-gather.5.cloned.1.call-done), kind=kOutput, calls=%fused_computation.32 | convolution fusion | flops 12913213440 | bytes 38797312 | tf_op jit(solution)/shard_map/dot_general | solution.py:224
  345.9 20.2 %fusion.72 = bf16[768,2048]{1,0:T(8,128)(2,1)} fusion(bf16[768,4096]{1,0:T(8,128)(2,1)} %get-tuple-element.85, bf16[2048,8192]{1,0:T(8,128)(2,1)} %all-gather.5.cloned.1.call-done), kind=kOutput, calls=%fused_computation.94 | convolution fusion | flops 12886474752 | bytes 26214400 | tf_op jit(solution)/shard_map/dot_general | solution.py:27
  369.2 18.0 %convolution_convert_fusion.1 = bf16[2048,2048]{1,0:T(8,128)(2,1)} fusion(bf16[768,2048]{1,0:T(8,128)(2,1)} %collective-permute-done.4, bf16[384,2048]{1,0:T(8,128)(2,1)S(1)} %copy-done.12, bf16[384,2048]{1,0:T(8,128)(2,1)S(1)} %copy-done.10, bf16[768,2048]{1,0:T(8,128)(2,1)} %collective-permute-done.5, bf16[768,2048]{1,0:T(8,128)(2,1)S(1)} %get-tuple-element.59), kind=kOutput, calls=%fused_computation.42 | convolution fusion | flops 12920553472 | bytes 20971520 | tf_op jit(solution)/shard_map/dot_general | solution.py:33
  387.2 27.9 %fusion.19 = bf16[768,4096]{1,0:T(8,128)(2,1)} fusion(f32[768,4096]{1,0:T(8,128)} %get-tuple-element.86, bf16[768,2048]{1,0:T(8,128)(2,1)} %pad_maximum_fusion.2, bf16[2048,8192]{1,0:T(8,128)(2,1)} %all-gather.5.cloned.1.call-done), kind=kOutput, calls=%fused_computation.31 | convolution fusion | flops 12947816448 | bytes 38797312 | tf_op jit(solution)/shard_map/dot_general | solution.py:230
  420.5 19.8 %fusion.69 = bf16[768,2048]{1,0:T(8,128)(2,1)} fusion(bf16[768,4096]{1,0:T(8,128)(2,1)} %fusion.19, bf16[2048,8192]{1,0:T(8,128)(2,1)} %all-gather.5.cloned.1.call-done), kind=kOutput, calls=%fused_computation.93 | convolution fusion | flops 12886474752 | bytes 26214400 | tf_op jit(solution)/shard_map/dot_general | solution.py:27
  451.1 19.7 %convolution_convert_fusion = bf16[2048,2048]{1,0:T(8,128)(2,1)} fusion(bf16[768,2048]{1,0:T(8,128)(2,1)} %collective-permute-done.7, bf16[768,2048]{1,0:T(8,128)(2,1)} %add_convert_fusion, bf16[768,2048]{1,0:T(8,128)(2,1)} %collective-permute-done.8, bf16[768,2048]{1,0:T(8,128)(2,1)} %get-tuple-element.57), kind=kOutput, calls=%fused_computation.41 | convolution fusion | flops 12914262016 | bytes 20971520 | tf_op jit(solution)/shard_map/dot_general | solution.py:33
  470.8 39.1 %collective-permute-done.6 = bf16[768,2048]{1,0:T(8,128)(2,1)} collective-permute-done((bf16[768,2048]{1,0:T(8,128)(2,1)}, bf16[768,2048]{1,0:T(8,128)(2,1)}, u32[]{:S(2)}, u32[]{:S(2)}) %collective-permute-start.6) | collective-permute-done | bytes 3145760 | tf_op jit(solution)/shard_map/ppermute | solution.py:105
  532.9 9.6 fusion.96
  542.6 12.0 %fusion = (f32[8,768]{1,0:T(8,128)S(1)}, f32[768,768,8]{1,0,2:T(8,128)}) fusion(f32[8,768,768]{1,2,0:T(8,128)} %get-tuple-element.84, f32[8,768]{1,0:T(8,128)S(1)} %copy-done.22, bf16[768,8,128]{0,2,1:T(8,128)(2,1)S(1)} %bitcast.125, bf16[768,1280]{1,0:T(8,128)(2,1)} %copy-done.16), kind=kOutput, calls=%fused_computation.6 | convolution fusion | flops 1222109184 | bytes 39567360 | tf_op jit(solution)/shard_map/qhd,kd->hqk/dot_general | solution.py:248
  554.6 12.9 %fusion.2 = bf16[8,768,768]{1,2,0:T(8,128)(2,1)S(1)} fusion(f32[768,768,8]{1,0,2:T(8,128)} %get-tuple-element.88, f32[8,768,768]{1,2,0:T(8,128)} %get-tuple-element.84, f32[8,768]{1,0:T(8,128)S(1)} %get-tuple-element.87, f32[8,768]{1,0:T(8,128)S(1)} %copy-done.22), kind=kLoop, calls=%fused_computation.8 | loop fusion | flops 18874368 | bytes 47235072 | tf_op jit(solution)/shard_map/convert_element_type | solution.py:252
  574.6 9.3 all-to-all-start.2
  584.4 7.4 fusion.66
  598.8 37.2 %collective-permute-done.13 = bf16[768,256]{0,1:T(8,128)(2,1)S(1)} collective-permute-done((bf16[768,256]{0,1:T(8,128)(2,1)S(1)}, bf16[768,256]{0,1:T(8,128)(2,1)S(1)}, u32[]{:S(2)}, u32[]{:S(2)}) %collective-permute-start.13) | collective-permute-done | bytes 393248 | tf_op jit(solution)/shard_map/ppermute | solution.py:105
  645.8 7.7 fusion.24
  654.7 7.7 fusion.75
  669.2 9.3 pad_maximum_fusion
  678.5 9.5 reshape.339
  688.0 13.5 %constant_dynamic-slice_fusion.5 = (bf16[4,1,256,1280]{2,1,0,3:T(2,128)(2,1)}, bf16[4,1,256,1280]{2,1,0,3:T(2,128)(2,1)}) fusion(bf16[4,2,256,1280]{2,1,0,3:T(2,128)(2,1)} %reshape.339, s32[]{:T(128)S(6)} %select_n.181, s32[]{:T(128)S(6)} %select_n.182), kind=kLoop, calls=%fused_computation.187 | loop fusion | bytes 10485768 | tf_op jit(solution)/shard_map/jit(dynamic_index_in_dim)/dynamic_slice | solution.py:82
  701.4 11.1 %copy.88 = bf16[4,1,256,1280]{3,2,0,1:T(8,128)(2,1)} copy(bf16[4,1,256,1280]{2,1,0,3:T(2,128)(2,1)} %get-tuple-element.62) | data formatting | bytes 5242880
  712.8 11.1 %copy.87 = bf16[4,1,256,1280]{3,2,0,1:T(8,128)(2,1)} copy(bf16[4,1,256,1280]{2,1,0,3:T(2,128)(2,1)} %get-tuple-element.61) | data formatting | bytes 5242880
  723.9 47.4 %collective-permute-done.19 = bf16[4,256,1280]{2,1,0:T(8,128)(2,1)} collective-permute-done((bf16[4,256,1280]{2,1,0:T(8,128)(2,1)}, bf16[4,256,1280]{2,1,0:T(8,128)(2,1)}, u32[]{:S(2)}, u32[]{:S(2)}) %collective-permute-start.19) | collective-permute-done | bytes 2621472 | tf_op jit(solution)/shard_map/ppermute | solution.py:84
  779.0 91.0 %collective-permute-done.22 = bf16[4,256,2048]{2,1,0:T(8,128)(2,1)S(1)} collective-permute-done((bf16[4,256,2048]{2,1,0:T(8,128)(2,1)S(1)}, bf16[4,256,2048]{2,1,0:T(8,128)(2,1)S(1)}, u32[]{:S(2)}, u32[]{:S(2)}) %collective-permute-start.22) | collective-permute-done | bytes 4194336 | tf_op jit(solution)/shard_map/ppermute | solution.py:84
  889.8 78.8 %all-to-all-done.3 = bf16[16,24,2048]{2,1,0:T(8,128)(2,1)} async-done(((bf16[16,24,2048]{2,1,0:T(8,128)(2,1)}), bf16[16,24,2048]{2,1,0:T(8,128)(2,1)}, u32[]{:S(2)}, u32[]{:S(2)}) %all-to-all-start.3) | async-done | bytes 1572896 | tf_op jit(solution)/shard_map/all_to_all | solution.py:310
  982.0 22.8 %collective-permute-done.11 = bf16[384,2048]{1,0:T(8,128)(2,1)} collective-permute-done((bf16[384,2048]{1,0:T(8,128)(2,1)}, bf16[384,2048]{1,0:T(8,128)(2,1)}, u32[]{:S(2)}, u32[]{:S(2)}) %collective-permute-start.11) | collective-permute-done | bytes 1572896 | tf_op jit(solution)/shard_map/ppermute | solution.py:105
  (269 shorter events, 214.0 us)
Async XLA Ops:
  7.2 134.2 %all-gather.3.cloned.1.call-start = ((), (), s32[]{:S(2)}) async-start(), calls=%async_computation.7 | async-start | bytes 10584064 | tf_op jit(solution)/shard_map/all_gather | solution.py:152
  13.0 304.0 %all-gather.5.cloned.1.call-start = ((), (), s32[]{:S(2)}) async-start(), calls=%async_computation.8 | async-start | bytes 35651584 | tf_op jit(solution)/shard_map/all_gather | solution.py:166
  101.9 35.9 %collective-permute-start = (bf16[384,2048]{1,0:T(8,128)(2,1)}, bf16[384,2048]{1,0:T(8,128)(2,1)}, u32[]{:S(2)}, u32[]{:S(2)}) collective-permute-start(bf16[384,2048]{1,0:T(8,128)(2,1)} %bitcast.1), channel_id=1, source_target_pairs={{0,1},{1,0},{2,3},{3,2},{4,5},{5,4},{6,7},{7,6},{8,9},{9,8},{10,11... | collective-permute-start | bytes 4718600 | tf_op jit(solution)/shard_map/ppermute | solution.py:105
  105.4 94.4 %all-to-all-start.1 = ((bf16[16,24,2048]{2,1,0:T(8,128)(2,1)}), bf16[16,24,2048]{2,1,0:T(8,128)(2,1)}, u32[]{:S(2)}, u32[]{:S(2)}) async-start(bf16[16,24,2048]{2,1,0:T(8,128)(2,1)} %bitcast.133), calls=%async_computation.1 | async-start | bytes 3145728 | tf_op jit(solution)/shard_map/all_to_all | solution.py:183
  199.4 109.5 %collective-permute-start.1 = (bf16[768,2048]{1,0:T(8,128)(2,1)}, bf16[768,2048]{1,0:T(8,128)(2,1)}, u32[]{:S(2)}, u32[]{:S(2)}) collective-permute-start(bf16[768,2048]{1,0:T(8,128)(2,1)} %fusion.60), channel_id=1, source_target_pairs={{0,1},{1,0},{2,3},{3,2},{4,5},{5,4},{6,7},{7,6},{8,9},{9,8},{10,11... | collective-permute-start | bytes 9437192 | tf_op jit(solution)/shard_map/ppermute | solution.py:105
  199.7 102.1 %collective-permute-start.3 = (bf16[384,2048]{1,0:T(8,128)(2,1)}, bf16[384,2048]{1,0:T(8,128)(2,1)}, u32[]{:S(2)}, u32[]{:S(2)}) collective-permute-start(bf16[384,2048]{1,0:T(8,128)(2,1)} %bitcast.18), channel_id=1, source_target_pairs={{0,1},{1,0},{2,3},{3,2},{4,5},{5,4},{6,7},{7,6},{8,9},{9,8},{10,11... | collective-permute-start | bytes 4718600 | tf_op jit(solution)/shard_map/ppermute | solution.py:105
  306.3 62.9 %collective-permute-start.4 = (bf16[768,2048]{1,0:T(8,128)(2,1)}, bf16[768,2048]{1,0:T(8,128)(2,1)}, u32[]{:S(2)}, u32[]{:S(2)}) collective-permute-start(bf16[768,2048]{1,0:T(8,128)(2,1)} %pad_maximum_fusion.2), channel_id=1, source_target_pairs={{0,2},{2,0},{4,6},{6,4},{8,10},{10,8},{12,14},{14,12},{16,18},{18,... | collective-permute-start | bytes 9437192 | tf_op jit(solution)/shard_map/ppermute | solution.py:55
  316.8 134.3 %collective-permute-start.7 = (bf16[768,2048]{1,0:T(8,128)(2,1)}, bf16[768,2048]{1,0:T(8,128)(2,1)}, u32[]{:S(2)}, u32[]{:S(2)}) collective-permute-start(bf16[768,2048]{1,0:T(8,128)(2,1)} %add_convert_fusion), channel_id=1, source_target_pairs={{0,2},{2,0},{4,6},{6,4},{8,10},{10,8},{12,14},{14,12},{16,18},{18,... | collective-permute-start | bytes 9437192 | tf_op jit(solution)/shard_map/ppermute | solution.py:55
  345.4 23.7 %collective-permute-start.5 = (bf16[768,2048]{1,0:T(8,128)(2,1)}, bf16[768,2048]{1,0:T(8,128)(2,1)}, u32[]{:S(2)}, u32[]{:S(2)}) collective-permute-start(bf16[768,2048]{1,0:T(8,128)(2,1)} %get-tuple-element.60), channel_id=1, source_target_pairs={{0,2},{2,0},{4,6},{6,4},{8,10},{10,8},{12,14},{14,12},{16,18},{18,... | collective-permute-start | bytes 9437192 | tf_op jit(solution)/shard_map/ppermute | solution.py:55
  368.8 72.6 %collective-permute-start.2 = (bf16[384,2048]{1,0:T(8,128)(2,1)}, bf16[384,2048]{1,0:T(8,128)(2,1)}, u32[]{:S(2)}, u32[]{:S(2)}) collective-permute-start(bf16[384,2048]{1,0:T(8,128)(2,1)} %constant_dynamic-slice_fusion.13), channel_id=1, source_target_pairs={{0,1},{1,0},{2,3},{3,2},{4,5},{5,4},{6,7},{7,6},{8,9},{9,8},{10,11... | collective-permute-start | bytes 4718600 | tf_op jit(solution)/shard_map/ppermute | solution.py:105
  420.4 30.7 %collective-permute-start.8 = (bf16[768,2048]{1,0:T(8,128)(2,1)S(1)}, bf16[768,2048]{1,0:T(8,128)(2,1)}, u32[]{:S(2)}, u32[]{:S(2)}) collective-permute-start(bf16[768,2048]{1,0:T(8,128)(2,1)S(1)} %get-tuple-element.58), channel_id=1, source_target_pairs={{0,2},{2,0},{4,6},{6,4},{8,10},{10,8},{12,14},{14,12},{16,18},{18,... | collective-permute-start | bytes 9437192 | tf_op jit(solution)/shard_map/ppermute | solution.py:55
  440.3 69.6 %collective-permute-start.6 = (bf16[768,2048]{1,0:T(8,128)(2,1)}, bf16[768,2048]{1,0:T(8,128)(2,1)}, u32[]{:S(2)}, u32[]{:S(2)}) collective-permute-start(bf16[768,2048]{1,0:T(8,128)(2,1)} %fusion.69), channel_id=1, source_target_pairs={{0,1},{1,0},{2,3},{3,2},{4,5},{5,4},{6,7},{7,6},{8,9},{9,8},{10,11... | collective-permute-start | bytes 9437192 | tf_op jit(solution)/shard_map/ppermute | solution.py:105
  451.1 193.3 %collective-permute-start.24 = (bf16[4,256,2048]{2,1,0:T(8,128)(2,1)}, bf16[4,256,2048]{2,1,0:T(8,128)(2,1)}, u32[]{:S(2)}, u32[]{:S(2)}) collective-permute-start(bf16[4,256,2048]{2,1,0:T(8,128)(2,1)} %dynamic-slice_bitcast_fusion), channel_id=1, source_target_pairs={{0,4},{2,6},{4,0},{6,2},{8,12},{10,14},{12,8},{14,10},{16,20},{18,... | collective-permute-start | bytes 12582920 | tf_op jit(solution)/shard_map/ppermute | solution.py:84
  574.6 66.7 %all-to-all-start.2 = ((bf16[16,24,2048]{2,1,0:T(8,128)(2,1)}), bf16[16,24,2048]{2,1,0:T(8,128)(2,1)}, u32[]{:S(2)}, u32[]{:S(2)}) async-start(bf16[16,24,2048]{2,1,0:T(8,128)(2,1)} %bitcast.24), calls=%async_computation.2 | async-start | bytes 3145728 | tf_op jit(solution)/shard_map/all_to_all | solution.py:271
  583.9 389.4 %reduce-scatter.8.cloned.1.call-start = ((), (), s32[]{:S(2)}) async-start(), calls=%async_computation.11 | async-start | bytes 5242880 | tf_op jit(solution)/shard_map/reduce_scatter | solution.py:87
  591.9 48.7 %collective-permute-start.9 = (bf16[384,2048]{1,0:T(8,128)(2,1)S(1)}, bf16[384,2048]{1,0:T(8,128)(2,1)S(1)}, u32[]{:S(2)}, u32[]{:S(2)}) collective-permute-start(bf16[384,2048]{1,0:T(8,128)(2,1)S(1)} %constant_dynamic-slice_fusion.8), channel_id=1, source_target_pairs={{0,1},{1,0},{2,3},{3,2},{4,5},{5,4},{6,7},{7,6},{8,9},{9,8},{10,11... | collective-permute-start | bytes 4718600 | tf_op jit(solution)/shard_map/ppermute | solution.py:105
  594.8 41.2 %collective-permute-start.13 = (bf16[768,256]{0,1:T(8,128)(2,1)S(1)}, bf16[768,256]{0,1:T(8,128)(2,1)S(1)}, u32[]{:S(2)}, u32[]{:S(2)}) collective-permute-start(bf16[768,256]{0,1:T(8,128)(2,1)S(1)} %pad_maximum_fusion.7), channel_id=1, source_target_pairs={{0,1},{1,0},{2,3},{3,2},{4,5},{5,4},{6,7},{7,6},{8,9},{9,8},{10,11... | collective-permute-start | bytes 1179656 | tf_op jit(solution)/shard_map/ppermute | solution.py:105
  596.7 58.0 %collective-permute-start.12 = (bf16[768,2048]{1,0:T(8,128)(2,1)}, bf16[768,2048]{1,0:T(8,128)(2,1)}, u32[]{:S(2)}, u32[]{:S(2)}) collective-permute-start(bf16[768,2048]{1,0:T(8,128)(2,1)} %add_convert_fusion.1), channel_id=1, source_target_pairs={{0,2},{2,0},{4,6},{6,4},{8,10},{10,8},{12,14},{14,12},{16,18},{18,... | collective-permute-start | bytes 9437192 | tf_op jit(solution)/shard_map/ppermute | solution.py:55
  598.8 63.9 %collective-permute-start.16 = (bf16[768,512]{0,1:T(8,128)(2,1)}, bf16[768,512]{0,1:T(8,128)(2,1)}, u32[]{:S(2)}, u32[]{:S(2)}) collective-permute-start(bf16[768,512]{0,1:T(8,128)(2,1)} %get-tuple-element.74), channel_id=1, source_target_pairs={{0,2},{2,0},{4,6},{6,4},{8,10},{10,8},{12,14},{14,12},{16,18},{18,... | collective-permute-start | bytes 2359304 | tf_op jit(solution)/shard_map/ppermute | solution.py:55
  636.0 26.7 %collective-permute-start.15 = (bf16[768,2048]{1,0:T(8,128)(2,1)}, bf16[768,2048]{1,0:T(8,128)(2,1)}, u32[]{:S(2)}, u32[]{:S(2)}) collective-permute-start(bf16[768,2048]{1,0:T(8,128)(2,1)} %get-tuple-element.51), channel_id=1, source_target_pairs={{0,2},{2,0},{4,6},{6,4},{8,10},{10,8},{12,14},{14,12},{16,18},{18,... | collective-permute-start | bytes 9437192 | tf_op jit(solution)/shard_map/ppermute | solution.py:55
  640.7 14.0 %collective-permute-start.14 = (bf16[768,640]{0,1:T(8,128)(2,1)}, bf16[768,640]{0,1:T(8,128)(2,1)}, u32[]{:S(2)}, u32[]{:S(2)}) collective-permute-start(bf16[768,640]{0,1:T(8,128)(2,1)} %get-tuple-element.68), channel_id=1, source_target_pairs={{0,2},{2,0},{4,6},{6,4},{8,10},{10,8},{12,14},{14,12},{16,18},{18,... | collective-permute-start | bytes 2949128 | tf_op jit(solution)/shard_map/ppermute | solution.py:55
  644.3 9.5 collective-permute-start.17
  653.6 360.7 %reduce-scatter.4.cloned.1.call-start = ((), (), s32[]{:S(2)}) async-start(), calls=%async_computation.9 | async-start | bytes 3276800 | tf_op jit(solution)/shard_map/reduce_scatter | solution.py:87
  653.9 8.6 collective-permute-start.18
  712.5 58.7 %collective-permute-start.19 = (bf16[4,256,1280]{2,1,0:T(8,128)(2,1)}, bf16[4,256,1280]{2,1,0:T(8,128)(2,1)}, u32[]{:S(2)}, u32[]{:S(2)}) collective-permute-start(bf16[4,256,1280]{2,1,0:T(8,128)(2,1)} %bitcast.135), channel_id=1, source_target_pairs={{0,4},{2,6},{4,0},{6,2},{8,12},{10,14},{12,8},{14,10},{16,20},{18,... | collective-permute-start | bytes 7864328 | tf_op jit(solution)/shard_map/ppermute | solution.py:84
  775.9 244.6 %reduce-scatter.6.cloned.1.call-start = ((), (), s32[]{:S(2)}) async-start(), calls=%async_computation.10 | async-start | bytes 5242880 | tf_op jit(solution)/shard_map/reduce_scatter | solution.py:87
  778.7 91.3 %collective-permute-start.22 = (bf16[4,256,2048]{2,1,0:T(8,128)(2,1)S(1)}, bf16[4,256,2048]{2,1,0:T(8,128)(2,1)S(1)}, u32[]{:S(2)}, u32[]{:S(2)}) collective-permute-start(bf16[4,256,2048]{2,1,0:T(8,128)(2,1)S(1)} %dynamic-slice_bitcast_fusion.1), channel_id=1, source_target_pairs={{0,4},{2,6},{4,0},{6,2},{8,12},{10,14},{12,8},{14,10},{16,20},{18,... | collective-permute-start | bytes 12582920 | tf_op jit(solution)/shard_map/ppermute | solution.py:84
  882.4 86.2 %all-to-all-start.3 = ((bf16[16,24,2048]{2,1,0:T(8,128)(2,1)}), bf16[16,24,2048]{2,1,0:T(8,128)(2,1)}, u32[]{:S(2)}, u32[]{:S(2)}) async-start(bf16[16,24,2048]{2,1,0:T(8,128)(2,1)} %bitcast.27), calls=%async_computation.3 | async-start | bytes 3145728 | tf_op jit(solution)/shard_map/all_to_all | solution.py:310
  889.8 85.7 %collective-permute-start.10 = (bf16[384,2048]{1,0:T(8,128)(2,1)}, bf16[384,2048]{1,0:T(8,128)(2,1)}, u32[]{:S(2)}, u32[]{:S(2)}) collective-permute-start(bf16[384,2048]{1,0:T(8,128)(2,1)} %bitcast.25), channel_id=1, source_target_pairs={{0,1},{1,0},{2,3},{3,2},{4,5},{5,4},{6,7},{7,6},{8,9},{9,8},{10,11... | collective-permute-start | bytes 4718600 | tf_op jit(solution)/shard_map/ppermute | solution.py:105
  968.6 36.2 %collective-permute-start.11 = (bf16[384,2048]{1,0:T(8,128)(2,1)}, bf16[384,2048]{1,0:T(8,128)(2,1)}, u32[]{:S(2)}, u32[]{:S(2)}) collective-permute-start(bf16[384,2048]{1,0:T(8,128)(2,1)} %bitcast.28), channel_id=1, source_target_pairs={{0,1},{1,0},{2,3},{3,2},{4,5},{5,4},{6,7},{7,6},{8,9},{9,8},{10,11... | collective-permute-start | bytes 4718600 | tf_op jit(solution)/shard_map/ppermute | solution.py:105
  975.2 36.2 %collective-permute-start.25 = (bf16[128,2048]{1,0:T(8,128)(2,1)}, bf16[128,2048]{1,0:T(8,128)(2,1)}, u32[]{:S(2)}, u32[]{:S(2)}) collective-permute-start(bf16[128,2048]{1,0:T(8,128)(2,1)} %constant_dynamic-slice_fusion), channel_id=1, source_target_pairs={{0,2},{2,0},{4,6},{6,4},{8,10},{10,8},{12,14},{14,12},{16,18},{18,... | collective-permute-start | bytes 1572872 | tf_op jit(solution)/shard_map/ppermute | solution.py:55
  1016.0 6.4 collective-permute-start.20
  (44 other events, 1314.7 us)
Sparse Core Ops, SparseCore 0:
  13.1 125.5 all-gather.2
  140.9 173.4 all-gather.4
  653.7 77.7 reduce-scatter.7
  776.1 50.9 reduce-scatter.3
  876.2 112.3 reduce-scatter.5

commit v4 on v3

--- a/solution.py
+++ b/solution.py
@@ -76,21 +76,8 @@
 
 def summed_rows(low):
     members = lax.axis_size("dp")
-    side = lax.rem(lax.axis_index("dp") // 2, 2)
-    rows, cols = low.shape
-    blocks = low.reshape(members // 4, 2, rows * 2 // members, cols)
-    kept = lax.dynamic_index_in_dim(blocks, side, axis=1, keepdims=False)
-    leaving = lax.dynamic_index_in_dim(blocks, 1 - side, axis=1, keepdims=False)
-    other = lax.ppermute(leaving, "dp", [(i, i ^ 2) for i in range(members)])
-    near = (kept.astype(jnp.float32) + other.astype(jnp.float32)).astype(jnp.bfloat16)
-    groups = [list(range(first, members, 4)) for first in range(4)]
-    return lax.psum_scatter(
-        near.reshape(rows // 2, cols),
-        "dp",
-        scatter_dimension=0,
-        axis_index_groups=groups,
-        tiled=True,
-    )
+    groups = [list(range(core, members, 2)) for core in range(2)]
+    return lax.psum_scatter(low, "dp", scatter_dimension=0, axis_index_groups=groups, tiled=True)
 
 
 def own_columns(chip_rows, core):

time: 1040 us -> 1140 us (1.096)
  the two profiles are of different devices: /device:TPU:15 before, /device:TPU:0 now
where the time goes in v4:
time: 1140 us; the launch traced here: 1130 us
  waiting for transfers between devices  606 us (53%)
  matrix products  219 us (19%)
  other arithmetic  133 us (12%)
  blocking collectives  75.3 us (7%)
  local copies, waits for them, and re-layouts  53.6 us (5%)
  starting transfers between devices  29.2 us (3%)
  between operations  15 us (1%)
    reduce_scatter x3, waiting for transfers between devices, summed_rows(): lax.psum_scatter(low, 'dp', scatter_dimension=0, axis_index_groups=groups...  318 us
    ppermute x10, waiting for transfers between devices, swap_tensor(): return lax.ppermute(values, 'tensor', [(0, 1), (1, 0)])  226 us
    all_to_all x1, blocking collectives, fetched(): lax.all_to_all(rows[own_sends], 'dp', split_axis=0, concat_axis=0, tiled=...  75.3 us
    all_to_all x1, waiting for transfers between devices, per_device(): lax.all_to_all(grad_resid, 'dp', split_axis=0, concat_axis=0, tiled=True)  54.9 us
    dot_general x4, matrix products, right_product(): lax.dot_general(first_op, second_op, (((1,), (1,)), ((), ())), preferred_...  54.8 us
    dot_general x4, matrix products, left_product(): lax.dot_general(first_op, second_op, (((0,), (0,)), ((), ())), preferred_...  50.7 us
    dot_general x1, matrix products, per_device(): jnp.dot(grad_here, full_down, preferred_element_type=jnp.float32)  27.9 us
    dot_general x1, matrix products, per_device(): jnp.dot(normed_two, full_up, preferred_element_type=jnp.float32)  23.2 us
  transfers between devices with their start and end apart: 31, of which 11 were waited for; matrix products, arithmetic and copies ran while one was open for 27% of the time, Pallas kernels for 0%

profile of v4, /device:TPU:0, one launch (start us, length us, event | category | flops | bytes accessed | tf_op | source)
XLA Modules:
  0.0 1131.3 jit_solution(722298358719726094)
XLA Ops:
  24.7 75.3 %all_to_all.48 = bf16[16,24,2048]{2,1,0:T(8,128)(2,1)} all-to-all(bf16[16,24,2048]{2,1,0:T(8,128)(2,1)} %bitcast.112), channel_id=1, replica_groups=mesh['dp'=16,'tensor'=2] {'dp'}, dimensions={0} | all-to-all | bytes 3145728 | tf_op jit(solution)/shard_map/all_to_all | solution.py:170
  104.6 7.8 all-to-all-start.1
  112.4 8.2 sort.63
  126.9 9.9 collective-permute-done
  153.0 6.9 fusion.60
  165.3 11.4 %fusion.122 = (f32[8,768]{1,0:T(8,128)S(1)}, f32[8,768,768]{1,2,0:T(8,128)}) fusion(bf16[768,8,128]{0,2,1:T(8,128)(2,1)} %bitcast.109, bf16[768,1280]{1,0:T(8,128)(2,1)} %copy-done.17, pred[768,768]{0,1:T(8,128)(4,1)} %compare_and_fusion), kind=kOutput, calls=%fused_computation.226 | convolution fusion | flops 1222109184 | bytes 21258240 | tf_op jit(solution)/shard_map/qhd,kd->hqk/dot_general | solution.py:107
  176.7 9.2 fusion.3
  186.0 10.6 fusion.84
  196.5 7.8 fusion.57
  206.4 102.3 %collective-permute-done.3 = bf16[384,2048]{1,0:T(8,128)(2,1)} collective-permute-done((bf16[384,2048]{1,0:T(8,128)(2,1)}, bf16[384,2048]{1,0:T(8,128)(2,1)}, u32[]{:S(2)}, u32[]{:S(2)}) %collective-permute-start.3) | collective-permute-done | bytes 1572896 | tf_op jit(solution)/shard_map/ppermute | solution.py:92
  323.4 23.2 %multiply_convert_fusion = (bf16[768,4096]{1,0:T(8,128)(2,1)}, f32[768,4096]{1,0:T(8,128)}) fusion(bf16[768,2048]{1,0:T(8,128)(2,1)} %add_convert_fusion, bf16[2048,8192]{1,0:T(8,128)(2,1)} %all-gather.5.cloned.1.call-done), kind=kOutput, calls=%fused_computation.32 | convolution fusion | flops 12913213440 | bytes 38797312 | tf_op jit(solution)/shard_map/dot_general | solution.py:211
  352.0 19.9 %fusion.69 = bf16[768,2048]{1,0:T(8,128)(2,1)} fusion(bf16[768,4096]{1,0:T(8,128)(2,1)} %get-tuple-element.127, bf16[2048,8192]{1,0:T(8,128)(2,1)} %all-gather.5.cloned.1.call-done), kind=kOutput, calls=%fused_computation.86 | convolution fusion | flops 12886474752 | bytes 26214400 | tf_op jit(solution)/shard_map/dot_general | solution.py:27
  376.5 18.0 %convolution_convert_fusion.1 = bf16[2048,2048]{1,0:T(8,128)(2,1)} fusion(bf16[768,2048]{1,0:T(8,128)(2,1)} %collective-permute-done.4, bf16[384,2048]{1,0:T(8,128)(2,1)S(1)} %copy-done.12, bf16[384,2048]{1,0:T(8,128)(2,1)S(1)} %copy-done.10, bf16[768,2048]{1,0:T(8,128)(2,1)} %collective-permute-done.5, bf16[768,2048]{1,0:T(8,128)(2,1)S(1)} %get-tuple-element.99), kind=kOutput, calls=%fused_computation.38 | convolution fusion | flops 12920553472 | bytes 20971520 | tf_op jit(solution)/shard_map/dot_general | solution.py:33
  394.5 27.9 %fusion.19 = bf16[768,4096]{1,0:T(8,128)(2,1)} fusion(f32[768,4096]{1,0:T(8,128)} %get-tuple-element.128, bf16[768,2048]{1,0:T(8,128)(2,1)} %pad_maximum_fusion.2, bf16[2048,8192]{1,0:T(8,128)(2,1)} %all-gather.5.cloned.1.call-done), kind=kOutput, calls=%fused_computation.31 | convolution fusion | flops 12947816448 | bytes 38797312 | tf_op jit(solution)/shard_map/dot_general | solution.py:217
  422.4 6.5 constant_dynamic-slice_fusion.9
  429.1 19.8 %fusion.66 = bf16[768,2048]{1,0:T(8,128)(2,1)} fusion(bf16[768,4096]{1,0:T(8,128)(2,1)} %fusion.19, bf16[2048,8192]{1,0:T(8,128)(2,1)} %all-gather.5.cloned.1.call-done), kind=kOutput, calls=%fused_computation.85 | convolution fusion | flops 12886474752 | bytes 26214400 | tf_op jit(solution)/shard_map/dot_general | solution.py:27
  454.1 18.8 %convolution_convert_fusion = bf16[2048,2048]{1,0:T(8,128)(2,1)} fusion(bf16[768,2048]{1,0:T(8,128)(2,1)} %collective-permute-done.7, bf16[768,2048]{1,0:T(8,128)(2,1)} %add_convert_fusion, bf16[768,2048]{1,0:T(8,128)(2,1)} %collective-permute-done.8, bf16[768,2048]{1,0:T(8,128)(2,1)S(1)} %copy-done.16), kind=kOutput, calls=%fused_computation.37 | convolution fusion | flops 12914262016 | bytes 20971520 | tf_op jit(solution)/shard_map/dot_general | solution.py:33
  472.9 46.6 %collective-permute-done.6 = bf16[768,2048]{1,0:T(8,128)(2,1)} collective-permute-done((bf16[768,2048]{1,0:T(8,128)(2,1)}, bf16[768,2048]{1,0:T(8,128)(2,1)}, u32[]{:S(2)}, u32[]{:S(2)}) %collective-permute-start.6) | collective-permute-done | bytes 3145760 | tf_op jit(solution)/shard_map/ppermute | solution.py:92
  537.7 6.6 fusion.81
  545.0 9.6 fusion.93
  554.6 12.0 %fusion = (f32[8,768]{1,0:T(8,128)S(1)}, f32[768,768,8]{1,0,2:T(8,128)}) fusion(f32[8,768,768]{1,2,0:T(8,128)} %get-tuple-element.126, f32[8,768]{1,0:T(8,128)S(1)} %log_add_fusion, bf16[768,8,128]{0,2,1:T(8,128)(2,1)S(1)} %bitcast.108, bf16[768,1280]{1,0:T(8,128)(2,1)} %copy-done.17), kind=kOutput, calls=%fused_computation.6 | convolution fusion | flops 1222109184 | bytes 39567360 | tf_op jit(solution)/shard_map/qhd,kd->hqk/dot_general | solution.py:235
  566.7 12.9 %fusion.2 = bf16[8,768,768]{1,2,0:T(8,128)(2,1)S(1)} fusion(f32[768,768,8]{1,0,2:T(8,128)} %get-tuple-element.130, f32[8,768,768]{1,2,0:T(8,128)} %get-tuple-element.126, f32[8,768]{1,0:T(8,128)S(1)} %get-tuple-element.129, f32[8,768]{1,0:T(8,128)S(1)} %log_add_fusion), kind=kLoop, calls=%fused_computation.8 | loop fusion | flops 18874368 | bytes 47235072 | tf_op jit(solution)/shard_map/convert_element_type | solution.py:239
  591.8 7.4 fusion.63
  604.9 39.6 %collective-permute-done.13 = bf16[768,256]{0,1:T(8,128)(2,1)S(1)} collective-permute-done((bf16[768,256]{0,1:T(8,128)(2,1)S(1)}, bf16[768,256]{0,1:T(8,128)(2,1)S(1)}, u32[]{:S(2)}, u32[]{:S(2)}) %collective-permute-start.13) | collective-permute-done | bytes 393248 | tf_op jit(solution)/shard_map/ppermute | solution.py:92
  655.6 7.6 fusion.72
  663.4 6.3 fusion.75
  669.7 9.3 pad_maximum_fusion
  693.2 54.9 %all-to-all-done.3 = bf16[16,24,2048]{2,1,0:T(8,128)(2,1)} async-done(((bf16[16,24,2048]{2,1,0:T(8,128)(2,1)}), bf16[16,24,2048]{2,1,0:T(8,128)(2,1)}, u32[]{:S(2)}, u32[]{:S(2)}) %all-to-all-start.3) | async-done | bytes 1572896 | tf_op jit(solution)/shard_map/all_to_all | solution.py:297
  759.9 25.1 %collective-permute-done.11 = bf16[384,2048]{1,0:T(8,128)(2,1)} collective-permute-done((bf16[384,2048]{1,0:T(8,128)(2,1)}, bf16[384,2048]{1,0:T(8,128)(2,1)}, u32[]{:S(2)}, u32[]{:S(2)}) %collective-permute-start.11) | collective-permute-done | bytes 1572896 | tf_op jit(solution)/shard_map/ppermute | solution.py:92
  791.5 26.0 %reduce-scatter.4.cloned.1.call-done = bf16[256,1280]{0,1:T(8,128)(2,1)} async-done(((bf16[2048,1280]{0,1:T(8,128)(2,1)}), bf16[256,1280]{0,1:T(8,128)(2,1)}) %reduce-scatter.4.cloned.1.call-update) | async-done | bytes 655376 | tf_op jit(solution)/shard_map/reduce_scatter | solution.py:80
  820.2 148.4 %reduce-scatter.8.cloned.1.call-done = bf16[256,2048]{1,0:T(8,128)(2,1)} async-done(((bf16[2048,2048]{1,0:T(8,128)(2,1)}), bf16[256,2048]{1,0:T(8,128)(2,1)}) %reduce-scatter.8.cloned.1.call-update) | async-done | bytes 1048592 | tf_op jit(solution)/shard_map/reduce_scatter | solution.py:80
  974.7 143.9 %reduce-scatter.6.cloned.1.call-done = bf16[256,2048]{1,0:T(8,128)(2,1)} async-done(((bf16[2048,2048]{1,0:T(8,128)(2,1)}), bf16[256,2048]{1,0:T(8,128)(2,1)}) %reduce-scatter.6.cloned.1.call-update) | async-done | bytes 1048592 | tf_op jit(solution)/shard_map/reduce_scatter | solution.py:80
  (262 shorter events, 176.8 us)
Async XLA Ops:
  7.2 138.5 %all-gather.3.cloned.1.call-start = ((), (), s32[]{:S(2)}) async-start(), calls=%async_computation.7 | async-start | bytes 10584064 | tf_op jit(solution)/shard_map/all_gather | solution.py:139
  13.0 310.5 %all-gather.5.cloned.1.call-start = ((), (), s32[]{:S(2)}) async-start(), calls=%async_computation.8 | async-start | bytes 35651584 | tf_op jit(solution)/shard_map/all_gather | solution.py:153
  100.0 36.7 %collective-permute-start = (bf16[384,2048]{1,0:T(8,128)(2,1)}, bf16[384,2048]{1,0:T(8,128)(2,1)}, u32[]{:S(2)}, u32[]{:S(2)}) collective-permute-start(bf16[384,2048]{1,0:T(8,128)(2,1)} %bitcast.1), channel_id=1, source_target_pairs={{0,1},{1,0},{2,3},{3,2},{4,5},{5,4},{6,7},{7,6},{8,9},{9,8},{10,11... | collective-permute-start | bytes 4718600 | tf_op jit(solution)/shard_map/ppermute | solution.py:92
  104.6 101.6 %all-to-all-start.1 = ((bf16[16,24,2048]{2,1,0:T(8,128)(2,1)}), bf16[16,24,2048]{2,1,0:T(8,128)(2,1)}, u32[]{:S(2)}, u32[]{:S(2)}) async-start(bf16[16,24,2048]{2,1,0:T(8,128)(2,1)} %bitcast.111), calls=%async_computation.1 | async-start | bytes 3145728 | tf_op jit(solution)/shard_map/all_to_all | solution.py:170
  138.8 174.7 %copy-start.4 = (bf16[384,2048]{1,0:T(8,128)(2,1)}, bf16[384,2048]{1,0:T(8,128)(2,1)S(1)}, u32[]{:S(2)}) copy-start(bf16[384,2048]{1,0:T(8,128)(2,1)S(1)} %get-tuple-element.103) | copy-start | bytes 4718596
  204.4 109.2 %collective-permute-start.1 = (bf16[768,2048]{1,0:T(8,128)(2,1)}, bf16[768,2048]{1,0:T(8,128)(2,1)}, u32[]{:S(2)}, u32[]{:S(2)}) collective-permute-start(bf16[768,2048]{1,0:T(8,128)(2,1)} %fusion.57), channel_id=1, source_target_pairs={{0,1},{1,0},{2,3},{3,2},{4,5},{5,4},{6,7},{7,6},{8,9},{9,8},{10,11... | collective-permute-start | bytes 9437192 | tf_op jit(solution)/shard_map/ppermute | solution.py:92
  206.2 102.5 %collective-permute-start.3 = (bf16[384,2048]{1,0:T(8,128)(2,1)}, bf16[384,2048]{1,0:T(8,128)(2,1)}, u32[]{:S(2)}, u32[]{:S(2)}) collective-permute-start(bf16[384,2048]{1,0:T(8,128)(2,1)} %bitcast.18), channel_id=1, source_target_pairs={{0,1},{1,0},{2,3},{3,2},{4,5},{5,4},{6,7},{7,6},{8,9},{9,8},{10,11... | collective-permute-start | bytes 4718600 | tf_op jit(solution)/shard_map/ppermute | solution.py:92
  313.5 63.0 %collective-permute-start.4 = (bf16[768,2048]{1,0:T(8,128)(2,1)}, bf16[768,2048]{1,0:T(8,128)(2,1)}, u32[]{:S(2)}, u32[]{:S(2)}) collective-permute-start(bf16[768,2048]{1,0:T(8,128)(2,1)} %pad_maximum_fusion.2), channel_id=1, source_target_pairs={{0,2},{2,0},{4,6},{6,4},{8,10},{10,8},{12,14},{14,12},{16,18},{18,... | collective-permute-start | bytes 9437192 | tf_op jit(solution)/shard_map/ppermute | solution.py:55
  323.0 131.1 %collective-permute-start.7 = (bf16[768,2048]{1,0:T(8,128)(2,1)}, bf16[768,2048]{1,0:T(8,128)(2,1)}, u32[]{:S(2)}, u32[]{:S(2)}) collective-permute-start(bf16[768,2048]{1,0:T(8,128)(2,1)} %add_convert_fusion), channel_id=1, source_target_pairs={{0,2},{2,0},{4,6},{6,4},{8,10},{10,8},{12,14},{14,12},{16,18},{18,... | collective-permute-start | bytes 9437192 | tf_op jit(solution)/shard_map/ppermute | solution.py:55
  351.9 24.5 %collective-permute-start.5 = (bf16[768,2048]{1,0:T(8,128)(2,1)}, bf16[768,2048]{1,0:T(8,128)(2,1)}, u32[]{:S(2)}, u32[]{:S(2)}) collective-permute-start(bf16[768,2048]{1,0:T(8,128)(2,1)} %get-tuple-element.100), channel_id=1, source_target_pairs={{0,2},{2,0},{4,6},{6,4},{8,10},{10,8},{12,14},{14,12},{16,18},{18,... | collective-permute-start | bytes 9437192 | tf_op jit(solution)/shard_map/ppermute | solution.py:55
  374.8 74.4 %collective-permute-start.2 = (bf16[384,2048]{1,0:T(8,128)(2,1)}, bf16[384,2048]{1,0:T(8,128)(2,1)}, u32[]{:S(2)}, u32[]{:S(2)}) collective-permute-start(bf16[384,2048]{1,0:T(8,128)(2,1)} %constant_dynamic-slice_fusion.12), channel_id=1, source_target_pairs={{0,1},{1,0},{2,3},{3,2},{4,5},{5,4},{6,7},{7,6},{8,9},{9,8},{10,11... | collective-permute-start | bytes 4718600 | tf_op jit(solution)/shard_map/ppermute | solution.py:92
  428.9 25.2 %collective-permute-start.8 = (bf16[768,2048]{1,0:T(8,128)(2,1)}, bf16[768,2048]{1,0:T(8,128)(2,1)}, u32[]{:S(2)}, u32[]{:S(2)}) collective-permute-start(bf16[768,2048]{1,0:T(8,128)(2,1)} %get-tuple-element.98), channel_id=1, source_target_pairs={{0,2},{2,0},{4,6},{6,4},{8,10},{10,8},{12,14},{14,12},{16,18},{18,... | collective-permute-start | bytes 9437192 | tf_op jit(solution)/shard_map/ppermute | solution.py:55
  448.8 70.7 %collective-permute-start.6 = (bf16[768,2048]{1,0:T(8,128)(2,1)}, bf16[768,2048]{1,0:T(8,128)(2,1)}, u32[]{:S(2)}, u32[]{:S(2)}) collective-permute-start(bf16[768,2048]{1,0:T(8,128)(2,1)} %fusion.66), channel_id=1, source_target_pairs={{0,1},{1,0},{2,3},{3,2},{4,5},{5,4},{6,7},{7,6},{8,9},{9,8},{10,11... | collective-permute-start | bytes 9437192 | tf_op jit(solution)/shard_map/ppermute | solution.py:92
  587.0 61.5 %all-to-all-start.2 = ((bf16[16,24,2048]{2,1,0:T(8,128)(2,1)}), bf16[16,24,2048]{2,1,0:T(8,128)(2,1)}, u32[]{:S(2)}, u32[]{:S(2)}) async-start(bf16[16,24,2048]{2,1,0:T(8,128)(2,1)} %bitcast.24), calls=%async_computation.2 | async-start | bytes 3145728 | tf_op jit(solution)/shard_map/all_to_all | solution.py:258
  591.4 226.1 %reduce-scatter.4.cloned.1.call-start = ((), (), s32[]{:S(2)}) async-start(), calls=%async_computation.9 | async-start | bytes 5898240 | tf_op jit(solution)/shard_map/reduce_scatter | solution.py:80
  599.4 48.5 %collective-permute-start.9 = (bf16[384,2048]{1,0:T(8,128)(2,1)S(1)}, bf16[384,2048]{1,0:T(8,128)(2,1)S(1)}, u32[]{:S(2)}, u32[]{:S(2)}) collective-permute-start(bf16[384,2048]{1,0:T(8,128)(2,1)S(1)} %constant_dynamic-slice_fusion.7), channel_id=1, source_target_pairs={{0,1},{1,0},{2,3},{3,2},{4,5},{5,4},{6,7},{7,6},{8,9},{9,8},{10,11... | collective-permute-start | bytes 4718600 | tf_op jit(solution)/shard_map/ppermute | solution.py:92
  602.2 53.4 %collective-permute-start.12 = (bf16[768,2048]{1,0:T(8,128)(2,1)}, bf16[768,2048]{1,0:T(8,128)(2,1)}, u32[]{:S(2)}, u32[]{:S(2)}) collective-permute-start(bf16[768,2048]{1,0:T(8,128)(2,1)} %add_convert_fusion.1), channel_id=1, source_target_pairs={{0,2},{2,0},{4,6},{6,4},{8,10},{10,8},{12,14},{14,12},{16,18},{18,... | collective-permute-start | bytes 9437192 | tf_op jit(solution)/shard_map/ppermute | solution.py:55
  602.5 41.9 %collective-permute-start.13 = (bf16[768,256]{0,1:T(8,128)(2,1)S(1)}, bf16[768,256]{0,1:T(8,128)(2,1)S(1)}, u32[]{:S(2)}, u32[]{:S(2)}) collective-permute-start(bf16[768,256]{0,1:T(8,128)(2,1)S(1)} %pad_maximum_fusion.7), channel_id=1, source_target_pairs={{0,1},{1,0},{2,3},{3,2},{4,5},{5,4},{6,7},{7,6},{8,9},{9,8},{10,11... | collective-permute-start | bytes 1179656 | tf_op jit(solution)/shard_map/ppermute | solution.py:92
  604.6 58.7 %collective-permute-start.15 = (bf16[768,2048]{1,0:T(8,128)(2,1)}, bf16[768,2048]{1,0:T(8,128)(2,1)}, u32[]{:S(2)}, u32[]{:S(2)}) collective-permute-start(bf16[768,2048]{1,0:T(8,128)(2,1)} %get-tuple-element.91), channel_id=1, source_target_pairs={{0,2},{2,0},{4,6},{6,4},{8,10},{10,8},{12,14},{14,12},{16,18},{18,... | collective-permute-start | bytes 9437192 | tf_op jit(solution)/shard_map/ppermute | solution.py:55
  647.9 7.7 collective-permute-start.14
  651.6 3.8 collective-permute-start.17
  652.2 11.2 collective-permute-start.16
  655.5 7.7 collective-permute-start.18
  679.0 289.5 %reduce-scatter.8.cloned.1.call-start = ((), (), s32[]{:S(2)}) async-start(), calls=%async_computation.11 | async-start | bytes 9437184 | tf_op jit(solution)/shard_map/reduce_scatter | solution.py:80
  679.6 439.0 %reduce-scatter.6.cloned.1.call-start = ((), (), s32[]{:S(2)}) async-start(), calls=%async_computation.10 | async-start | bytes 9437184 | tf_op jit(solution)/shard_map/reduce_scatter | solution.py:80
  686.5 61.6 %all-to-all-start.3 = ((bf16[16,24,2048]{2,1,0:T(8,128)(2,1)}), bf16[16,24,2048]{2,1,0:T(8,128)(2,1)}, u32[]{:S(2)}, u32[]{:S(2)}) async-start(bf16[16,24,2048]{2,1,0:T(8,128)(2,1)} %bitcast.27), calls=%async_computation.3 | async-start | bytes 3145728 | tf_op jit(solution)/shard_map/all_to_all | solution.py:297
  692.8 60.6 %collective-permute-start.10 = (bf16[384,2048]{1,0:T(8,128)(2,1)}, bf16[384,2048]{1,0:T(8,128)(2,1)}, u32[]{:S(2)}, u32[]{:S(2)}) collective-permute-start(bf16[384,2048]{1,0:T(8,128)(2,1)} %bitcast.25), channel_id=1, source_target_pairs={{0,1},{1,0},{2,3},{3,2},{4,5},{5,4},{6,7},{7,6},{8,9},{9,8},{10,11... | collective-permute-start | bytes 4718600 | tf_op jit(solution)/shard_map/ppermute | solution.py:92
  748.1 36.9 %collective-permute-start.11 = (bf16[384,2048]{1,0:T(8,128)(2,1)}, bf16[384,2048]{1,0:T(8,128)(2,1)}, u32[]{:S(2)}, u32[]{:S(2)}) collective-permute-start(bf16[384,2048]{1,0:T(8,128)(2,1)} %bitcast.28), channel_id=1, source_target_pairs={{0,1},{1,0},{2,3},{3,2},{4,5},{5,4},{6,7},{7,6},{8,9},{9,8},{10,11... | collective-permute-start | bytes 4718600 | tf_op jit(solution)/shard_map/ppermute | solution.py:92
  818.5 154.2 %collective-permute-start.19 = (bf16[128,640]{0,1:T(8,128)(2,1)S(1)}, bf16[128,640]{0,1:T(8,128)(2,1)S(1)}, u32[]{:S(2)}, u32[]{:S(2)}) collective-permute-start(bf16[128,640]{0,1:T(8,128)(2,1)S(1)} %constant_dynamic-slice_fusion.4), channel_id=1, source_target_pairs={{0,2},{2,0},{4,6},{6,4},{8,10},{10,8},{12,14},{14,12},{16,18},{18,... | collective-permute-start | bytes 491528 | tf_op jit(solution)/shard_map/ppermute | solution.py:55
  819.6 152.0 %collective-permute-start.20 = (bf16[128,512]{0,1:T(8,128)(2,1)S(1)}, bf16[128,512]{0,1:T(8,128)(2,1)S(1)}, u32[]{:S(2)}, u32[]{:S(2)}) collective-permute-start(bf16[128,512]{0,1:T(8,128)(2,1)S(1)} %constant_dynamic-slice_fusion.3), channel_id=1, source_target_pairs={{0,2},{2,0},{4,6},{6,4},{8,10},{10,8},{12,14},{14,12},{16,18},{18,... | collective-permute-start | bytes 393224 | tf_op jit(solution)/shard_map/ppermute | solution.py:55
  970.4 149.5 %collective-permute-start.22 = (bf16[128,2048]{1,0:T(8,128)(2,1)}, bf16[128,2048]{1,0:T(8,128)(2,1)}, u32[]{:S(2)}, u32[]{:S(2)}) collective-permute-start(bf16[128,2048]{1,0:T(8,128)(2,1)} %constant_dynamic-slice_fusion.1), channel_id=1, source_target_pairs={{0,2},{2,0},{4,6},{6,4},{8,10},{10,8},{12,14},{14,12},{16,18},{18,... | collective-permute-start | bytes 1572872 | tf_op jit(solution)/shard_map/ppermute | solution.py:55
  1119.8 2.9 collective-permute-start.21
  (44 other events, 1156.8 us)
Sparse Core Ops, SparseCore 0:
  13.1 132.6 all-gather.2
  147.9 168.3 all-gather.4
  679.1 138.3 reduce-scatter.3
  821.0 147.4 reduce-scatter.7
  972.0 146.5 reduce-scatter.5

commit v5 on v4

--- a/solution.py
+++ b/solution.py
@@ -78,6 +78,24 @@
     members = lax.axis_size("dp")
     groups = [list(range(core, members, 2)) for core in range(2)]
     return lax.psum_scatter(low, "dp", scatter_dimension=0, axis_index_groups=groups, tiled=True)
+
+
+def near_sum(low):
+    members = lax.axis_size("dp")
+    side = lax.rem(lax.axis_index("dp") // 2, 2)
+    rows, cols = low.shape
+    blocks = low.reshape(members // 4, 2, rows * 2 // members, cols)
+    leaving = lax.dynamic_index_in_dim(blocks, 1 - side, axis=1, keepdims=False)
+    other = lax.ppermute(leaving, "dp", [(i, i ^ 2) for i in range(members)])
+    kept = lax.dynamic_index_in_dim(blocks, side, axis=1, keepdims=False)
+    near = kept.astype(jnp.float32) + other.astype(jnp.float32)
+    return near.astype(jnp.bfloat16).reshape(rows // 2, cols)
+
+
+def far_rows(near):
+    members = lax.axis_size("dp")
+    groups = [list(range(first, members, 4)) for first in range(4)]
+    return lax.psum_scatter(near, "dp", scatter_dimension=0, axis_index_groups=groups, tiled=True)
 
 
 def own_columns(chip_rows, core):
@@ -218,10 +236,11 @@
     gelu_back = jax.vjp(gelu_tanh, hidden_pre)[1]
     grad_up = gelu_back(grad_active)[0].astype(jnp.bfloat16)
     norm_two_part = right_product(grad_up, full_up)
-    wup_term = weight_term(both_normed_two, half_of_both(grad_up, core))
+    both_grad_up = half_of_both(grad_up, core)
+    wup_term = weight_term(both_normed_two, both_grad_up)
     mlp_part = right_product(active, full_down)
-    grad_norm_two, wup_term = tensor_sum(norm_two_part, wup_term)
-    wup_rows = summed_rows(wup_term)
+    grad_norm_two = tensor_sum(norm_two_part)
+    wup_rows = far_rows(near_sum(wup_term))
     norm_two_back = jax.vjp(layer_norm, resid_mid, second_gain, second_shift)[1]
     grad_mid_norm, grad_gain_two, grad_shift_two = norm_two_back(grad_norm_two)
     grad_mid = grad_out + grad_mid_norm

time: 1140 us -> 1100 us (0.965)
  waiting for transfers between devices: 606 us -> 544 us
    reduce_scatter x3 -> x2, waiting for transfers between devices: 318 us -> 171 us  [summed_rows(): lax.psum_scatter(low, 'dp', scatter_dimension=0, axis_index_groups=groups...]
    ppermute x0 -> x1, waiting for transfers between devices: none -> 51.6 us  [near_sum(): other = lax.ppermute(leaving, 'dp', [(i, i ^ 2) for i in range(members)])]
    ppermute x10, waiting for transfers between devices: 226 us -> 256 us  [swap_tensor(): return lax.ppermute(values, 'tensor', [(0, 1), (1, 0)])]
  transfers between devices with their start and end apart: 31 -> 32, of which waited for: 11 -> 12; matrix products, arithmetic and copies ran while one was open for 27% -> 29% of each run, Pallas kernels for 0% -> 0%
where the time goes in v5:
time: 1100 us; the launch traced here: 1090 us
  waiting for transfers between devices  544 us (49%)
  matrix products  222 us (20%)
  other arithmetic  143 us (13%)
  blocking collectives  75.3 us (7%)
  local copies, waits for them, and re-layouts  58.7 us (5%)
  starting transfers between devices  34.6 us (3%)
  between operations  15.2 us (1%)
    ppermute x10, waiting for transfers between devices, swap_tensor(): return lax.ppermute(values, 'tensor', [(0, 1), (1, 0)])  256 us
    reduce_scatter x2, waiting for transfers between devices, summed_rows(): lax.psum_scatter(low, 'dp', scatter_dimension=0, axis_index_groups=groups...  171 us
    all_to_all x1, blocking collectives, fetched(): lax.all_to_all(rows[own_sends], 'dp', split_axis=0, concat_axis=0, tiled=...  75.3 us
    dot_general x4, matrix products, right_product(): lax.dot_general(first_op, second_op, (((1,), (1,)), ((), ())), preferred_...  54.3 us
    all_to_all x1, waiting for transfers between devices, per_device(): lax.all_to_all(grad_resid, 'dp', split_axis=0, concat_axis=0, tiled=True)  54 us
    dot_general x4, matrix products, left_product(): lax.dot_general(first_op, second_op, (((0,), (0,)), ((), ())), preferred_...  52.2 us
    ppermute x1, waiting for transfers between devices, near_sum(): other = lax.ppermute(leaving, 'dp', [(i, i ^ 2) for i in range(members)])  51.6 us
    dot_general x1, matrix products, per_device(): jnp.dot(grad_here, full_down, preferred_element_type=jnp.float32)  27.7 us
  transfers between devices with their start and end apart: 32, of which 12 were waited for; matrix products, arithmetic and copies ran while one was open for 29% of the time, Pallas kernels for 0%

profile of v5, /device:TPU:0, one launch (start us, length us, event | category | flops | bytes accessed | tf_op | source)
XLA Modules:
  0.0 1093.0 jit_solution(5561553933162365108)
XLA Ops:
  24.7 75.3 %all_to_all.48 = bf16[16,24,2048]{2,1,0:T(8,128)(2,1)} all-to-all(bf16[16,24,2048]{2,1,0:T(8,128)(2,1)} %bitcast.128), channel_id=1, replica_groups=mesh['dp'=16,'tensor'=2] {'dp'}, dimensions={0} | all-to-all | bytes 3145728 | tf_op jit(solution)/shard_map/all_to_all | solution.py:188
  104.6 7.6 all-to-all-start.1
  112.3 8.2 sort.63
  126.7 10.0 collective-permute-done
  153.1 7.0 fusion.61
  165.4 11.4 %fusion.123 = (f32[8,768]{1,0:T(8,128)S(1)}, f32[8,768,768]{1,2,0:T(8,128)}) fusion(bf16[768,8,128]{0,2,1:T(8,128)(2,1)} %bitcast.123, bf16[768,1280]{1,0:T(8,128)(2,1)} %copy-done.19, pred[768,768]{0,1:T(8,128)(4,1)} %compare_and_fusion), kind=kOutput, calls=%fused_computation.229 | convolution fusion | flops 1222109184 | bytes 21258240 | tf_op jit(solution)/shard_map/qhd,kd->hqk/dot_general | solution.py:125
  176.8 9.2 fusion.3
  186.0 10.6 fusion.85
  196.6 7.8 fusion.58
  206.5 102.3 %collective-permute-done.3 = bf16[384,2048]{1,0:T(8,128)(2,1)} collective-permute-done((bf16[384,2048]{1,0:T(8,128)(2,1)}, bf16[384,2048]{1,0:T(8,128)(2,1)}, u32[]{:S(2)}, u32[]{:S(2)}) %collective-permute-start.3) | collective-permute-done | bytes 1572896 | tf_op jit(solution)/shard_map/ppermute | solution.py:110
  321.2 23.4 %multiply_convert_fusion = (bf16[768,4096]{1,0:T(8,128)(2,1)}, f32[768,4096]{1,0:T(8,128)}) fusion(bf16[768,2048]{1,0:T(8,128)(2,1)S(1)} %add_convert_fusion, bf16[2048,8192]{1,0:T(8,128)(2,1)} %all-gather.5.cloned.1.call-done), kind=kOutput, calls=%fused_computation.32 | convolution fusion | flops 12913213440 | bytes 38797312 | tf_op jit(solution)/shard_map/dot_general | solution.py:229
  344.7 6.8 constant_dynamic-slice_fusion.11
  357.5 18.9 %convolution_convert_fusion.1 = bf16[2048,2048]{1,0:T(8,128)(2,1)} fusion(bf16[768,2048]{1,0:T(8,128)(2,1)} %collective-permute-done.4, bf16[384,2048]{1,0:T(8,128)(2,1)S(1)} %copy-done.12, bf16[384,2048]{1,0:T(8,128)(2,1)S(1)} %copy-done.10, bf16[768,2048]{1,0:T(8,128)(2,1)} %collective-permute-done.5, bf16[768,2048]{1,0:T(8,128)(2,1)} %get-tuple-element.95), kind=kOutput, calls=%fused_computation.40 | convolution fusion | flops 12920553472 | bytes 20971520 | tf_op jit(solution)/shard_map/dot_general | solution.py:33
  376.4 27.7 %fusion.19 = bf16[768,4096]{1,0:T(8,128)(2,1)} fusion(f32[768,4096]{1,0:T(8,128)} %get-tuple-element.124, bf16[768,2048]{1,0:T(8,128)(2,1)} %pad_maximum_fusion.2, bf16[2048,8192]{1,0:T(8,128)(2,1)} %all-gather.5.cloned.1.call-done), kind=kOutput, calls=%fused_computation.31 | convolution fusion | flops 12947816448 | bytes 38797312 | tf_op jit(solution)/shard_map/dot_general | solution.py:235
  404.1 20.0 %fusion.67 = bf16[768,2048]{1,0:T(8,128)(2,1)} fusion(bf16[768,4096]{1,0:T(8,128)(2,1)} %fusion.19, bf16[2048,8192]{1,0:T(8,128)(2,1)} %all-gather.5.cloned.1.call-done), kind=kOutput, calls=%fused_computation.88 | convolution fusion | flops 12886474752 | bytes 26214400 | tf_op jit(solution)/shard_map/dot_general | solution.py:27
  425.7 19.0 %fusion.70 = bf16[768,2048]{1,0:T(8,128)(2,1)S(1)} fusion(bf16[768,4096]{1,0:T(8,128)(2,1)} %get-tuple-element.123, bf16[2048,8192]{1,0:T(8,128)(2,1)} %all-gather.5.cloned.1.call-done), kind=kOutput, calls=%fused_computation.89 | convolution fusion | flops 12886474752 | bytes 26214400 | tf_op jit(solution)/shard_map/dot_general | solution.py:27
  448.1 80.3 %collective-permute-done.2 = bf16[384,2048]{1,0:T(8,128)(2,1)} collective-permute-done((bf16[384,2048]{1,0:T(8,128)(2,1)}, bf16[384,2048]{1,0:T(8,128)(2,1)}, u32[]{:S(2)}, u32[]{:S(2)}) %collective-permute-start.2) | collective-permute-done | bytes 1572896 | tf_op jit(solution)/shard_map/ppermute | solution.py:110
  551.8 6.5 fusion.82
  559.1 19.6 %convolution_convert_fusion = bf16[2048,2048]{1,0:T(8,128)(2,1)} fusion(bf16[768,2048]{1,0:T(8,128)(2,1)} %collective-permute-done.19, bf16[768,2048]{1,0:T(8,128)(2,1)} %copy-done.17, bf16[768,2048]{1,0:T(8,128)(2,1)} %collective-permute-done.20, bf16[768,2048]{1,0:T(8,128)(2,1)} %get-tuple-element.93), kind=kOutput, calls=%fused_computation.39 | convolution fusion | flops 12914262016 | bytes 20971520 | tf_op jit(solution)/shard_map/dot_general | solution.py:33
  585.7 12.1 %fusion = (f32[8,768]{1,0:T(8,128)S(1)}, f32[768,768,8]{1,0,2:T(8,128)}) fusion(f32[8,768,768]{1,2,0:T(8,128)} %get-tuple-element.122, f32[8,768]{1,0:T(8,128)S(1)} %log_add_fusion, bf16[768,8,128]{0,2,1:T(8,128)(2,1)S(1)} %bitcast.121, bf16[768,1280]{1,0:T(8,128)(2,1)} %copy-done.19), kind=kOutput, calls=%fused_computation.6 | convolution fusion | flops 1222109184 | bytes 39567360 | tf_op jit(solution)/shard_map/qhd,kd->hqk/dot_general | solution.py:254
  597.8 17.8 %fusion.2 = bf16[8,768,768]{1,2,0:T(8,128)(2,1)} fusion(f32[768,768,8]{1,0,2:T(8,128)} %get-tuple-element.126, f32[8,768,768]{1,2,0:T(8,128)} %get-tuple-element.122, f32[8,768]{1,0:T(8,128)S(1)} %get-tuple-element.125, f32[8,768]{1,0:T(8,128)S(1)} %log_add_fusion), kind=kLoop, calls=%fused_computation.8 | loop fusion | flops 18874368 | bytes 47235072 | tf_op jit(solution)/shard_map/convert_element_type | solution.py:258
  621.8 7.4 fusion.97
  638.4 51.6 %collective-permute-done.21 = bf16[4,256,2048]{2,1,0:T(8,128)(2,1)} collective-permute-done((bf16[4,256,2048]{2,1,0:T(8,128)(2,1)}, bf16[4,256,2048]{2,1,0:T(8,128)(2,1)}, u32[]{:S(2)}, u32[]{:S(2)}) %collective-permute-start.21) | collective-permute-done | bytes 4194336 | tf_op jit(solution)/shard_map/ppermute | solution.py:89
  690.1 7.8 fusion.24
  699.4 7.5 fusion.64
  712.6 39.1 %collective-permute-done.11 = bf16[768,256]{0,1:T(8,128)(2,1)S(1)} collective-permute-done((bf16[768,256]{0,1:T(8,128)(2,1)S(1)}, bf16[768,256]{0,1:T(8,128)(2,1)S(1)}, u32[]{:S(2)}, u32[]{:S(2)}) %collective-permute-start.11) | collective-permute-done | bytes 393248 | tf_op jit(solution)/shard_map/ppermute | solution.py:110
  762.9 7.4 fusion.73
  776.8 9.4 pad_maximum_fusion
  799.4 54.0 %all-to-all-done.3 = bf16[16,24,2048]{2,1,0:T(8,128)(2,1)} async-done(((bf16[16,24,2048]{2,1,0:T(8,128)(2,1)}), bf16[16,24,2048]{2,1,0:T(8,128)(2,1)}, u32[]{:S(2)}, u32[]{:S(2)}) %all-to-all-start.3) | async-done | bytes 1572896 | tf_op jit(solution)/shard_map/all_to_all | solution.py:316
  867.9 22.2 %collective-permute-done.9 = bf16[384,2048]{1,0:T(8,128)(2,1)} collective-permute-done((bf16[384,2048]{1,0:T(8,128)(2,1)}, bf16[384,2048]{1,0:T(8,128)(2,1)}, u32[]{:S(2)}, u32[]{:S(2)}) %collective-permute-start.9) | collective-permute-done | bytes 1572896 | tf_op jit(solution)/shard_map/ppermute | solution.py:110
  899.7 23.2 %reduce-scatter.4.cloned.1.call-done = bf16[256,1280]{0,1:T(8,128)(2,1)} async-done(((bf16[2048,1280]{0,1:T(8,128)(2,1)}), bf16[256,1280]{0,1:T(8,128)(2,1)}) %reduce-scatter.4.cloned.1.call-update) | async-done | bytes 655376 | tf_op jit(solution)/shard_map/reduce_scatter | solution.py:80
  925.5 148.0 %reduce-scatter.8.cloned.1.call-done = bf16[256,2048]{1,0:T(8,128)(2,1)} async-done(((bf16[2048,2048]{1,0:T(8,128)(2,1)}), bf16[256,2048]{1,0:T(8,128)(2,1)}) %reduce-scatter.8.cloned.1.call-update) | async-done | bytes 1048592 | tf_op jit(solution)/shard_map/reduce_scatter | solution.py:80
  (288 shorter events, 198.6 us)
Async XLA Ops:
  7.2 138.6 %all-gather.3.cloned.1.call-start = ((), (), s32[]{:S(2)}) async-start(), calls=%async_computation.7 | async-start | bytes 10584064 | tf_op jit(solution)/shard_map/all_gather | solution.py:157
  13.0 308.2 %all-gather.5.cloned.1.call-start = ((), (), s32[]{:S(2)}) async-start(), calls=%async_computation.8 | async-start | bytes 35651584 | tf_op jit(solution)/shard_map/all_gather | solution.py:171
  100.0 36.7 %collective-permute-start = (bf16[384,2048]{1,0:T(8,128)(2,1)}, bf16[384,2048]{1,0:T(8,128)(2,1)}, u32[]{:S(2)}, u32[]{:S(2)}) collective-permute-start(bf16[384,2048]{1,0:T(8,128)(2,1)} %bitcast.1), channel_id=1, source_target_pairs={{0,1},{1,0},{2,3},{3,2},{4,5},{5,4},{6,7},{7,6},{8,9},{9,8},{10,11... | collective-permute-start | bytes 4718600 | tf_op jit(solution)/shard_map/ppermute | solution.py:110
  104.6 101.7 %all-to-all-start.1 = ((bf16[16,24,2048]{2,1,0:T(8,128)(2,1)}), bf16[16,24,2048]{2,1,0:T(8,128)(2,1)}, u32[]{:S(2)}, u32[]{:S(2)}) async-start(bf16[16,24,2048]{2,1,0:T(8,128)(2,1)} %bitcast.127), calls=%async_computation.1 | async-start | bytes 3145728 | tf_op jit(solution)/shard_map/all_to_all | solution.py:188
  204.4 109.0 %collective-permute-start.1 = (bf16[768,2048]{1,0:T(8,128)(2,1)}, bf16[768,2048]{1,0:T(8,128)(2,1)}, u32[]{:S(2)}, u32[]{:S(2)}) collective-permute-start(bf16[768,2048]{1,0:T(8,128)(2,1)} %fusion.58), channel_id=1, source_target_pairs={{0,1},{1,0},{2,3},{3,2},{4,5},{5,4},{6,7},{7,6},{8,9},{9,8},{10,11... | collective-permute-start | bytes 9437192 | tf_op jit(solution)/shard_map/ppermute | solution.py:110
  206.3 102.5 %collective-permute-start.3 = (bf16[384,2048]{1,0:T(8,128)(2,1)}, bf16[384,2048]{1,0:T(8,128)(2,1)}, u32[]{:S(2)}, u32[]{:S(2)}) collective-permute-start(bf16[384,2048]{1,0:T(8,128)(2,1)} %bitcast.18), channel_id=1, source_target_pairs={{0,1},{1,0},{2,3},{3,2},{4,5},{5,4},{6,7},{7,6},{8,9},{9,8},{10,11... | collective-permute-start | bytes 4718600 | tf_op jit(solution)/shard_map/ppermute | solution.py:110
  313.4 38.4 %collective-permute-start.4 = (bf16[768,2048]{1,0:T(8,128)(2,1)}, bf16[768,2048]{1,0:T(8,128)(2,1)}, u32[]{:S(2)}, u32[]{:S(2)}) collective-permute-start(bf16[768,2048]{1,0:T(8,128)(2,1)} %pad_maximum_fusion.2), channel_id=1, source_target_pairs={{0,2},{2,0},{4,6},{6,4},{8,10},{10,8},{12,14},{14,12},{16,18},{18,... | collective-permute-start | bytes 9437192 | tf_op jit(solution)/shard_map/ppermute | solution.py:55
  351.5 6.0 collective-permute-start.5
  424.1 112.5 %collective-permute-start.6 = (bf16[768,2048]{1,0:T(8,128)(2,1)}, bf16[768,2048]{1,0:T(8,128)(2,1)}, u32[]{:S(2)}, u32[]{:S(2)}) collective-permute-start(bf16[768,2048]{1,0:T(8,128)(2,1)} %fusion.67), channel_id=1, source_target_pairs={{0,1},{1,0},{2,3},{3,2},{4,5},{5,4},{6,7},{7,6},{8,9},{9,8},{10,11... | collective-permute-start | bytes 9437192 | tf_op jit(solution)/shard_map/ppermute | solution.py:110
  447.6 80.8 %collective-permute-start.2 = (bf16[384,2048]{1,0:T(8,128)(2,1)}, bf16[384,2048]{1,0:T(8,128)(2,1)}, u32[]{:S(2)}, u32[]{:S(2)}) collective-permute-start(bf16[384,2048]{1,0:T(8,128)(2,1)} %constant_dynamic-slice_fusion.12), channel_id=1, source_target_pairs={{0,1},{1,0},{2,3},{3,2},{4,5},{5,4},{6,7},{7,6},{8,9},{9,8},{10,11... | collective-permute-start | bytes 4718600 | tf_op jit(solution)/shard_map/ppermute | solution.py:110
  448.0 111.1 %collective-permute-start.19 = (bf16[768,2048]{1,0:T(8,128)(2,1)}, bf16[768,2048]{1,0:T(8,128)(2,1)}, u32[]{:S(2)}, u32[]{:S(2)}) collective-permute-start(bf16[768,2048]{1,0:T(8,128)(2,1)} %copy-done.17), channel_id=1, source_target_pairs={{0,2},{2,0},{4,6},{6,4},{8,10},{10,8},{12,14},{14,12},{16,18},{18,... | collective-permute-start | bytes 9437192 | tf_op jit(solution)/shard_map/ppermute | solution.py:55
  536.6 22.5 %collective-permute-start.20 = (bf16[768,2048]{1,0:T(8,128)(2,1)}, bf16[768,2048]{1,0:T(8,128)(2,1)}, u32[]{:S(2)}, u32[]{:S(2)}) collective-permute-start(bf16[768,2048]{1,0:T(8,128)(2,1)} %get-tuple-element.94), channel_id=1, source_target_pairs={{0,2},{2,0},{4,6},{6,4},{8,10},{10,8},{12,14},{14,12},{16,18},{18,... | collective-permute-start | bytes 9437192 | tf_op jit(solution)/shard_map/ppermute | solution.py:55
  583.5 106.6 %collective-permute-start.21 = (bf16[4,256,2048]{2,1,0:T(8,128)(2,1)}, bf16[4,256,2048]{2,1,0:T(8,128)(2,1)}, u32[]{:S(2)}, u32[]{:S(2)}) collective-permute-start(bf16[4,256,2048]{2,1,0:T(8,128)(2,1)} %dynamic-slice_bitcast_fusion), channel_id=1, source_target_pairs={{0,4},{2,6},{4,0},{6,2},{8,12},{10,14},{12,8},{14,10},{16,20},{18,... | collective-permute-start | bytes 12582920 | tf_op jit(solution)/shard_map/ppermute | solution.py:89
  634.0 121.7 %all-to-all-start.2 = ((bf16[16,24,2048]{2,1,0:T(8,128)(2,1)}), bf16[16,24,2048]{2,1,0:T(8,128)(2,1)}, u32[]{:S(2)}, u32[]{:S(2)}) async-start(bf16[16,24,2048]{2,1,0:T(8,128)(2,1)} %bitcast.24), calls=%async_computation.2 | async-start | bytes 3145728 | tf_op jit(solution)/shard_map/all_to_all | solution.py:277
  638.4 221.1 %reduce-scatter.6.cloned.1.call-start = ((), (), s32[]{:S(2)}) async-start(), calls=%async_computation.10 | async-start | bytes 5242880 | tf_op jit(solution)/shard_map/reduce_scatter | solution.py:98
  697.9 225.0 %reduce-scatter.4.cloned.1.call-start = ((), (), s32[]{:S(2)}) async-start(), calls=%async_computation.9 | async-start | bytes 5898240 | tf_op jit(solution)/shard_map/reduce_scatter | solution.py:80
  707.1 48.0 %collective-permute-start.7 = (bf16[384,2048]{1,0:T(8,128)(2,1)S(1)}, bf16[384,2048]{1,0:T(8,128)(2,1)S(1)}, u32[]{:S(2)}, u32[]{:S(2)}) collective-permute-start(bf16[384,2048]{1,0:T(8,128)(2,1)S(1)} %constant_dynamic-slice_fusion.9), channel_id=1, source_target_pairs={{0,1},{1,0},{2,3},{3,2},{4,5},{5,4},{6,7},{7,6},{8,9},{9,8},{10,11... | collective-permute-start | bytes 4718600 | tf_op jit(solution)/shard_map/ppermute | solution.py:110
  710.1 52.8 %collective-permute-start.10 = (bf16[768,2048]{1,0:T(8,128)(2,1)}, bf16[768,2048]{1,0:T(8,128)(2,1)}, u32[]{:S(2)}, u32[]{:S(2)}) collective-permute-start(bf16[768,2048]{1,0:T(8,128)(2,1)} %add_convert_fusion.1), channel_id=1, source_target_pairs={{0,2},{2,0},{4,6},{6,4},{8,10},{10,8},{12,14},{14,12},{16,18},{18,... | collective-permute-start | bytes 9437192 | tf_op jit(solution)/shard_map/ppermute | solution.py:55
  710.2 41.4 %collective-permute-start.11 = (bf16[768,256]{0,1:T(8,128)(2,1)S(1)}, bf16[768,256]{0,1:T(8,128)(2,1)S(1)}, u32[]{:S(2)}, u32[]{:S(2)}) collective-permute-start(bf16[768,256]{0,1:T(8,128)(2,1)S(1)} %pad_maximum_fusion.7), channel_id=1, source_target_pairs={{0,1},{1,0},{2,3},{3,2},{4,5},{5,4},{6,7},{7,6},{8,9},{9,8},{10,11... | collective-permute-start | bytes 1179656 | tf_op jit(solution)/shard_map/ppermute | solution.py:110
  712.3 58.2 %collective-permute-start.13 = (bf16[768,2048]{1,0:T(8,128)(2,1)}, bf16[768,2048]{1,0:T(8,128)(2,1)}, u32[]{:S(2)}, u32[]{:S(2)}) collective-permute-start(bf16[768,2048]{1,0:T(8,128)(2,1)} %get-tuple-element.87), channel_id=1, source_target_pairs={{0,2},{2,0},{4,6},{6,4},{8,10},{10,8},{12,14},{14,12},{16,18},{18,... | collective-permute-start | bytes 9437192 | tf_op jit(solution)/shard_map/ppermute | solution.py:55
  755.1 7.8 collective-permute-start.12
  758.9 3.8 collective-permute-start.15
  760.9 9.6 collective-permute-start.14
  762.8 7.5 collective-permute-start.16
  786.2 287.3 %reduce-scatter.8.cloned.1.call-start = ((), (), s32[]{:S(2)}) async-start(), calls=%async_computation.11 | async-start | bytes 9437184 | tf_op jit(solution)/shard_map/reduce_scatter | solution.py:80
  793.1 60.3 %all-to-all-start.3 = ((bf16[16,24,2048]{2,1,0:T(8,128)(2,1)}), bf16[16,24,2048]{2,1,0:T(8,128)(2,1)}, u32[]{:S(2)}, u32[]{:S(2)}) async-start(bf16[16,24,2048]{2,1,0:T(8,128)(2,1)} %bitcast.27), calls=%async_computation.3 | async-start | bytes 3145728 | tf_op jit(solution)/shard_map/all_to_all | solution.py:316
  797.6 63.8 %collective-permute-start.8 = (bf16[384,2048]{1,0:T(8,128)(2,1)}, bf16[384,2048]{1,0:T(8,128)(2,1)}, u32[]{:S(2)}, u32[]{:S(2)}) collective-permute-start(bf16[384,2048]{1,0:T(8,128)(2,1)} %bitcast.25), channel_id=1, source_target_pairs={{0,1},{1,0},{2,3},{3,2},{4,5},{5,4},{6,7},{7,6},{8,9},{9,8},{10,11... | collective-permute-start | bytes 4718600 | tf_op jit(solution)/shard_map/ppermute | solution.py:110
  853.4 36.7 %collective-permute-start.9 = (bf16[384,2048]{1,0:T(8,128)(2,1)}, bf16[384,2048]{1,0:T(8,128)(2,1)}, u32[]{:S(2)}, u32[]{:S(2)}) collective-permute-start(bf16[384,2048]{1,0:T(8,128)(2,1)} %bitcast.28), channel_id=1, source_target_pairs={{0,1},{1,0},{2,3},{3,2},{4,5},{5,4},{6,7},{7,6},{8,9},{9,8},{10,11... | collective-permute-start | bytes 4718600 | tf_op jit(solution)/shard_map/ppermute | solution.py:110
  861.4 35.3 %collective-permute-start.22 = (bf16[128,2048]{1,0:T(8,128)(2,1)}, bf16[128,2048]{1,0:T(8,128)(2,1)}, u32[]{:S(2)}, u32[]{:S(2)}) collective-permute-start(bf16[128,2048]{1,0:T(8,128)(2,1)} %constant_dynamic-slice_fusion.2), channel_id=1, source_target_pairs={{0,2},{2,0},{4,6},{6,4},{8,10},{10,8},{12,14},{14,12},{16,18},{18,... | collective-permute-start | bytes 1572872 | tf_op jit(solution)/shard_map/ppermute | solution.py:55
  923.9 153.8 %collective-permute-start.17 = (bf16[128,640]{0,1:T(8,128)(2,1)S(1)}, bf16[128,640]{0,1:T(8,128)(2,1)S(1)}, u32[]{:S(2)}, u32[]{:S(2)}) collective-permute-start(bf16[128,640]{0,1:T(8,128)(2,1)S(1)} %constant_dynamic-slice_fusion.6), channel_id=1, source_target_pairs={{0,2},{2,0},{4,6},{6,4},{8,10},{10,8},{12,14},{14,12},{16,18},{18,... | collective-permute-start | bytes 491528 | tf_op jit(solution)/shard_map/ppermute | solution.py:55
  925.0 151.6 %collective-permute-start.18 = (bf16[128,512]{0,1:T(8,128)(2,1)S(1)}, bf16[128,512]{0,1:T(8,128)(2,1)S(1)}, u32[]{:S(2)}, u32[]{:S(2)}) collective-permute-start(bf16[128,512]{0,1:T(8,128)(2,1)S(1)} %constant_dynamic-slice_fusion.5), channel_id=1, source_target_pairs={{0,2},{2,0},{4,6},{6,4},{8,10},{10,8},{12,14},{14,12},{16,18},{18,... | collective-permute-start | bytes 393224 | tf_op jit(solution)/shard_map/ppermute | solution.py:55
  1075.4 7.9 collective-permute-start.23
  (55 other events, 1444.8 us)
Sparse Core Ops, SparseCore 0:
  13.1 132.6 all-gather.2
  148.0 168.3 all-gather.4
  698.0 75.7 reduce-scatter.5
  786.4 136.4 reduce-scatter.3
  926.3 147.1 reduce-scatter.7
